TPU v7x, 512 devices: a whole 4x4x16 slice. The times are simulated.
512 devices in a mesh: tok: 128 (over z, y, core), head: 4 (over x).
Axes of the slice: x: 4, y: 4, z: 16, core: 2. Of those that a mesh axis runs over, the one named last changes fastest.
Arguments:
- tokens: bfloat16 [32768, 2048], P('tok', 'head'), may hold values from -6 to 6
- norm_gain: float32 [2048], replicated, may hold values from 0.25 to 1.75
- w_query: bfloat16 [2048, 4096], P('tok', 'head'), may hold values from -0.125 to 0.125
- key_weight: bfloat16 [2048, 512], P('tok', 'head'), may hold values from -0.125 to 0.125
- value_weight: bfloat16 [2048, 512], P('tok', 'head'), may hold values from -0.125 to 0.125
- query_gain: float32 [128], replicated, may hold values from 0.6 to 12
- key_gain: float32 [128], replicated, may hold values from 0.6 to 12
- w_out: bfloat16 [4096, 2048], P('head', 'tok'), may hold values from -0.09375 to 0.09375
- doc_ids: int32 [32768], P('tok'), may hold values from 0 to 15, never falling along the last dimension, each value on 1 to 8192 neighbouring positions
- sentinel: int32 [32768], P('tok'), may hold values 0 or 1
- tile_reach: int32 [256], P('tok'), may hold values from 1 to 28, as said below
Outputs:
- attn_out: bfloat16 [32768, 2048], P('tok', 'head')
Inputs may be any that keep to these rules, and one draw needn't show every extreme that they name: `tile_reach`: some tile's entry is 28.
All inputs are finite; a program needn't handle non-finite values. No bound on the sum of `sentinel` on one device may be relied on, other than what follows from the above.
Results may differ from a plain program's by a relative error of at most 0.014.
The roundings to bfloat16 on the way count: a program that leaves them out, or rounds other values in their place, can miss the bound.
Values may be sent and summed in bfloat16 or wider, within the bound.
No kernel may reach another device: no remote copies, remote signals or barrier semaphores. Data moves between devices by JAX's collectives and lax.ppermute only.
A program may use at most 64 MiB of HBM per device.

v0:
```python
import math

import jax
import jax.numpy as jnp
from jax import lax
from jax.sharding import PartitionSpec as P

HEAD_SIZE = 128
TILE_TOKENS = 128
REACH_DEVS = 14


EPSILON = 1e-06
THETA = 10000000.0


def copy_for_each(shard, axis):
    count = lax.axis_size(axis)
    return lax.all_to_all(
        jnp.broadcast_to(shard[None], (count, *shard.shape)), axis, 0, 0, tiled=True
    )


def in_order(parts, dim):
    shape = list(parts.shape[1:])
    shape[dim] *= parts.shape[0]
    return jnp.moveaxis(parts, 0, dim).reshape(shape)


def gathered_copies(shard, axis, dim):
    parts = copy_for_each(shard, axis)
    return in_order(parts, dim)


def in_one_piece(arrays, axis, dim, along):
    widths = [a.shape[along] for a in arrays]
    both = jnp.concatenate(arrays, axis=along)
    filled = lax.all_gather(both, axis, axis=dim, tiled=True)
    return tuple(jnp.split(filled, [sum(widths[:k]) for k in range(1, len(widths))], axis=along))


def shortened(shard):
    return jax.tree.map(lambda a: a.astype(jnp.bfloat16) if a.dtype == jnp.float32 else a, shard)


def passed_along(value, axis, steps):
    count = lax.axis_size(axis)
    leading, last = (max(0, -steps), min(count, count - steps))
    return lax.ppermute(value, axis, [(source, source + steps) for source in range(leading, last)])


def split_up(shard, dim, count):
    shape = shard.shape
    parts = shard.reshape(*shape[:dim], count, shape[dim] // count, *shape[dim + 1 :])
    return jnp.moveaxis(parts, dim, 0)


def summed_on_arrival(shard, axis, dim):
    count = lax.axis_size(axis)
    parts = lax.all_to_all(split_up(shard, dim, count), axis, 0, 0, tiled=True)
    return jnp.sum(parts.astype(jnp.float32), axis=0)


def rms_norm(values, gain):
    mean_square = jnp.mean(values * values, axis=-1, keepdims=True)
    return values * lax.rsqrt(mean_square + EPSILON) * gain


def rotate(values, positions):
    width = values.shape[-1]
    half_width = width // 2
    freqs = THETA ** (-2.0 * jnp.arange(half_width, dtype=jnp.float32) / width)
    angles = positions[:, None] * freqs[None, :]
    cosine = jnp.cos(angles)[:, None, :]
    sine = jnp.sin(angles)[:, None, :]
    first = values[..., :half_width]
    second = values[..., half_width:]
    return jnp.concatenate(
        [first * cosine - second * sine, second * cosine + first * sine], axis=-1
    )


def on_device(
    tokens,
    norm_gain,
    w_query,
    key_weight,
    value_weight,
    query_gain,
    key_gain,
    w_out,
    doc_ids,
    sentinel,
    tile_reach,
):
    whole = gathered_copies(tokens, "head", 1)
    row_count = whole.shape[0]
    normalized_rows = rms_norm(whole.astype(jnp.float32), norm_gain).astype(jnp.bfloat16)
    query_cols = w_query.shape[1]
    key_cols = key_weight.shape[1]
    portions = in_one_piece((w_query, key_weight, value_weight), "tok", 0, 1)
    proj_query, proj_key, proj_value = tuple(
        (
            jnp.dot(normalized_rows, portion, preferred_element_type=jnp.float32)
            for portion in portions
        )
    )
    base_row = lax.axis_index("tok") * row_count
    positions = (base_row + jnp.arange(row_count, dtype=jnp.int32)).astype(jnp.float32)
    local_heads = query_cols // HEAD_SIZE
    local_kv = key_cols // HEAD_SIZE
    head_groups = local_heads // local_kv
    query_matrix = rotate(
        rms_norm(proj_query.reshape(row_count, local_heads, HEAD_SIZE), query_gain), positions
    )
    query_matrix = query_matrix.astype(jnp.bfloat16).reshape(
        row_count, local_kv, head_groups, HEAD_SIZE
    )
    keys_own = rotate(
        rms_norm(proj_key.reshape(row_count, local_kv, HEAD_SIZE), key_gain), positions
    ).astype(jnp.bfloat16)
    values_own = proj_value.astype(jnp.bfloat16).reshape(row_count, local_kv, HEAD_SIZE)
    tags_own = jnp.where(sentinel == 1, 0, doc_ids + 1).astype(jnp.bfloat16)
    blocks = REACH_DEVS + 1
    stacked = (keys_own[None], values_own[None], tags_own[None])
    for level in range(REACH_DEVS.bit_length()):
        incoming = jax.tree.map(
            lambda part, own: part.astype(own.dtype),
            passed_along(shortened(stacked), "tok", 1 << level),
            stacked,
        )
        stacked = tuple(
            (jnp.concatenate([earlier, later], axis=0) for earlier, later in zip(incoming, stacked))
        )
    key_store = stacked[0][-blocks:]
    value_store = stacked[1][-blocks:]
    tag_store = stacked[2][-blocks:]
    factor_scale = 1.0 / math.sqrt(HEAD_SIZE)
    outputs = []
    for tile_index in range(row_count // TILE_TOKENS):
        query_tile = query_matrix[tile_index * TILE_TOKENS : (tile_index + 1) * TILE_TOKENS]
        query_pos = base_row + tile_index * TILE_TOKENS + jnp.arange(TILE_TOKENS, dtype=jnp.int32)
        query_docs = doc_ids[tile_index * TILE_TOKENS : (tile_index + 1) * TILE_TOKENS] + 1
        lowest = base_row // TILE_TOKENS + tile_index - tile_reach[tile_index]

        def update(
            block,
            state,
            query_tile=query_tile,
            query_pos=query_pos,
            query_docs=query_docs,
            lowest=lowest,
        ):
            key_block = key_store[block]
            value_block = value_store[block]
            tag_block = tag_store[block].astype(jnp.int32)
            key_pos = (
                base_row + (block - REACH_DEVS) * row_count + jnp.arange(row_count, dtype=jnp.int32)
            )
            same_doc = (tag_block[None, :] == query_docs[:, None]) | (
                key_pos[None, :] == query_pos[:, None]
            )
            visible = (
                same_doc
                & (key_pos[None, :] <= query_pos[:, None])
                & (jnp.floor_divide(key_pos, TILE_TOKENS)[None, :] >= lowest)
            )

            def compute(inner):
                peak_run, weight_sum, accum_out = inner
                scores = (
                    jnp.einsum(
                        "qcgd,kcd->cgqk", query_tile, key_block, preferred_element_type=jnp.float32
                    )
                    * factor_scale
                )
                scores = jnp.where(visible, scores, -jnp.inf)
                peak_new = jnp.maximum(peak_run, jnp.max(scores, axis=-1))
                shrink = jnp.exp(peak_run - peak_new)
                weights = jnp.exp(scores - peak_new[..., None])
                weight_sum = weight_sum * shrink + jnp.sum(weights, axis=-1)
                mixed = jnp.einsum(
                    "cgqk,kcd->cgqd",
                    weights.astype(jnp.bfloat16),
                    value_block,
                    preferred_element_type=jnp.float32,
                )
                return (peak_new, weight_sum, accum_out * shrink[..., None] + mixed)

            return lax.cond(jnp.any(visible), compute, lambda inner: inner, state)

        initial = (
            jnp.full((local_kv, head_groups, TILE_TOKENS), -1e30, jnp.float32),
            jnp.zeros((local_kv, head_groups, TILE_TOKENS), jnp.float32),
            jnp.zeros((local_kv, head_groups, TILE_TOKENS, HEAD_SIZE), jnp.float32),
        )
        peak_run, weight_sum, accum_out = lax.fori_loop(0, blocks, update, initial)
        result = accum_out / weight_sum[..., None]
        outputs.append(
            jnp.transpose(result, (2, 0, 1, 3))
            .reshape(TILE_TOKENS, query_cols)
            .astype(jnp.bfloat16)
        )
    attended = jnp.concatenate(outputs, axis=0)
    partials = jnp.dot(
        attended,
        lax.all_gather(w_out, "tok", axis=1, tiled=True),
        preferred_element_type=jnp.float32,
    )
    return summed_on_arrival(partials.astype(jnp.bfloat16), "head", 1).astype(jnp.bfloat16)


def solution(mesh):
    return jax.shard_map(
        on_device,
        mesh=mesh,
        in_specs=(
            P("tok", "head"),
            P(),
            P("tok", "head"),
            P("tok", "head"),
            P("tok", "head"),
            P(),
            P(),
            P("head", "tok"),
            P("tok"),
            P("tok"),
            P("tok"),
        ),
        out_specs=P("tok", "head"),
        check_vma=False,
    )
```

profile of v0, /device:TPU:160, one launch (start us, length us, event | category | flops | bytes accessed | tf_op | source)
XLA Modules:
  0.0 334.7 jit_solution(1347269938544471688)
XLA Ops:
  6.5 1.4 pad_maximum_fusion.5
  8.0 2.0 broadcast_in_dim.92
  10.0 4.3 %all-to-all-start = ((bf16[4,256,512]{2,1,0:T(8,128)(2,1)}), bf16[4,256,512]{2,1,0:T(8,128)(2,1)S(1)}, u32[]{:S(2)}, u32[]{:S(2)}) async-start(bf16[4,256,512]{2,1,0:T(8,128)(2,1)} %broadcast_in_dim.92), calls=%async_computation | async-start | bytes 2097152 | tf_op jit(solution)/shard_map/all_to_all | solution.py:19
  15.0 1.9 collective-permute-start
  17.0 5.0 %collective-permute-done = bf16[1,256]{1,0:T(2,128)(2,1)S(1)} collective-permute-done((bf16[1,256]{1,0:T(2,128)(2,1)S(1)}, bf16[1,256]{1,0:T(2,128)(2,1)S(1)}, u32[]{:S(2)}, u32[]{:S(2)}) %collective-permute-start) | collective-permute-done | bytes 544 | tf_op jit(solution)/shard_map/ppermute | solution.py:49
  22.0 1.9 collective-permute-start.1
  24.9 4.7 %collective-permute-done.1 = bf16[2,256]{1,0:T(2,128)(2,1)S(1)} collective-permute-done((bf16[2,256]{1,0:T(2,128)(2,1)S(1)}, bf16[2,256]{1,0:T(2,128)(2,1)S(1)}, u32[]{:S(2)}, u32[]{:S(2)}) %collective-permute-start.1) | collective-permute-done | bytes 1056 | tf_op jit(solution)/shard_map/ppermute | solution.py:49
  29.6 1.9 collective-permute-start.2
  32.3 5.2 %collective-permute-done.2 = bf16[4,256]{1,0:T(4,128)(2,1)S(1)} collective-permute-done((bf16[4,256]{1,0:T(4,128)(2,1)S(1)}, bf16[4,256]{1,0:T(4,128)(2,1)S(1)}, u32[]{:S(2)}, u32[]{:S(2)}) %collective-permute-start.2) | collective-permute-done | bytes 2080 | tf_op jit(solution)/shard_map/ppermute | solution.py:49
  37.5 3.8 %collective-permute-start.3 = (bf16[8,256]{1,0:T(8,128)(2,1)S(1)}, bf16[8,256]{1,0:T(8,128)(2,1)S(1)}, u32[]{:S(2)}, u32[]{:S(2)}) collective-permute-start(bf16[8,256]{1,0:T(8,128)(2,1)S(1)} %pad_maximum_fusion.6), channel_id=1, source_target_pairs={{0,32},{4,36},{8,40},{12,44},{16,48},{20,52},{24,56},{28,60},{32,6... | collective-permute-start | bytes 12296 | tf_op jit(solution)/shard_map/ppermute | solution.py:49
  41.3 1.3 fusion.66
  46.3 107.1 %all-gather.3.cloned.1.call-done = bf16[2048,1280]{1,0:T(8,128)(2,1)} async-done(((bf16[16,1280]{1,0:T(8,128)(2,1)}), bf16[2048,1280]{1,0:T(8,128)(2,1)}) %all-gather.3.cloned.1.call-update) | async-done | bytes 5242896 | tf_op jit(solution)/shard_map/all_gather | solution.py:38
  153.4 1.5 fusion.40
  155.0 2.1 collective-permute-start.8
  157.1 1.4 multiply_reduce_fusion.2
  159.0 2.0 collective-permute-start.4
  161.0 4.7 %slice_bitcast_fusion = bf16[1024,2048]{0,1:T(8,128)(2,1)} fusion(bf16[2048,1280]{1,0:T(8,128)(2,1)} %all-gather.3.cloned.1.call-done), kind=kLoop, calls=%fused_computation.62 | loop fusion | bytes 8388608 | tf_op jit(solution)/shard_map/dot_general | solution.py:104
  165.7 6.5 %copy.41 = bf16[1024,2048]{1,0:T(8,128)(2,1)} copy(bf16[1024,2048]{0,1:T(8,128)(2,1)} %slice_bitcast_fusion) | data formatting | bytes 8388608 | tf_op jit(solution)/shard_map/dot_general | solution.py:104
  172.3 3.5 %multiply_reduce_fusion.1 = (f32[256,8]{0,1:T(8,128)S(1)}, f32[256,8,128]{0,2,1:T(8,128)S(1)}) fusion(bf16[256,2048,1]{0,1,2:T(8,128)(2,1)S(1)} %bitcast.139, bf16[8,128,2048]{2,1,0:T(8,128)(2,1)} %bitcast.132), kind=kOutput, calls=%fused_computation.73 | convolution fusion | flops 1074264064 | bytes 6299648 | tf_op jit(solution)/shard_map/dot_general | solution.py:104
  175.8 3.1 collective-permute-start.9
  179.0 2.8 collective-permute-start.5
  181.8 4.0 %collective-permute-done.9 = bf16[2,256,1,128]{3,1,2,0:T(8,128)(2,1)S(1)} collective-permute-done((bf16[2,256,1,128]{3,1,2,0:T(8,128)(2,1)S(1)}, bf16[2,256,1,128]{3,1,2,0:T(8,128)(2,1)S(1)}, u32[]{:S(2)}, u32[]{:S(2)}) %collective-permute-start.9) | collective-permute-done | bytes 131104 | tf_op jit(solution)/shard_map/ppermute | solution.py:49
  185.8 2.3 collective-permute-start.10
  188.3 9.8 %collective-permute-done.10 = bf16[4,256,1,128]{3,1,2,0:T(8,128)(2,1)S(1)} collective-permute-done((bf16[4,256,1,128]{3,1,2,0:T(8,128)(2,1)S(1)}, bf16[4,256,1,128]{3,1,2,0:T(8,128)(2,1)S(1)}, u32[]{:S(2)}, u32[]{:S(2)}) %collective-permute-start.10) | collective-permute-done | bytes 262176 | tf_op jit(solution)/shard_map/ppermute | solution.py:49
  198.2 2.4 collective-permute-start.11
  200.6 2.0 collective-permute-start.6
  203.2 14.2 %collective-permute-done.6 = bf16[4,256,1,128]{1,3,2,0:T(8,128)(2,1)S(1)} collective-permute-done((bf16[4,256,1,128]{1,3,2,0:T(8,128)(2,1)S(1)}, bf16[4,256,1,128]{1,3,2,0:T(8,128)(2,1)S(1)}, u32[]{:S(2)}, u32[]{:S(2)}) %collective-permute-start.6) | collective-permute-done | bytes 262176 | tf_op jit(solution)/shard_map/ppermute | solution.py:49
  217.5 3.4 %collective-permute-start.7 = (bf16[8,256,1,128]{1,3,2,0:T(8,128)(2,1)S(1)}, bf16[8,256,1,128]{1,3,2,0:T(8,128)(2,1)S(1)}, u32[]{:S(2)}, u32[]{:S(2)}) collective-permute-start(bf16[8,256,1,128]{1,3,2,0:T(8,128)(2,1)S(1)} %maximum_maximum_fusion), channel_id=1, source_target_pairs={{0,32},{4,36},{8,40},{12,44},{16,48},{20,52},{24,56},{28,60},{32,6... | collective-permute-start | bytes 1572872 | tf_op jit(solution)/shard_map/ppermute | solution.py:49
  221.2 10.8 %collective-permute-done.7 = bf16[8,256,1,128]{1,3,2,0:T(8,128)(2,1)S(1)} collective-permute-done((bf16[8,256,1,128]{1,3,2,0:T(8,128)(2,1)S(1)}, bf16[8,256,1,128]{1,3,2,0:T(8,128)(2,1)S(1)}, u32[]{:S(2)}, u32[]{:S(2)}) %collective-permute-start.7) | collective-permute-done | bytes 524320 | tf_op jit(solution)/shard_map/ppermute | solution.py:49
  233.1 37.0 %while.42 = (s32[]{:T(128)}, f32[1,8,128]{2,1,0:T(8,128)S(1)}, f32[1,8,128]{2,1,0:T(8,128)S(1)}, f32[1,8,128,128]{3,2,1,0:T(8,128)S(1)}, bf16[15,256]{1,0:T(8,12...) while((s32[]{:T(128)}, f32[1,8,128]{2,1,0:T(8,128)S(1)}, ...), condition=%wide.region_9.10_spmd.clone.clone, body=%wide.region_3.9_spmd.clone.clone.sunk | while | flops 136552320 | bytes 4725571 | solution.py:197
  237.7 1.1 conditional.8
  245.6 1.1 conditional.8
  248.2 1.1 conditional.8
  263.8 1.1 conditional.8
  271.1 37.0 %while.41 = (s32[]{:T(128)}, f32[1,8,128]{2,1,0:T(8,128)S(1)}, f32[1,8,128]{2,1,0:T(8,128)S(1)}, f32[1,8,128,128]{3,2,1,0:T(8,128)S(1)}, bf16[15,256]{1,0:T(8,12...) while((s32[]{:T(128)}, f32[1,8,128]{2,1,0:T(8,128)S(1)}, ...), condition=%wide.region_16.17_spmd.clone, body=%wide.region_10.16_spmd.clone.sunk | while | flops 136552320 | bytes 4725579 | solution.py:197
  278.4 1.1 conditional.7
  283.6 1.1 conditional.7
  286.2 1.1 conditional.7
  288.8 1.1 conditional.7
  291.4 1.1 conditional.7
  294.0 1.1 conditional.7
  296.6 1.1 conditional.7
  299.2 1.1 conditional.7
  301.8 1.1 conditional.7
  304.4 1.1 conditional.7
  307.0 1.1 conditional.7
  308.4 3.5 %convolution_convert_fusion = bf16[256,2048]{1,0:T(8,128)(2,1)S(1)} fusion(bf16[1024,2048]{0,1:T(8,128)(2,1)} %all-gather.5.cloned.1.call-done, bf16[128,1024]{0,1:T(8,128)(2,1)S(1)} %bitcast.141, bf16[128,1024]{0,1:T(8,128)(2,1)S(1)} %bitcast.140), kind=kOutput, calls=%fused_computation.63 | convolution fusion | flops 1075314688 | bytes 5767168 | tf_op jit(solution)/shard_map/dot_general | solution.py:205
  312.0 14.9 %all_to_all.10 = bf16[4,256,512]{2,1,0:T(8,128)(2,1)S(1)} all-to-all(bf16[4,256,512]{2,1,0:T(8,128)(2,1)S(1)} %bitcast.133), channel_id=1, replica_groups=mesh['tok'=128,'head'=4] {'head'}, dimensions={0} | all-to-all | bytes 2097152 | tf_op jit(solution)/shard_map/all_to_all | solution.py:60
  (400 shorter events, 72.5 us)
Async XLA Ops:
  6.5 39.1 %copy-start.2 = (f32[2048]{0:T(1024)S(1)}, f32[2048]{0:T(1024)}, u32[]{:S(2)}) copy-start(f32[2048]{0:T(1024)} %param.20) | copy-start | bytes 24580
  6.5 146.9 %all-gather.3.cloned.1.call-start = ((), (), s32[]{:S(2)}) async-start(), calls=%async_computation.2 | async-start | bytes 5283840 | tf_op jit(solution)/shard_map/all_gather | solution.py:38
  10.0 34.8 %all-to-all-start = ((bf16[4,256,512]{2,1,0:T(8,128)(2,1)}), bf16[4,256,512]{2,1,0:T(8,128)(2,1)S(1)}, u32[]{:S(2)}, u32[]{:S(2)}) async-start(bf16[4,256,512]{2,1,0:T(8,128)(2,1)} %broadcast_in_dim.92), calls=%async_computation | async-start | bytes 2097152 | tf_op jit(solution)/shard_map/all_to_all | solution.py:19
  14.3 294.1 %all-gather.5.cloned.1.call-start = ((), (), s32[]{:S(2)}) async-start(), calls=%async_computation.3 | async-start | bytes 4227072 | tf_op jit(solution)/shard_map/all_gather | solution.py:207
  15.0 7.0 %collective-permute-start = (bf16[1,256]{1,0:T(2,128)(2,1)S(1)}, bf16[1,256]{1,0:T(2,128)(2,1)S(1)}, u32[]{:S(2)}, u32[]{:S(2)}) collective-permute-start(bf16[1,256]{1,0:T(2,128)(2,1)S(1)} %broadcast_in_dim.91), channel_id=1, source_target_pairs={{0,4},{4,8},{8,12},{12,16},{16,20},{20,24},{24,28},{28,32},{32,36}... | collective-permute-start | bytes 1544 | tf_op jit(solution)/shard_map/ppermute | solution.py:49
  22.0 7.6 %collective-permute-start.1 = (bf16[2,256]{1,0:T(2,128)(2,1)S(1)}, bf16[2,256]{1,0:T(2,128)(2,1)S(1)}, u32[]{:S(2)}, u32[]{:S(2)}) collective-permute-start(bf16[2,256]{1,0:T(2,128)(2,1)S(1)} %pad_maximum_fusion.8), channel_id=1, source_target_pairs={{0,8},{4,12},{8,16},{12,20},{16,24},{20,28},{24,32},{28,36},{32,40... | collective-permute-start | bytes 3080 | tf_op jit(solution)/shard_map/ppermute | solution.py:49
  29.6 7.9 %collective-permute-start.2 = (bf16[4,256]{1,0:T(4,128)(2,1)S(1)}, bf16[4,256]{1,0:T(4,128)(2,1)S(1)}, u32[]{:S(2)}, u32[]{:S(2)}) collective-permute-start(bf16[4,256]{1,0:T(4,128)(2,1)S(1)} %pad_maximum_fusion.7), channel_id=1, source_target_pairs={{0,16},{4,20},{8,24},{12,28},{16,32},{20,36},{24,40},{28,44},{32,4... | collective-permute-start | bytes 6152 | tf_op jit(solution)/shard_map/ppermute | solution.py:49
  37.5 7.2 %collective-permute-start.3 = (bf16[8,256]{1,0:T(8,128)(2,1)S(1)}, bf16[8,256]{1,0:T(8,128)(2,1)S(1)}, u32[]{:S(2)}, u32[]{:S(2)}) collective-permute-start(bf16[8,256]{1,0:T(8,128)(2,1)S(1)} %pad_maximum_fusion.6), channel_id=1, source_target_pairs={{0,32},{4,36},{8,40},{12,44},{16,48},{20,52},{24,56},{28,60},{32,6... | collective-permute-start | bytes 12296 | tf_op jit(solution)/shard_map/ppermute | solution.py:49
  45.3 113.3 %copy-start.3 = (f32[128]{0:T(128)S(1)}, f32[128]{0:T(128)}, u32[]{:S(2)}) copy-start(f32[128]{0:T(128)} %param.25) | copy-start | bytes 1540
  155.0 20.7 %collective-permute-start.8 = (bf16[1,256,1,128]{3,1,2,0:T(8,128)(2,1)S(1)}, bf16[1,256,1,128]{3,1,2,0:T(8,128)(2,1)S(1)}, u32[]{:S(2)}, u32[]{:S(2)}) collective-permute-start(bf16[1,256,1,128]{3,1,2,0:T(8,128)(2,1)S(1)} %fusion.40), channel_id=1, source_target_pairs={{0,4},{4,8},{8,12},{12,16},{16,20},{20,24},{24,28},{28,32},{32,36}... | collective-permute-start | bytes 196616 | tf_op jit(solution)/shard_map/ppermute | solution.py:49
  159.0 19.9 %collective-permute-start.4 = (bf16[1,256,1,128]{1,3,2,0:T(8,128)(2,1)S(1)}, bf16[1,256,1,128]{1,3,2,0:T(8,128)(2,1)S(1)}, u32[]{:S(2)}, u32[]{:S(2)}) collective-permute-start(bf16[1,256,1,128]{1,3,2,0:T(8,128)(2,1)S(1)} %pad_maximum_fusion.4), channel_id=1, source_target_pairs={{0,4},{4,8},{8,12},{12,16},{16,20},{20,24},{24,28},{28,32},{32,36}... | collective-permute-start | bytes 196616 | tf_op jit(solution)/shard_map/ppermute | solution.py:49
  172.3 15.8 %copy-start.4 = (f32[128]{0:T(128)S(1)}, f32[128]{0:T(128)}, u32[]{:S(2)}) copy-start(f32[128]{0:T(128)} %param.24) | copy-start | bytes 1540
  175.7 26.9 %copy-start.1 = (f32[256,64]{0,1:T(8,128)S(1)}, f32[256,64]{0,1:T(8,128)}, u32[]{:S(2)}) copy-start(f32[256,64]{0,1:T(8,128)} %get-tuple-element.1015) | copy-start | bytes 196612
  175.8 10.0 %collective-permute-start.9 = (bf16[2,256,1,128]{3,1,2,0:T(8,128)(2,1)S(1)}, bf16[2,256,1,128]{3,1,2,0:T(8,128)(2,1)S(1)}, u32[]{:S(2)}, u32[]{:S(2)}) collective-permute-start(bf16[2,256,1,128]{3,1,2,0:T(8,128)(2,1)S(1)} %pad_maximum_fusion.3), channel_id=1, source_target_pairs={{0,8},{4,12},{8,16},{12,20},{16,24},{20,28},{24,32},{28,36},{32,40... | collective-permute-start | bytes 393224 | tf_op jit(solution)/shard_map/ppermute | solution.py:49
  179.0 21.6 %collective-permute-start.5 = (bf16[2,256,1,128]{1,3,2,0:T(8,128)(2,1)S(1)}, bf16[2,256,1,128]{1,3,2,0:T(8,128)(2,1)S(1)}, u32[]{:S(2)}, u32[]{:S(2)}) collective-permute-start(bf16[2,256,1,128]{1,3,2,0:T(8,128)(2,1)S(1)} %maximum_maximum_fusion.2), channel_id=1, source_target_pairs={{0,8},{4,12},{8,16},{12,20},{16,24},{20,28},{24,32},{28,36},{32,40... | collective-permute-start | bytes 393224 | tf_op jit(solution)/shard_map/ppermute | solution.py:49
  185.8 12.3 %collective-permute-start.10 = (bf16[4,256,1,128]{3,1,2,0:T(8,128)(2,1)S(1)}, bf16[4,256,1,128]{3,1,2,0:T(8,128)(2,1)S(1)}, u32[]{:S(2)}, u32[]{:S(2)}) collective-permute-start(bf16[4,256,1,128]{3,1,2,0:T(8,128)(2,1)S(1)} %pad_maximum_fusion.2), channel_id=1, source_target_pairs={{0,16},{4,20},{8,24},{12,28},{16,32},{20,36},{24,40},{28,44},{32,4... | collective-permute-start | bytes 786440 | tf_op jit(solution)/shard_map/ppermute | solution.py:49
  198.2 22.8 %collective-permute-start.11 = (bf16[8,256,1,128]{3,1,2,0:T(8,128)(2,1)S(1)}, bf16[8,256,1,128]{3,1,2,0:T(8,128)(2,1)S(1)}, u32[]{:S(2)}, u32[]{:S(2)}) collective-permute-start(bf16[8,256,1,128]{3,1,2,0:T(8,128)(2,1)S(1)} %pad_maximum_fusion), channel_id=1, source_target_pairs={{0,32},{4,36},{8,40},{12,44},{16,48},{20,52},{24,56},{28,60},{32,6... | collective-permute-start | bytes 1572872 | tf_op jit(solution)/shard_map/ppermute | solution.py:49
  200.6 16.9 %collective-permute-start.6 = (bf16[4,256,1,128]{1,3,2,0:T(8,128)(2,1)S(1)}, bf16[4,256,1,128]{1,3,2,0:T(8,128)(2,1)S(1)}, u32[]{:S(2)}, u32[]{:S(2)}) collective-permute-start(bf16[4,256,1,128]{1,3,2,0:T(8,128)(2,1)S(1)} %maximum_maximum_fusion.1), channel_id=1, source_target_pairs={{0,16},{4,20},{8,24},{12,28},{16,32},{20,36},{24,40},{28,44},{32,4... | collective-permute-start | bytes 786440 | tf_op jit(solution)/shard_map/ppermute | solution.py:49
  217.5 14.5 %collective-permute-start.7 = (bf16[8,256,1,128]{1,3,2,0:T(8,128)(2,1)S(1)}, bf16[8,256,1,128]{1,3,2,0:T(8,128)(2,1)S(1)}, u32[]{:S(2)}, u32[]{:S(2)}) collective-permute-start(bf16[8,256,1,128]{1,3,2,0:T(8,128)(2,1)S(1)} %maximum_maximum_fusion), channel_id=1, source_target_pairs={{0,32},{4,36},{8,40},{12,44},{16,48},{20,52},{24,56},{28,60},{32,6... | collective-permute-start | bytes 1572872 | tf_op jit(solution)/shard_map/ppermute | solution.py:49
  271.1 37.2 %copy-start = (f32[1,8,128,128]{2,3,1,0:T(8,128)S(1)}, f32[1,8,128,128]{2,3,1,0:T(8,128)}, u32[]{:S(2)}) copy-start(f32[1,8,128,128]{2,3,1,0:T(8,128)} %copy.45) | copy-start | bytes 1572868
Sparse Core Ops, SparseCore 0:
  10.5 142.9 all-gather.2
  156.6 137.9 all-gather.4
where the time goes:
time: 334 us; the launch traced here: 335 us
  waiting for transfers between devices  161 us (48%)
  other arithmetic  36.8 us (11%)
  starting transfers between devices  34 us (10%)
  matrix products  31.2 us (9%)
  loops' own time  22.8 us (7%)
  local copies, waits for them, and re-layouts  18.8 us (6%)
  between operations  15.3 us (5%)
  blocking collectives  14.9 us (4%)
    all_gather x1, waiting for transfers between devices, in_one_piece(): filled = lax.all_gather(both, axis, axis=dim, tiled=True)  107 us
    ppermute x12, waiting for transfers between devices, passed_along(): lax.ppermute(value, axis, [(source, source + steps) for source in range(l...  53.7 us
    ppermute x12, starting transfers between devices, passed_along(): lax.ppermute(value, axis, [(source, source + steps) for source in range(l...  29.7 us
    reduce_or x30, other arithmetic, update(): return lax.cond(jnp.any(visible), compute, lambda inner: inner, state)  24.1 us
    another operation x2, loops' own time, on_device(): peak_run, weight_sum, accum_out = lax.fori_loop(0, blocks, update, initial)  21.2 us
    all_to_all x1, blocking collectives, summed_on_arrival(): parts = lax.all_to_all(split_up(shard, dim, count), axis, 0, 0, tiled=True)  14.9 us
    dot_general x26, matrix products, compute(): jnp.einsum('cgqk,kcd->cgqd', weights.astype(jnp.bfloat16), value_block, p...  13.2 us
    dot_general x2, local copies, waits for them, and re-layouts, on_device(): jnp.dot(normalized_rows, portion, preferred_element_type=jnp.float32)  11.2 us
  transfers between devices with their start and end apart: 15, of which 8 were waited for; matrix products, arithmetic and copies ran while one was open for 24% of the time, Pallas kernels for 0%

commit v1 on v0

v1 whole, which is shorter than its diff:
```python
import math

import jax
import jax.numpy as jnp
from jax import lax
from jax.experimental import pallas as pl
from jax.experimental.pallas import tpu as pltpu
from jax.sharding import Mesh, PartitionSpec as P


HEAD = 128
TILE = 128
BACK = 7
EPSILON = 1e-06
THETA = 10000000.0
TOK = ("z", "y", "core")
CHIP = ("z", "y")


def copies(shard, axis):
    count = lax.axis_size(axis)
    return lax.all_to_all(
        jnp.broadcast_to(shard[None], (count, *shard.shape)), axis, 0, 0, tiled=True
    )


def normed_and_turned(values, gain, cosine, sine):
    mean_square = jnp.mean(values * values, axis=-1, keepdims=True)
    scaled = values * lax.rsqrt(mean_square + EPSILON) * gain
    return scaled * cosine + pltpu.roll(scaled, HEAD // 2, 1) * sine


def query_kernel(x_ref, w_ref, gain_ref, cos_ref, sin_ref, out_ref, acc_ref):
    step = pl.program_id(0)

    @pl.when(step == 0)
    def _():
        acc_ref[...] = jnp.zeros_like(acc_ref)

    for half in range(2):
        rows = pl.ds(half * 256, 256)
        acc_ref[rows, :] += jnp.dot(
            x_ref[half, 0], w_ref[...], preferred_element_type=jnp.float32
        )

    @pl.when(step == pl.num_programs(0) - 1)
    def _():
        for tile in range(4):
            rows = pl.ds(tile * TILE, TILE)
            for head in range(4):
                one = acc_ref[rows, head * HEAD : (head + 1) * HEAD]
                turned = normed_and_turned(one, gain_ref[...], cos_ref[rows, :], sin_ref[rows, :])
                out_ref[tile, head] = turned.astype(jnp.bfloat16)


def project_queries(x, weights, gain, cosine, sine):
    return pl.pallas_call(
        query_kernel,
        grid=(4,),
        in_specs=[
            pl.BlockSpec((2, 1, 256, 512), lambda k: (0, k, 0, 0)),
            pl.BlockSpec((512, 512), lambda k: (k, 0)),
            pl.BlockSpec((1, HEAD), lambda k: (0, 0)),
            pl.BlockSpec((512, HEAD), lambda k: (0, 0)),
            pl.BlockSpec((512, HEAD), lambda k: (0, 0)),
        ],
        out_specs=pl.BlockSpec((4, 4, TILE, HEAD), lambda k: (0, 0, 0, 0)),
        out_shape=jax.ShapeDtypeStruct((4, 4, TILE, HEAD), jnp.bfloat16),
        scratch_shapes=[pltpu.VMEM((512, 512), jnp.float32)],
        name="project_queries",
    )(x, weights, gain, cosine, sine)


def key_value_kernel(core_ref, x_ref, w_ref, gain_ref, cos_ref, sin_ref, extra_ref, out_ref):
    is_key = core_ref[0] == 0
    for half in range(2):
        rows = pl.ds(half * 256, 256)
        total = jnp.zeros((256, HEAD), jnp.float32)
        for part in range(4):
            total += jnp.dot(
                x_ref[half, part],
                w_ref[part * 512 : (part + 1) * 512, :],
                preferred_element_type=jnp.float32,
            )
        turned = normed_and_turned(total, gain_ref[...], cos_ref[rows, :], sin_ref[rows, :])
        out_ref[rows, :] = jnp.where(is_key, turned, total).astype(jnp.bfloat16)
    out_ref[512:528, :] = extra_ref[...]


def project_keys_or_values(core, x, weights, gain, cosine, sine, extra):
    vmem = pl.BlockSpec(memory_space=pltpu.VMEM)
    return pl.pallas_call(
        key_value_kernel,
        in_specs=[pl.BlockSpec(memory_space=pltpu.SMEM)] + [vmem] * 6,
        out_specs=vmem,
        out_shape=jax.ShapeDtypeStruct((528, HEAD), jnp.bfloat16),
        name="project_keys_or_values",
    )(core, x, weights, gain, cosine, sine, extra)


def window_kernel(*refs):
    out_ref = refs[-1]
    for place, ref in enumerate(refs[:-1]):
        for core in range(2):
            out_ref[core, place] = ref[...]


def lay_window(blocks):
    vmem = pl.BlockSpec(memory_space=pltpu.VMEM)
    return pl.pallas_call(
        window_kernel,
        in_specs=[vmem] * len(blocks),
        out_specs=vmem,
        out_shape=jax.ShapeDtypeStruct((2, len(blocks), *blocks[0].shape), blocks[0].dtype),
        name="lay_window",
    )(*blocks)


def attention_kernel(q_ref, kv_ref, out_ref, tags_ref, docs_ref, m_ref, l_ref, acc_ref):
    tile = pl.program_id(0)
    lanes = lax.broadcasted_iota(jnp.int32, (1, TILE), 1)

    @pl.when(tile == 0)
    def _():
        for chip in range(BACK + 1):
            for core in range(2):
                extra = kv_ref[core, chip, 512:528, :].astype(jnp.float32)
                block = 2 * chip + core
                tags_ref[block : block + 1, :TILE] = extra[0:1]
                tags_ref[block : block + 1, TILE:] = extra[1:2]
                if chip == BACK:
                    docs_ref[core : core + 1, :] = extra[2:3]

    own_block = 2 * BACK + tile // 2
    odd = (tile % 2) == 1
    tag_row = jnp.abs(tags_ref[pl.ds(own_block, 1), :])
    doc_row = jnp.where(odd, tag_row[:, TILE:], tag_row[:, :TILE])
    diagonal = lax.broadcasted_iota(jnp.int32, (TILE, TILE), 0) == lax.broadcasted_iota(
        jnp.int32, (TILE, TILE), 1
    )
    query_doc = jnp.sum(jnp.where(diagonal, doc_row, 0.0), axis=1, keepdims=True)
    first_doc = jnp.sum(jnp.where(lanes == 0, doc_row, 0.0))
    before = jnp.sum(jnp.where(jnp.abs(tags_ref[...]) < first_doc, 1.0, 0.0)).astype(jnp.int32)
    reach_row = docs_ref[pl.ds(tile // 2, 1), :]
    reach = jnp.sum(jnp.where(lanes == tile % 2, reach_row, 0.0)).astype(jnp.int32)
    own_tile = 4 * BACK + tile
    lowest = jnp.maximum(own_tile - reach, 0)
    first_block = jnp.maximum(lowest, before // TILE) // 2

    m_ref[...] = jnp.full_like(m_ref, -1e30)
    l_ref[...] = jnp.zeros_like(l_ref)
    acc_ref[...] = jnp.zeros_like(acc_ref)
    query_pos = own_tile * TILE + lax.broadcasted_iota(jnp.int32, (TILE, 2 * TILE), 0)
    factor = math.log2(math.e) / math.sqrt(HEAD)

    def one_block(block, carry):
        chip = block // 2
        start = pl.multiple_of((block % 2) * 256, 256)
        keys = kv_ref[0, chip, pl.ds(start, 256), :]
        values = kv_ref[1, chip, pl.ds(start, 256), :]
        key_pos = block * 256 + lax.broadcasted_iota(jnp.int32, (TILE, 2 * TILE), 1)
        tags = tags_ref[pl.ds(block, 1), :]
        visible = (
            ((tags == query_doc) | (key_pos == query_pos))
            & (key_pos <= query_pos)
            & (key_pos >= lowest * TILE)
        )
        bias = jnp.where(visible, 0.0, -1e30)
        for head in range(4):
            scores = lax.dot_general(
                q_ref[0, head], keys, (((1,), (1,)), ((), ())), preferred_element_type=jnp.float32
            )
            scores = scores * factor + bias
            m_old = m_ref[head]
            peak = jnp.maximum(scores[:, :TILE], scores[:, TILE:])
            m_new = jnp.maximum(m_old, jnp.max(peak, axis=1, keepdims=True))
            shrink = jnp.exp2(m_old - m_new)
            left = jnp.exp2(scores[:, :TILE] - m_new)
            right = jnp.exp2(scores[:, TILE:] - m_new)
            m_ref[head] = m_new
            l_ref[head] = l_ref[head] * shrink + (left + right)
            weights = jnp.concatenate([left, right], axis=1).astype(jnp.bfloat16)
            mixed = jnp.dot(weights, values, preferred_element_type=jnp.float32)
            acc_ref[head] = acc_ref[head] * shrink + mixed
        return carry

    lax.fori_loop(first_block, own_block + 1, one_block, 0)
    for head in range(4):
        total = jnp.sum(l_ref[head], axis=1, keepdims=True)
        out_ref[:, head * HEAD : (head + 1) * HEAD] = (acc_ref[head] / total).astype(jnp.bfloat16)


def attend(queries, keys_values):
    return pl.pallas_call(
        attention_kernel,
        grid=(4,),
        in_specs=[
            pl.BlockSpec((1, 4, TILE, HEAD), lambda i: (i, 0, 0, 0)),
            pl.BlockSpec((2, BACK + 1, 528, HEAD), lambda i: (0, 0, 0, 0)),
        ],
        out_specs=pl.BlockSpec((TILE, 4 * HEAD), lambda i: (i, 0)),
        out_shape=jax.ShapeDtypeStruct((4 * TILE, 4 * HEAD), jnp.bfloat16),
        scratch_shapes=[
            pltpu.VMEM((2 * (BACK + 1), 2 * TILE), jnp.float32),
            pltpu.VMEM((8, TILE), jnp.float32),
            pltpu.VMEM((4, TILE, HEAD), jnp.float32),
            pltpu.VMEM((4, TILE, HEAD), jnp.float32),
            pltpu.VMEM((4, TILE, HEAD), jnp.float32),
        ],
        name="attend",
    )(queries, keys_values)


def output_kernel(core_ref, a_ref, own_ref, other_ref, out_ref):
    core = core_ref[0]
    dims = (((1,), (1,)), ((), ()))
    total = lax.dot_general(a_ref[core], own_ref[...], dims, preferred_element_type=jnp.float32)
    total += lax.dot_general(
        a_ref[1 - core], other_ref[...], dims, preferred_element_type=jnp.float32
    )
    out_ref[0] = total.astype(jnp.bfloat16)


def project_out(core, attended, gathered, other):
    return pl.pallas_call(
        output_kernel,
        grid=(4,),
        in_specs=[
            pl.BlockSpec(memory_space=pltpu.SMEM),
            pl.BlockSpec((2, 256, 512), lambda j: (0, 0, 0)),
            pl.BlockSpec((512, 512), lambda j: (j, 1)),
            pl.BlockSpec((512, 512), lambda j: (j, 0)),
        ],
        out_specs=pl.BlockSpec((1, 256, 512), lambda j: (j, 0, 0)),
        out_shape=jax.ShapeDtypeStruct((4, 256, 512), jnp.bfloat16),
        name="project_out",
    )(core, attended, gathered, other)


def layer(
    tokens,
    norm_gain,
    w_query,
    key_weight,
    value_weight,
    query_gain,
    key_gain,
    w_out,
    doc_ids,
    sentinel,
    tile_reach,
):
    core = lax.axis_index("core")
    core_arg = core.astype(jnp.int32).reshape(1)
    chip = lax.axis_index(CHIP)

    out_rows = w_out.T
    halves = [
        jnp.concatenate(
            [
                w_query[:, 512 * half : 512 * (half + 1)],
                out_rows[:, 512 * half : 512 * (half + 1)],
                (key_weight, value_weight)[half],
            ],
            axis=1,
        )
        for half in range(2)
    ]
    pieces = jnp.broadcast_to(jnp.stack(halves)[None], (4, 2, 16, 1152)).reshape(8, 16, 1152)
    plane = lax.all_to_all(pieces, ("y", "core"), 0, 0, tiled=True).reshape(128, 1152)
    wide = lax.all_gather(plane[:, :1024], "z", axis=0, tiled=True)
    narrow = lax.all_gather(plane[:, 1024:], "z", axis=0, tiled=True)

    whole = copies(tokens, "head").astype(jnp.float32)
    mean_square = jnp.mean(jnp.mean(whole * whole, axis=2, keepdims=True), axis=0, keepdims=True)
    normed = whole * lax.rsqrt(mean_square + EPSILON) * norm_gain.reshape(4, 1, 512)
    normed = copies(normed.astype(jnp.bfloat16), "core")

    positions = (chip * 512 + jnp.arange(512, dtype=jnp.int32)).astype(jnp.float32)
    freqs = THETA ** (-2.0 * jnp.arange(HEAD // 2, dtype=jnp.float32) / HEAD)
    angles = positions[:, None] * freqs[None, :]
    cosine, sine = jnp.cos(angles), jnp.sin(angles)
    cosine = jnp.concatenate([cosine, cosine], axis=1)
    sine = jnp.concatenate([-sine, sine], axis=1)

    tags = jnp.where(sentinel == 1, -(doc_ids + 1), doc_ids + 1).astype(jnp.bfloat16)
    extra = jnp.concatenate(
        [
            tags.reshape(2, TILE),
            jnp.pad(tile_reach.astype(jnp.bfloat16).reshape(1, 2), ((0, 0), (0, TILE - 2))),
            jnp.zeros((13, TILE), jnp.bfloat16),
        ]
    )
    own = project_keys_or_values(
        core_arg, normed, narrow, key_gain.reshape(1, HEAD), cosine, sine, extra
    )
    earlier = [
        lax.ppermute(own, CHIP, [(source, source + back) for source in range(64 - back)])
        for back in range(BACK, 0, -1)
    ]
    both = lay_window([*earlier, own])
    keys_values = lax.all_to_all(both, "core", 0, 0, tiled=True)

    queries = project_queries(normed, wide, query_gain.reshape(1, HEAD), cosine, sine)
    other = lax.ppermute(wide[:, 512:], "core", [(0, 1), (1, 0)])
    attended = attend(queries, keys_values)
    attended = lax.all_to_all(attended.reshape(2, 256, 512), "core", 0, 0, tiled=True)
    partials = project_out(core_arg, attended, wide, other)
    shares = lax.all_to_all(partials, "head", 0, 0, tiled=True)
    return jnp.sum(shares.astype(jnp.float32), axis=0).astype(jnp.bfloat16)


def solution(mesh):
    split = Mesh(mesh.devices.reshape(16, 4, 2, 4), ("z", "y", "core", "head"))
    return jax.shard_map(
        layer,
        mesh=split,
        in_specs=(
            P(TOK, "head"),
            P(),
            P(TOK, "head"),
            P(TOK, "head"),
            P(TOK, "head"),
            P(),
            P(),
            P("head", TOK),
            P(TOK),
            P(TOK),
            P(TOK),
        ),
        out_specs=P(TOK, "head"),
        check_vma=False,
    )
```

time: 334 us -> 273 us (0.82)
  the two profiles are of different devices: /device:TPU:160 before, /device:TPU:96 now
where the time goes in v1:
time: 273 us; the launch traced here: 272 us
  waiting for transfers between devices  82 us (30%)
  blocking collectives  75.7 us (28%)
  Pallas kernels  49.2 us (18%)
  starting transfers between devices  37.3 us (14%)
  between operations  13.7 us (5%)
  local copies, waits for them, and re-layouts  8.72 us (3%)
  other arithmetic  4.92 us (2%)
    all_gather x1, waiting for transfers between devices, layer(): wide = lax.all_gather(plane[:, :1024], 'z', axis=0, tiled=True)  72 us
    all_gather x1, blocking collectives, layer(): narrow = lax.all_gather(plane[:, 1024:], 'z', axis=0, tiled=True)  31.6 us
    pallas_call x1, Pallas kernels, attend(): pl.pallas_call(attention_kernel, grid=(4,), in_specs=[pl.BlockSpec((1, 4,...  31 us
    ppermute x7, starting transfers between devices, layer(): lax.ppermute(own, CHIP, [(source, source + back) for source in range(64 -...  27.3 us
    all_to_all x1, blocking collectives, layer(): shares = lax.all_to_all(partials, 'head', 0, 0, tiled=True)  19.6 us
    all_to_all x1, blocking collectives, layer(): lax.all_to_all(pieces, ('y', 'core'), 0, 0, tiled=True).reshape(128, 1152)  12.1 us
    ppermute x7, waiting for transfers between devices, layer(): lax.ppermute(own, CHIP, [(source, source + back) for source in range(64 -...  10 us
    pallas_call x1, Pallas kernels, project_queries(): pl.pallas_call(query_kernel, grid=(4,), in_specs=[pl.BlockSpec((2, 1, 256...  6.68 us
  transfers between devices with their start and end apart: 11, of which 4 were waited for; matrix products, arithmetic and copies ran while one was open for 3% of the time, Pallas kernels for 16%

profile of v1, /device:TPU:96, one launch (start us, length us, event | category | flops | bytes accessed | tf_op | source)
XLA Modules:
  0.0 271.5 jit_solution(3573886846664156835)
XLA Ops:
  6.5 0.8 fusion.11
  7.3 0.7 fusion.10
  8.1 0.7 maximum_bitcast_fusion
  8.8 12.1 %all_to_all.30 = bf16[8,16,1152]{2,1,0:T(8,128)(2,1)S(1)} all-to-all(bf16[8,16,1152]{2,1,0:T(8,128)(2,1)S(1)} %bitcast.18), channel_id=1, replica_groups=mesh['z'=16,'y'=4,'core'=2,'head'=4] {'y','core'}, dimensions={0} | all-to-all | bytes 589824 | tf_op jit(solution)/shard_map/all_to_all | solution.py:270
  20.9 0.7 slice.30
  21.7 0.0 all-gather.2.cloned.1.call-update
  21.7 1.1 broadcast_in_dim.8
  22.8 4.3 %all-to-all-start = ((bf16[4,256,512]{2,1,0:T(8,128)(2,1)}), bf16[4,256,512]{2,1,0:T(8,128)(2,1)S(1)}, u32[]{:S(2)}, u32[]{:S(2)}) async-start(bf16[4,256,512]{2,1,0:T(8,128)(2,1)} %broadcast_in_dim.8), calls=%async_computation | async-start | bytes 2097152 | tf_op jit(solution)/shard_map/all_to_all | solution.py:22
  27.1 0.1 pad.7.clone
  27.2 1.0 fusion.3
  28.2 0.0 copy-start.12
  28.2 0.0 copy-start.10
  28.2 0.0 copy-start.11
  28.2 72.0 %all-gather.2.cloned.1.call-done.w_ref.own_ref = bf16[2048,1024]{1,0:T(8,128)(2,1)} async-done(((bf16[128,1024]{1,0:T(8,128)(2,1)}), bf16[2048,1024]{1,0:T(8,128)(2,1)}) %all-gather.2.cloned.1.call-update) | async-done | bytes 4194320 | tf_op jit(solution)/shard_map/all_gather | solution.py:271
  100.2 3.1 %slice.32 = bf16[2048,512]{1,0:T(8,128)(2,1)} slice(bf16[2048,1024]{1,0:T(8,128)(2,1)} %all-gather.2.cloned.1.call-done.w_ref.own_ref), slice={[0:2048], [512:1024]} | slice | bytes 4194304 | tf_op jit(solution)/shard_map/slice | solution.py:305
  103.3 1.9 collective-permute-start.7
  105.2 1.0 pad_maximum_fusion
  106.2 0.6 fusion.7.extra_ref
  106.9 31.6 %all_gather.7.w_ref = bf16[2048,128]{1,0:T(8,128)(2,1)} all-gather(bf16[128,128]{1,0:T(8,128)(2,1)S(1)} %slice.31), channel_id=1, replica_groups=mesh['z'=16,'y'=4,'core'=2,'head'=4] {'z'}, dimensions={0}, use_global_device_ids=true | all-gather | bytes 557056 | tf_op jit(solution)/shard_map/all_gather | solution.py:272
  138.5 0.3 fusion
  138.8 0.3 fusion.2
  139.1 0.2 broadcast_in_dim.9
  139.3 6.3 %all_to_all.31.x_ref = bf16[2,4,256,512]{3,2,1,0:T(8,128)(2,1)} all-to-all(bf16[2,4,256,512]{3,2,1,0:T(8,128)(2,1)S(1)} %broadcast_in_dim.9), channel_id=1, replica_groups=mesh['z'=16,'y'=4,'core'=2,'head'=4] {'core'}, dimensions={0} | all-to-all | bytes 4194304 | tf_op jit(solution)/shard_map/all_to_all | solution.py:22
  145.6 3.4 %project_keys_or_values.1.refs_7_ = bf16[528,128]{1,0:T(8,128)(2,1)} custom-call(s32[1]{0:T(128)} %bitcast.core_ref, bf16[2,4,256,512]{3,2,1,0:T(8,128)(2,1)} %all_to_all.31.x_ref, bf16[2048,128]{1,0:T(8,128)(2,1)} %all_gather.7.w_ref, f32[1,128]{1,0:T(1,128)} %bitcast.20, f32[512,128]{1,0:T(8,128)} %get-tuple-element.14.cos_ref, ...), custom_call_target="tpu_custom_call" | custom-call | tf_op jit(solution)/shard_map/project_keys_or_values/pallas_call | solution.py:92
  149.0 6.6 %collective-permute-start = (bf16[528,128]{1,0:T(8,128)(2,1)}, bf16[528,128]{1,0:T(8,128)(2,1)S(1)}, u32[]{:S(2)}, u32[]{:S(2)}) collective-permute-start(bf16[528,128]{1,0:T(8,128)(2,1)} %project_keys_or_values.1.refs_7_), channel_id=1, source_target_pairs={{0,56},{8,64},{16,72},{24,80},{32,88},{40,96},{48,104},{56,112},{6... | collective-permute-start | bytes 405512 | tf_op jit(solution)/shard_map/ppermute | solution.py:298
  155.6 2.6 collective-permute-start.1
  158.2 3.2 %collective-permute-start.2 = (bf16[528,128]{1,0:T(8,128)(2,1)}, bf16[528,128]{1,0:T(8,128)(2,1)S(1)}, u32[]{:S(2)}, u32[]{:S(2)}) collective-permute-start(bf16[528,128]{1,0:T(8,128)(2,1)} %project_keys_or_values.1.refs_7_), channel_id=1, source_target_pairs={{0,40},{8,48},{16,56},{24,64},{32,72},{40,80},{48,88},{56,96},{64,... | collective-permute-start | bytes 405512 | tf_op jit(solution)/shard_map/ppermute | solution.py:298
  161.4 5.4 %collective-permute-start.3 = (bf16[528,128]{1,0:T(8,128)(2,1)}, bf16[528,128]{1,0:T(8,128)(2,1)S(1)}, u32[]{:S(2)}, u32[]{:S(2)}) collective-permute-start(bf16[528,128]{1,0:T(8,128)(2,1)} %project_keys_or_values.1.refs_7_), channel_id=1, source_target_pairs={{0,32},{8,40},{16,48},{24,56},{32,64},{40,72},{48,80},{56,88},{64,... | collective-permute-start | bytes 405512 | tf_op jit(solution)/shard_map/ppermute | solution.py:298
  166.8 0.0 collective-permute-done.refs_0_
  166.8 3.7 %collective-permute-start.4 = (bf16[528,128]{1,0:T(8,128)(2,1)}, bf16[528,128]{1,0:T(8,128)(2,1)S(1)}, u32[]{:S(2)}, u32[]{:S(2)}) collective-permute-start(bf16[528,128]{1,0:T(8,128)(2,1)} %project_keys_or_values.1.refs_7_), channel_id=1, source_target_pairs={{0,24},{8,32},{16,40},{24,48},{32,56},{40,64},{48,72},{56,80},{64,... | collective-permute-start | bytes 405512 | tf_op jit(solution)/shard_map/ppermute | solution.py:298
  170.5 0.0 collective-permute-done.1.refs_1_
  170.5 3.9 %collective-permute-start.5 = (bf16[528,128]{1,0:T(8,128)(2,1)}, bf16[528,128]{1,0:T(8,128)(2,1)S(1)}, u32[]{:S(2)}, u32[]{:S(2)}) collective-permute-start(bf16[528,128]{1,0:T(8,128)(2,1)} %project_keys_or_values.1.refs_7_), channel_id=1, source_target_pairs={{0,16},{8,24},{16,32},{24,40},{32,48},{40,56},{48,64},{56,72},{64,... | collective-permute-start | bytes 405512 | tf_op jit(solution)/shard_map/ppermute | solution.py:298
  174.4 0.9 collective-permute-done.2.refs_2_
  175.3 1.9 collective-permute-start.6
  177.2 0.0 collective-permute-done.3.refs_3_
  177.3 0.0 collective-permute-done.4.refs_4_
  177.3 3.1 %collective-permute-done.5.refs_5_ = bf16[528,128]{1,0:T(8,128)(2,1)S(1)} collective-permute-done((bf16[528,128]{1,0:T(8,128)(2,1)}, bf16[528,128]{1,0:T(8,128)(2,1)S(1)}, u32[]{:S(2)}, u32[]{:S(2)}) %collective-permute-start.5) | collective-permute-done | bytes 135200 | tf_op jit(solution)/shard_map/ppermute | solution.py:298
  180.4 6.0 %collective-permute-done.6.refs_6_ = bf16[528,128]{1,0:T(8,128)(2,1)S(1)} collective-permute-done((bf16[528,128]{1,0:T(8,128)(2,1)}, bf16[528,128]{1,0:T(8,128)(2,1)S(1)}, u32[]{:S(2)}, u32[]{:S(2)}) %collective-permute-start.6) | collective-permute-done | bytes 135200 | tf_op jit(solution)/shard_map/ppermute | solution.py:298
  186.5 0.6 copy-done.8
  187.1 3.0 %lay_window.1 = bf16[2,8,528,128]{3,2,1,0:T(8,128)(2,1)} custom-call(bf16[528,128]{1,0:T(8,128)(2,1)} %copy-done.2, bf16[528,128]{1,0:T(8,128)(2,1)} %copy-done.3, bf16[528,128]{1,0:T(8,128)(2,1)} %copy-done.4, bf16[528,128]{1,0:T(8,128)(2,1)} %copy-done.5, bf16[528,128]{1,0:T(8,128)(2,1)} %copy-done.6, bf16[528,128]{1,0:T(8,128)(2,1)} %copy-done.7, ...), custom_call_target="tpu_custom_call" | custom-call | tf_op jit(solution)/shard_map/lay_window/pallas_call | solution.py:110
  190.1 3.8 %all-to-all-start.3 = ((bf16[2,8,528,128]{3,2,1,0:T(8,128)(2,1)}), bf16[2,8,528,128]{3,2,1,0:T(8,128)(2,1)S(1)}, u32[]{:S(2)}, u32[]{:S(2)}) async-start(bf16[2,8,528,128]{3,2,1,0:T(8,128)(2,1)} %lay_window.1), calls=%async_computation.3 | async-start | bytes 4325376 | tf_op jit(solution)/shard_map/all_to_all | solution.py:302
  193.9 6.7 %project_queries.1.q_ref = bf16[4,4,128,128]{3,2,1,0:T(8,128)(2,1)} custom-call(bf16[2,4,256,512]{3,2,1,0:T(8,128)(2,1)} %all_to_all.31.x_ref, bf16[2048,1024]{1,0:T(8,128)(2,1)} %all-gather.2.cloned.1.call-done.w_ref.own_ref, f32[1,128]{1,0:T(1,128)} %bitcast.21, f32[512,128]{1,0:T(8,128)} %get-tuple-element.14.cos_ref, f32[512,128]{1,0:T(8,128)} %get-tuple-element.15.sin_ref), custom_call_target="tpu_custom_call" | custom-call | tf_op jit(solution)/shard_map/project_queries/pallas_call | solution.py:57
  200.6 1.3 copy-done
  201.9 31.0 %attend.1 = bf16[512,512]{1,0:T(8,128)(2,1)} custom-call(bf16[4,4,128,128]{3,2,1,0:T(8,128)(2,1)} %project_queries.1.q_ref, bf16[2,8,528,128]{3,2,1,0:T(8,128)(2,1)} %copy-done), custom_call_target="tpu_custom_call" | custom-call | tf_op jit(solution)/shard_map/attend/pallas_call | solution.py:194
  232.9 6.1 %all_to_all.32.a_ref = bf16[2,256,512]{2,1,0:T(8,128)(2,1)} all-to-all(bf16[2,256,512]{2,1,0:T(8,128)(2,1)} %bitcast.15), channel_id=1, replica_groups=mesh['z'=16,'y'=4,'core'=2,'head'=4] {'core'}, dimensions={0} | all-to-all | bytes 1048576 | tf_op jit(solution)/shard_map/all_to_all | solution.py:307
  239.0 5.1 %project_out.1 = bf16[4,256,512]{2,1,0:T(8,128)(2,1)} custom-call(s32[1]{0:T(128)} %bitcast.core_ref, bf16[2,256,512]{2,1,0:T(8,128)(2,1)} %all_to_all.32.a_ref, bf16[2048,1024]{1,0:T(8,128)(2,1)} %all-gather.2.cloned.1.call-done.w_ref.own_ref, bf16[2048,512]{1,0:T(8,128)(2,1)} %collective-permute-done.7.other_ref), custom_call_target="tpu_custom_call" | custom-call | tf_op jit(solution)/shard_map/project_out/pallas_call | solution.py:225
  244.1 19.6 %all_to_all.33 = bf16[4,256,512]{2,1,0:T(8,128)(2,1)S(1)} all-to-all(bf16[4,256,512]{2,1,0:T(8,128)(2,1)} %project_out.1), channel_id=1, replica_groups=mesh['z'=16,'y'=4,'core'=2,'head'=4] {'head'}, dimensions={0} | all-to-all | bytes 2097152 | tf_op jit(solution)/shard_map/all_to_all | solution.py:309
  263.8 0.9 reduce_sum.32
  (36 shorter events, 0.2 us)
Async XLA Ops:
  6.5 15.2 %copy-start.1 = (bf16[256,512]{1,0:T(8,128)(2,1)S(1)}, bf16[256,512]{1,0:T(8,128)(2,1)}, u32[]{:S(2)}) copy-start(bf16[256,512]{1,0:T(8,128)(2,1)} %param.11) | copy-start | bytes 786436
  6.5 93.6 %all-gather.2.cloned.1.call-start = ((), (), s32[]{:S(2)}) async-start(), calls=%async_computation.6 | async-start | bytes 4456448 | tf_op jit(solution)/shard_map/all_gather | solution.py:271
  20.9 6.1 %copy-start.9 = (f32[2048]{0:T(1024)S(1)}, f32[2048]{0:T(1024)}, u32[]{:S(2)}) copy-start(f32[2048]{0:T(1024)} %param.12) | copy-start | bytes 24580
  22.8 115.7 %all-to-all-start = ((bf16[4,256,512]{2,1,0:T(8,128)(2,1)}), bf16[4,256,512]{2,1,0:T(8,128)(2,1)S(1)}, u32[]{:S(2)}, u32[]{:S(2)}) async-start(bf16[4,256,512]{2,1,0:T(8,128)(2,1)} %broadcast_in_dim.8), calls=%async_computation | async-start | bytes 2097152 | tf_op jit(solution)/shard_map/all_to_all | solution.py:22
  28.2 77.0 %copy-start.12 = (s32[2]{0:T(128)S(1)}, s32[2]{0:T(128)}, u32[]{:S(2)}) copy-start(s32[2]{0:T(128)} %param.21) | copy-start | bytes 28
  28.2 78.0 %copy-start.10 = (s32[256]{0:T(256)S(1)}, s32[256]{0:T(256)}, u32[]{:S(2)}) copy-start(s32[256]{0:T(256)} %param.19) | copy-start | bytes 3076
  28.2 78.0 %copy-start.11 = (s32[256]{0:T(256)S(1)}, s32[256]{0:T(256)}, u32[]{:S(2)}) copy-start(s32[256]{0:T(256)} %param.20) | copy-start | bytes 3076
  103.3 135.7 %collective-permute-start.7 = (bf16[2048,512]{1,0:T(8,128)(2,1)}, bf16[2048,512]{1,0:T(8,128)(2,1)}, u32[]{:S(2)}, u32[]{:S(2)}) collective-permute-start(bf16[2048,512]{1,0:T(8,128)(2,1)} %slice.32), channel_id=1, source_target_pairs={{0,4},{4,0},{1,5},{5,1},{2,6},{6,2},{3,7},{7,3},{8,12},{12,8},{9,1... | collective-permute-start | bytes 6291464 | tf_op jit(solution)/shard_map/ppermute | solution.py:305
  149.0 17.8 %collective-permute-start = (bf16[528,128]{1,0:T(8,128)(2,1)}, bf16[528,128]{1,0:T(8,128)(2,1)S(1)}, u32[]{:S(2)}, u32[]{:S(2)}) collective-permute-start(bf16[528,128]{1,0:T(8,128)(2,1)} %project_keys_or_values.1.refs_7_), channel_id=1, source_target_pairs={{0,56},{8,64},{16,72},{24,80},{32,88},{40,96},{48,104},{56,112},{6... | collective-permute-start | bytes 405512 | tf_op jit(solution)/shard_map/ppermute | solution.py:298
  155.6 14.9 %collective-permute-start.1 = (bf16[528,128]{1,0:T(8,128)(2,1)}, bf16[528,128]{1,0:T(8,128)(2,1)S(1)}, u32[]{:S(2)}, u32[]{:S(2)}) collective-permute-start(bf16[528,128]{1,0:T(8,128)(2,1)} %project_keys_or_values.1.refs_7_), channel_id=1, source_target_pairs={{0,48},{8,56},{16,64},{24,72},{32,80},{40,88},{48,96},{56,104},{64... | collective-permute-start | bytes 405512 | tf_op jit(solution)/shard_map/ppermute | solution.py:298
  158.2 17.2 %collective-permute-start.2 = (bf16[528,128]{1,0:T(8,128)(2,1)}, bf16[528,128]{1,0:T(8,128)(2,1)S(1)}, u32[]{:S(2)}, u32[]{:S(2)}) collective-permute-start(bf16[528,128]{1,0:T(8,128)(2,1)} %project_keys_or_values.1.refs_7_), channel_id=1, source_target_pairs={{0,40},{8,48},{16,56},{24,64},{32,72},{40,80},{48,88},{56,96},{64,... | collective-permute-start | bytes 405512 | tf_op jit(solution)/shard_map/ppermute | solution.py:298
  161.4 15.8 %collective-permute-start.3 = (bf16[528,128]{1,0:T(8,128)(2,1)}, bf16[528,128]{1,0:T(8,128)(2,1)S(1)}, u32[]{:S(2)}, u32[]{:S(2)}) collective-permute-start(bf16[528,128]{1,0:T(8,128)(2,1)} %project_keys_or_values.1.refs_7_), channel_id=1, source_target_pairs={{0,32},{8,40},{16,48},{24,56},{32,64},{40,72},{48,80},{56,88},{64,... | collective-permute-start | bytes 405512 | tf_op jit(solution)/shard_map/ppermute | solution.py:298
  166.8 19.7 %copy-start.2 = (bf16[528,128]{1,0:T(8,128)(2,1)}, bf16[528,128]{1,0:T(8,128)(2,1)S(1)}, u32[]{:S(2)}) copy-start(bf16[528,128]{1,0:T(8,128)(2,1)S(1)} %collective-permute-done.refs_0_) | copy-start | bytes 405508
  166.8 10.5 %collective-permute-start.4 = (bf16[528,128]{1,0:T(8,128)(2,1)}, bf16[528,128]{1,0:T(8,128)(2,1)S(1)}, u32[]{:S(2)}, u32[]{:S(2)}) collective-permute-start(bf16[528,128]{1,0:T(8,128)(2,1)} %project_keys_or_values.1.refs_7_), channel_id=1, source_target_pairs={{0,24},{8,32},{16,40},{24,48},{32,56},{40,64},{48,72},{56,80},{64,... | collective-permute-start | bytes 405512 | tf_op jit(solution)/shard_map/ppermute | solution.py:298
  170.5 15.9 %copy-start.3 = (bf16[528,128]{1,0:T(8,128)(2,1)}, bf16[528,128]{1,0:T(8,128)(2,1)S(1)}, u32[]{:S(2)}) copy-start(bf16[528,128]{1,0:T(8,128)(2,1)S(1)} %collective-permute-done.1.refs_1_) | copy-start | bytes 405508
  170.5 9.9 %collective-permute-start.5 = (bf16[528,128]{1,0:T(8,128)(2,1)}, bf16[528,128]{1,0:T(8,128)(2,1)S(1)}, u32[]{:S(2)}, u32[]{:S(2)}) collective-permute-start(bf16[528,128]{1,0:T(8,128)(2,1)} %project_keys_or_values.1.refs_7_), channel_id=1, source_target_pairs={{0,16},{8,24},{16,32},{24,40},{32,48},{40,56},{48,64},{56,72},{64,... | collective-permute-start | bytes 405512 | tf_op jit(solution)/shard_map/ppermute | solution.py:298
  175.3 11.1 %copy-start.4 = (bf16[528,128]{1,0:T(8,128)(2,1)}, bf16[528,128]{1,0:T(8,128)(2,1)S(1)}, u32[]{:S(2)}) copy-start(bf16[528,128]{1,0:T(8,128)(2,1)S(1)} %collective-permute-done.2.refs_2_) | copy-start | bytes 405508
  175.3 11.1 %collective-permute-start.6 = (bf16[528,128]{1,0:T(8,128)(2,1)}, bf16[528,128]{1,0:T(8,128)(2,1)S(1)}, u32[]{:S(2)}, u32[]{:S(2)}) collective-permute-start(bf16[528,128]{1,0:T(8,128)(2,1)} %project_keys_or_values.1.refs_7_), channel_id=1, source_target_pairs={{0,8},{8,16},{16,24},{24,32},{32,40},{40,48},{48,56},{56,64},{64,7... | collective-permute-start | bytes 405512 | tf_op jit(solution)/shard_map/ppermute | solution.py:298
  177.2 9.2 %copy-start.5 = (bf16[528,128]{1,0:T(8,128)(2,1)}, bf16[528,128]{1,0:T(8,128)(2,1)S(1)}, u32[]{:S(2)}) copy-start(bf16[528,128]{1,0:T(8,128)(2,1)S(1)} %collective-permute-done.3.refs_3_) | copy-start | bytes 405508
  177.3 9.2 %copy-start.6 = (bf16[528,128]{1,0:T(8,128)(2,1)}, bf16[528,128]{1,0:T(8,128)(2,1)S(1)}, u32[]{:S(2)}) copy-start(bf16[528,128]{1,0:T(8,128)(2,1)S(1)} %collective-permute-done.4.refs_4_) | copy-start | bytes 405508
  180.4 6.0 %copy-start.7 = (bf16[528,128]{1,0:T(8,128)(2,1)}, bf16[528,128]{1,0:T(8,128)(2,1)S(1)}, u32[]{:S(2)}) copy-start(bf16[528,128]{1,0:T(8,128)(2,1)S(1)} %collective-permute-done.5.refs_5_) | copy-start | bytes 405508
  186.5 0.7 copy-start.8
  190.1 10.5 %all-to-all-start.3 = ((bf16[2,8,528,128]{3,2,1,0:T(8,128)(2,1)}), bf16[2,8,528,128]{3,2,1,0:T(8,128)(2,1)S(1)}, u32[]{:S(2)}, u32[]{:S(2)}) async-start(bf16[2,8,528,128]{3,2,1,0:T(8,128)(2,1)} %lay_window.1), calls=%async_computation.3 | async-start | bytes 4325376 | tf_op jit(solution)/shard_map/all_to_all | solution.py:302
  200.6 1.3 copy-start
Sparse Core Ops, SparseCore 0:
  21.8 78.3 all-gather.1

commit v2 on v1

v2 whole, which is shorter than its diff:
```python
import functools
import math

import jax
import jax.numpy as jnp
from jax import lax
from jax.experimental import pallas as pl
from jax.experimental.pallas import tpu as pltpu
from jax.sharding import Mesh, PartitionSpec as P


HEAD = 128
TILE = 128
KEYS = 512
WINDOW = 4096
BACK = 7
EPSILON = 1e-06
THETA = 10000000.0
TOK = ("z", "y", "core")
CHIP = ("z", "y")


def copies(shard, axis):
    count = lax.axis_size(axis)
    return lax.all_to_all(
        jnp.broadcast_to(shard[None], (count, *shard.shape)), axis, 0, 0, tiled=True
    )


def normed_and_turned(values, gain, cosine, sine):
    mean_square = jnp.mean(values * values, axis=-1, keepdims=True)
    scaled = values * lax.rsqrt(mean_square + EPSILON) * gain
    return scaled * cosine + pltpu.roll(scaled, HEAD // 2, 1) * sine


def query_kernel(x_ref, w_ref, gain_ref, cos_ref, sin_ref, out_ref):
    total = functools.reduce(
        jnp.add,
        [
            jnp.dot(
                x_ref[0, part],
                w_ref[part * 512 : (part + 1) * 512, :],
                preferred_element_type=jnp.float32,
            )
            for part in range(4)
        ],
    )
    for tile in range(2):
        rows = slice(tile * TILE, (tile + 1) * TILE)
        for head in range(4):
            one = total[rows, head * HEAD : (head + 1) * HEAD]
            turned = normed_and_turned(one, gain_ref[...], cos_ref[rows, :], sin_ref[rows, :])
            out_ref[tile, head] = turned.astype(jnp.bfloat16)


def project_queries(x, weights, gain, cosine, sine):
    return pl.pallas_call(
        query_kernel,
        grid=(2,),
        in_specs=[
            pl.BlockSpec((1, 4, 256, 512), lambda k: (k, 0, 0, 0)),
            pl.BlockSpec((2048, 512), lambda k: (0, 0)),
            pl.BlockSpec((1, HEAD), lambda k: (0, 0)),
            pl.BlockSpec((256, HEAD), lambda k: (k, 0)),
            pl.BlockSpec((256, HEAD), lambda k: (k, 0)),
        ],
        out_specs=pl.BlockSpec((2, 4, TILE, HEAD), lambda k: (k, 0, 0, 0)),
        out_shape=jax.ShapeDtypeStruct((4, 4, TILE, HEAD), jnp.bfloat16),
        name="project_queries",
    )(x, weights, gain, cosine, sine)


def key_value_kernel(
    core_ref, x_ref, norm_ref, w_ref, gain_ref, cos_ref, sin_ref, extra_ref, out_ref, normed_ref
):
    is_key = core_ref[0] == 0
    for half in range(2):
        rows = pl.ds(half * 256, 256)
        parts = [x_ref[half, part].astype(jnp.float32) for part in range(4)]
        squares = functools.reduce(jnp.add, [part * part for part in parts])
        mean_square = jnp.sum(squares, axis=1, keepdims=True) / 2048
        level = lax.rsqrt(mean_square + EPSILON)
        products = []
        for part in range(4):
            normed = (parts[part] * level * norm_ref[part]).astype(jnp.bfloat16)
            normed_ref[half, part] = normed
            products.append(
                jnp.dot(
                    normed,
                    w_ref[part * 512 : (part + 1) * 512, :],
                    preferred_element_type=jnp.float32,
                )
            )
        total = functools.reduce(jnp.add, products)
        turned = normed_and_turned(total, gain_ref[...], cos_ref[rows, :], sin_ref[rows, :])
        out_ref[rows, :] = jnp.where(is_key, turned, total).astype(jnp.bfloat16)
    out_ref[512:528, :] = extra_ref[...]


def project_keys_or_values(core, x, norm_gain, weights, gain, cosine, sine, extra):
    vmem = pl.BlockSpec(memory_space=pltpu.VMEM)
    return pl.pallas_call(
        key_value_kernel,
        in_specs=[pl.BlockSpec(memory_space=pltpu.SMEM)] + [vmem] * 7,
        out_specs=(vmem, vmem),
        out_shape=(
            jax.ShapeDtypeStruct((528, HEAD), jnp.bfloat16),
            jax.ShapeDtypeStruct((2, 4, 256, 512), jnp.bfloat16),
        ),
        name="project_keys_or_values",
    )(core, x, norm_gain, weights, gain, cosine, sine, extra)


def window_kernel(*refs):
    out_ref = refs[-1]
    for place, ref in enumerate(refs[:-1]):
        out_ref[512 * place : 512 * (place + 1), :] = ref[:512, :]
        out_ref[WINDOW + 16 * place : WINDOW + 16 * (place + 1), :] = ref[512:, :]


def lay_window(blocks):
    vmem = pl.BlockSpec(memory_space=pltpu.VMEM)
    return pl.pallas_call(
        window_kernel,
        in_specs=[vmem] * len(blocks),
        out_specs=vmem,
        out_shape=jax.ShapeDtypeStruct((WINDOW + 128, HEAD), jnp.bfloat16),
        name="lay_window",
    )(*blocks)


def attention_kernel(
    core_ref, q_ref, own_ref, other_ref, out_ref, kv_ref, tags_ref, reach_ref, m_ref, l_ref, acc_ref
):
    tile = pl.program_id(0)
    lanes = lax.broadcasted_iota(jnp.int32, (1, TILE), 1)

    @pl.when(tile == 0)
    def _():
        kv_ref[core_ref[0]] = own_ref[...]
        kv_ref[1 - core_ref[0]] = other_ref[...]
        for chip in range(BACK + 1):
            for core in range(2):
                row = WINDOW + 16 * chip
                extra = kv_ref[core, row : row + 16, :].astype(jnp.float32)
                place = 4 * chip + 2 * core
                tags_ref[place : place + 2, :] = extra[0:2]
                if chip == BACK:
                    reach_ref[core : core + 1, :] = extra[2:3]

    own_tile = 4 * BACK + tile
    doc_row = jnp.abs(tags_ref[pl.ds(own_tile, 1), :])
    diagonal = lax.broadcasted_iota(jnp.int32, (TILE, TILE), 0) == lax.broadcasted_iota(
        jnp.int32, (TILE, TILE), 1
    )
    query_doc = jnp.sum(jnp.where(diagonal, doc_row, 0.0), axis=1, keepdims=True)
    first_doc = jnp.sum(jnp.where(lanes == 0, doc_row, 0.0))
    before = jnp.sum(jnp.where(jnp.abs(tags_ref[...]) < first_doc, 1.0, 0.0)).astype(jnp.int32)
    reach_row = reach_ref[pl.ds(tile // 2, 1), :]
    reach = jnp.sum(jnp.where(lanes == tile % 2, reach_row, 0.0)).astype(jnp.int32)
    lowest = jnp.maximum(own_tile - reach, 0)
    first_tile = jnp.maximum(lowest, before // TILE)
    block_count = (own_tile - first_tile) // 4 + 1
    factor = math.log2(math.e) / math.sqrt(HEAD)
    query = q_ref[0].reshape(4 * TILE, HEAD)
    wide_doc = jnp.broadcast_to(query_doc, (TILE, TILE))

    def scores_of(start_tile):
        start = pl.multiple_of(start_tile * TILE, TILE)
        return lax.dot_general(
            query,
            kv_ref[0, pl.ds(start, KEYS), :],
            (((1,), (1,)), ((), ())),
            preferred_element_type=jnp.float32,
        )

    def values_of(start_tile):
        return kv_ref[1, pl.ds(pl.multiple_of(start_tile * TILE, TILE), KEYS), :]

    def tags_of(start_tile, end_tile):
        rows = []
        for place in range(4):
            inside = (start_tile + place >= lowest) & (start_tile + place < end_tile)
            rows.append(jnp.where(inside, tags_ref[pl.ds(start_tile + place, 1), :], 0.0))
        return rows

    def lay_sums(pieces, peak):
        exps = [jnp.exp2(piece * factor - peak) for piece in pieces]
        return functools.reduce(jnp.add, exps), [piece.astype(jnp.bfloat16) for piece in exps]

    start_tile = own_tile - 3
    scores = scores_of(start_tile)
    tags = tags_of(start_tile, own_tile + 1)
    key_lane = lax.broadcasted_iota(jnp.int32, (TILE, TILE), 1)
    query_row = lax.broadcasted_iota(jnp.int32, (TILE, TILE), 0)
    visible = [wide_doc == tags[place] for place in range(4)]
    visible[3] = (visible[3] & (key_lane < query_row)) | diagonal
    weights = []
    for head in range(4):
        rows = slice(head * TILE, (head + 1) * TILE)
        pieces = [
            jnp.where(visible[place], scores[rows, place * TILE : (place + 1) * TILE], -1e30)
            for place in range(4)
        ]
        peak = jnp.max(functools.reduce(jnp.maximum, pieces), axis=1, keepdims=True) * factor
        peak = jnp.broadcast_to(peak, (TILE, HEAD))
        total, exps = lay_sums(pieces, peak)
        m_ref[rows, :] = peak
        l_ref[rows, :] = total
        weights.append(jnp.concatenate(exps, axis=1))
    acc_ref[...] = jnp.dot(
        jnp.concatenate(weights, axis=0), values_of(start_tile), preferred_element_type=jnp.float32
    )

    def one_block(block, carry):
        end_tile = own_tile + 1 - 4 * block
        start_tile = jnp.maximum(end_tile - 4, 0)
        scores = scores_of(start_tile)
        tags = tags_of(start_tile, end_tile)
        visible = [wide_doc == tags[place] for place in range(4)]
        weights, shrinks = [], []
        for head in range(4):
            rows = slice(head * TILE, (head + 1) * TILE)
            pieces = [
                jnp.where(visible[place], scores[rows, place * TILE : (place + 1) * TILE], -1e30)
                for place in range(4)
            ]
            peak = jnp.max(functools.reduce(jnp.maximum, pieces), axis=1, keepdims=True) * factor
            m_old = m_ref[rows, :]
            m_new = jnp.maximum(m_old, peak)
            total, exps = lay_sums(pieces, m_new)
            shrink = jnp.exp2(m_old - m_new)
            m_ref[rows, :] = m_new
            l_ref[rows, :] = l_ref[rows, :] * shrink + total
            shrinks.append(shrink)
            weights.append(jnp.concatenate(exps, axis=1))
        mixed = jnp.dot(
            jnp.concatenate(weights, axis=0),
            values_of(start_tile),
            preferred_element_type=jnp.float32,
        )
        for head in range(4):
            rows = slice(head * TILE, (head + 1) * TILE)
            acc_ref[rows, :] = acc_ref[rows, :] * shrinks[head] + mixed[rows]
        return carry

    lax.fori_loop(1, block_count, one_block, 0)
    for head in range(4):
        rows = slice(head * TILE, (head + 1) * TILE)
        total = jnp.sum(l_ref[rows, :], axis=1, keepdims=True)
        out_ref[:, head * HEAD : (head + 1) * HEAD] = (acc_ref[rows, :] / total).astype(
            jnp.bfloat16
        )


def attend(core, queries, own, other):
    rows = WINDOW + 128
    return pl.pallas_call(
        attention_kernel,
        grid=(4,),
        in_specs=[
            pl.BlockSpec(memory_space=pltpu.SMEM),
            pl.BlockSpec((1, 4, TILE, HEAD), lambda i: (i, 0, 0, 0)),
            pl.BlockSpec((rows, HEAD), lambda i: (0, 0)),
            pl.BlockSpec((rows, HEAD), lambda i: (0, 0)),
        ],
        out_specs=pl.BlockSpec((TILE, 4 * HEAD), lambda i: (i, 0)),
        out_shape=jax.ShapeDtypeStruct((4 * TILE, 4 * HEAD), jnp.bfloat16),
        scratch_shapes=[
            pltpu.VMEM((2, rows, HEAD), jnp.bfloat16),
            pltpu.VMEM((4 * (BACK + 1), TILE), jnp.float32),
            pltpu.VMEM((8, TILE), jnp.float32),
            pltpu.VMEM((4 * TILE, HEAD), jnp.float32),
            pltpu.VMEM((4 * TILE, HEAD), jnp.float32),
            pltpu.VMEM((4 * TILE, HEAD), jnp.float32),
        ],
        name="attend",
    )(core, queries, own, other)


def output_kernel(core_ref, a_ref, own_ref, other_ref, out_ref):
    core = core_ref[0]
    dims = (((1,), (1,)), ((), ()))
    total = lax.dot_general(a_ref[core], own_ref[...], dims, preferred_element_type=jnp.float32)
    total += lax.dot_general(
        a_ref[1 - core], other_ref[...], dims, preferred_element_type=jnp.float32
    )
    out_ref[0] = total.astype(jnp.bfloat16)


def project_out(core, attended, gathered, other):
    return pl.pallas_call(
        output_kernel,
        grid=(4,),
        in_specs=[
            pl.BlockSpec(memory_space=pltpu.SMEM),
            pl.BlockSpec((2, 256, 512), lambda j: (0, 0, 0)),
            pl.BlockSpec((512, 512), lambda j: (j, 1)),
            pl.BlockSpec((512, 512), lambda j: (j, 0)),
        ],
        out_specs=pl.BlockSpec((1, 256, 512), lambda j: (j, 0, 0)),
        out_shape=jax.ShapeDtypeStruct((4, 256, 512), jnp.bfloat16),
        name="project_out",
    )(core, attended, gathered, other)


def layer(
    tokens,
    norm_gain,
    w_query,
    key_weight,
    value_weight,
    query_gain,
    key_gain,
    w_out,
    doc_ids,
    sentinel,
    tile_reach,
):
    core = lax.axis_index("core")
    core_arg = core.astype(jnp.int32).reshape(1)
    chip = lax.axis_index(CHIP)

    out_rows = w_out.T
    halves = [
        jnp.concatenate(
            [
                w_query[:, 512 * half : 512 * (half + 1)],
                out_rows[:, 512 * half : 512 * (half + 1)],
                (key_weight, value_weight)[half],
            ],
            axis=1,
        )
        for half in range(2)
    ]
    pieces = jnp.broadcast_to(jnp.stack(halves)[None], (4, 2, 16, 1152)).reshape(8, 16, 1152)
    plane = lax.all_to_all(pieces, ("y", "core"), 0, 0, tiled=True).reshape(128, 1152)
    wide = lax.all_gather(plane[:, :1024], "z", axis=0, tiled=True)
    narrow = lax.all_gather(plane[:, 1024:], "z", axis=0, tiled=True)

    whole = copies(tokens, ("core", "head")).reshape(2, 4, 256, 512)

    positions = (chip * 512 + jnp.arange(512, dtype=jnp.int32)).astype(jnp.float32)
    freqs = THETA ** (-2.0 * jnp.arange(HEAD // 2, dtype=jnp.float32) / HEAD)
    angles = positions[:, None] * freqs[None, :]
    cosine, sine = jnp.cos(angles), jnp.sin(angles)
    cosine = jnp.concatenate([cosine, cosine], axis=1)
    sine = jnp.concatenate([-sine, sine], axis=1)

    tags = jnp.where(sentinel == 1, -(doc_ids + 1), doc_ids + 1).astype(jnp.bfloat16)
    extra = jnp.concatenate(
        [
            tags.reshape(2, TILE),
            jnp.pad(tile_reach.astype(jnp.bfloat16).reshape(1, 2), ((0, 0), (0, TILE - 2))),
            jnp.zeros((13, TILE), jnp.bfloat16),
        ]
    )
    own, normed = project_keys_or_values(
        core_arg,
        whole,
        norm_gain.reshape(4, 1, 512),
        narrow,
        key_gain.reshape(1, HEAD),
        cosine,
        sine,
        extra,
    )
    earlier = [
        lax.ppermute(own, CHIP, [(source, source + back) for source in range(64 - back)])
        for back in range(BACK, 0, -1)
    ]
    window = lay_window([*earlier, own])
    window_other = lax.ppermute(window, "core", [(0, 1), (1, 0)])

    queries = project_queries(normed, wide, query_gain.reshape(1, HEAD), cosine, sine)
    other = lax.ppermute(wide[:, 512:], "core", [(0, 1), (1, 0)])
    attended = attend(core_arg, queries, window, window_other)
    attended = lax.all_to_all(attended.reshape(2, 256, 512), "core", 0, 0, tiled=True)
    partials = project_out(core_arg, attended, wide, other)
    shares = lax.all_to_all(partials, "head", 0, 0, tiled=True)
    return jnp.sum(shares.astype(jnp.float32), axis=0).astype(jnp.bfloat16)


def solution(mesh):
    split = Mesh(mesh.devices.reshape(16, 4, 2, 4), ("z", "y", "core", "head"))
    return jax.shard_map(
        layer,
        mesh=split,
        in_specs=(
            P(TOK, "head"),
            P(),
            P(TOK, "head"),
            P(TOK, "head"),
            P(TOK, "head"),
            P(),
            P(),
            P("head", TOK),
            P(TOK),
            P(TOK),
            P(TOK),
        ),
        out_specs=P(TOK, "head"),
        check_vma=False,
    )
```

time: 273 us -> 245 us (0.90)
  Pallas kernels: 49.2 us -> 32.3 us
  blocking collectives: 75.7 us -> 69.7 us
  waiting for transfers between devices: 82 us -> 78.5 us
    pallas_call x2, Pallas kernels: 37.7 us -> 20.5 us  [the longest x1 15.7 us: attend(): pl.pallas_call(attention_kernel, grid=(4,), in_specs=[pl.BlockSpec(memory...]
    all_to_all x1 -> x0, blocking collectives: 6.3 us -> none  [copies(): lax.all_to_all(jnp.broadcast_to(shard[None], (count, *shard.shape)), axis...]
    all_to_all x1 -> x0, starting transfers between devices: 3.77 us -> none  [layer(): keys_values = lax.all_to_all(both, 'core', 0, 0, tiled=True)]
    ppermute x7, waiting for transfers between devices: 10 us -> 7.27 us  [layer(): lax.ppermute(own, CHIP, [(source, source + back) for source in range(64 -...]
  transfers between devices with their start and end apart: 11 -> 11, of which waited for: 4 -> 3; matrix products, arithmetic and copies ran while one was open for 3% -> 3% of each run, Pallas kernels for 16% -> 11%
where the time goes in v2:
time: 245 us; the launch traced here: 244 us
  waiting for transfers between devices  78.5 us (32%)
  blocking collectives  69.7 us (28%)
  starting transfers between devices  35.1 us (14%)
  Pallas kernels  32.3 us (13%)
  between operations  13.7 us (6%)
  local copies, waits for them, and re-layouts  10.1 us (4%)
  other arithmetic  4.3 us (2%)
    all_gather x1, waiting for transfers between devices, layer(): wide = lax.all_gather(plane[:, :1024], 'z', axis=0, tiled=True)  71.2 us
    all_gather x1, blocking collectives, layer(): narrow = lax.all_gather(plane[:, 1024:], 'z', axis=0, tiled=True)  31.6 us
    ppermute x7, starting transfers between devices, layer(): lax.ppermute(own, CHIP, [(source, source + back) for source in range(64 -...  26.9 us
    all_to_all x1, blocking collectives, layer(): shares = lax.all_to_all(partials, 'head', 0, 0, tiled=True)  19.8 us
    pallas_call x1, Pallas kernels, attend(): pl.pallas_call(attention_kernel, grid=(4,), in_specs=[pl.BlockSpec(memory...  15.7 us
    all_to_all x1, blocking collectives, layer(): lax.all_to_all(pieces, ('y', 'core'), 0, 0, tiled=True).reshape(128, 1152)  12.1 us
    ppermute x7, waiting for transfers between devices, layer(): lax.ppermute(own, CHIP, [(source, source + back) for source in range(64 -...  7.27 us
    all_to_all x1, blocking collectives, layer(): lax.all_to_all(attended.reshape(2, 256, 512), 'core', 0, 0, tiled=True)  6.1 us
  transfers between devices with their start and end apart: 11, of which 3 were waited for; matrix products, arithmetic and copies ran while one was open for 3% of the time, Pallas kernels for 11%

profile of v2, /device:TPU:96, one launch (start us, length us, event | category | flops | bytes accessed | tf_op | source)
XLA Modules:
  0.0 243.7 jit_solution(8901835065982334188)
XLA Ops:
  6.5 0.0 all-gather.2.cloned.1.call-start
  6.5 0.8 fusion.8
  7.3 0.7 fusion.7
  8.1 0.7 maximum_bitcast_fusion
  8.8 12.1 %all_to_all.20 = bf16[8,16,1152]{2,1,0:T(8,128)(2,1)S(1)} all-to-all(bf16[8,16,1152]{2,1,0:T(8,128)(2,1)S(1)} %bitcast.21), channel_id=1, replica_groups=mesh['z'=16,'y'=4,'core'=2,'head'=4] {'y','core'}, dimensions={0} | all-to-all | bytes 589824 | tf_op jit(solution)/shard_map/all_to_all | solution.py:337
  20.9 0.7 slice.31
  21.7 0.0 all-gather.2.cloned.1.call-update
  21.7 1.6 broadcast_in_dim.6
  23.3 4.4 %all-to-all-start = ((bf16[8,256,512]{2,1,0:T(8,128)(2,1)}), bf16[8,256,512]{2,1,0:T(8,128)(2,1)S(1)}, u32[]{:S(2)}, u32[]{:S(2)}) async-start(bf16[8,256,512]{2,1,0:T(8,128)(2,1)} %broadcast_in_dim.6), calls=%async_computation | async-start | bytes 4194304 | tf_op jit(solution)/shard_map/all_to_all | solution.py:25
  27.7 1.0 fusion
  28.7 0.0 copy-start.10
  28.8 0.0 copy-start.11
  28.8 71.2 %all-gather.2.cloned.1.call-done.w_ref.own_ref = bf16[2048,1024]{1,0:T(8,128)(2,1)} async-done(((bf16[128,1024]{1,0:T(8,128)(2,1)}), bf16[2048,1024]{1,0:T(8,128)(2,1)}) %all-gather.2.cloned.1.call-update) | async-done | bytes 4194320 | tf_op jit(solution)/shard_map/all_gather | solution.py:338
  99.9 3.1 %slice.32 = bf16[2048,512]{1,0:T(8,128)(2,1)} slice(bf16[2048,1024]{1,0:T(8,128)(2,1)} %all-gather.2.cloned.1.call-done.w_ref.own_ref), slice={[0:2048], [512:1024]} | slice | bytes 4194304 | tf_op jit(solution)/shard_map/slice | solution.py:376
  103.1 1.9 collective-permute-start.8
  105.0 1.0 pad_maximum_fusion
  106.0 0.1 pad.7.clone
  106.1 0.7 fusion.4.extra_ref
  106.7 31.6 %all_gather.6.w_ref = bf16[2048,128]{1,0:T(8,128)(2,1)} all-gather(bf16[128,128]{1,0:T(8,128)(2,1)S(1)} %slice.30), channel_id=1, replica_groups=mesh['z'=16,'y'=4,'core'=2,'head'=4] {'z'}, dimensions={0}, use_global_device_ids=true | all-gather | bytes 557056 | tf_op jit(solution)/shard_map/all_gather | solution.py:339
  138.4 0.0 all-to-all-done
  138.4 1.4 copy-done
  139.7 4.3 %project_keys_or_values.1 = (bf16[528,128]{1,0:T(8,128)(2,1)}, bf16[2,4,256,512]{3,2,1,0:T(8,128)(2,1)}) custom-call(s32[1]{0:T(128)} %bitcast.core_ref, bf16[2,4,256,512]{3,2,1,0:T(8,128)(2,1)} %bitcast.17, f32[4,1,512]{2,1,0:T(1,128)} %bitcast.23, bf16[2048,128]{1,0:T(8,128)(2,1)} %all_gather.6.w_ref, f32[1,128]{1,0:T(1,128)} %bitcast.24, ...), custom_call_target="tpu_custom_call" | custom-call | tf_op jit(solution)/shard_map/project_keys_or_values/pallas_call | solution.py:102
  144.0 7.0 %collective-permute-start = (bf16[528,128]{1,0:T(8,128)(2,1)}, bf16[528,128]{1,0:T(8,128)(2,1)S(1)}, u32[]{:S(2)}, u32[]{:S(2)}) collective-permute-start(bf16[528,128]{1,0:T(8,128)(2,1)} %get-tuple-element.8.refs_7_), channel_id=1, source_target_pairs={{0,56},{8,64},{16,72},{24,80},{32,88},{40,96},{48,104},{56,112},{6... | collective-permute-start | bytes 405512 | tf_op jit(solution)/shard_map/ppermute | solution.py:369
  151.0 2.2 collective-permute-start.1
  153.3 3.5 %collective-permute-start.2 = (bf16[528,128]{1,0:T(8,128)(2,1)}, bf16[528,128]{1,0:T(8,128)(2,1)S(1)}, u32[]{:S(2)}, u32[]{:S(2)}) collective-permute-start(bf16[528,128]{1,0:T(8,128)(2,1)} %get-tuple-element.8.refs_7_), channel_id=1, source_target_pairs={{0,40},{8,48},{16,56},{24,64},{32,72},{40,80},{48,88},{56,96},{64,... | collective-permute-start | bytes 405512 | tf_op jit(solution)/shard_map/ppermute | solution.py:369
  156.8 5.0 %collective-permute-start.3 = (bf16[528,128]{1,0:T(8,128)(2,1)}, bf16[528,128]{1,0:T(8,128)(2,1)S(1)}, u32[]{:S(2)}, u32[]{:S(2)}) collective-permute-start(bf16[528,128]{1,0:T(8,128)(2,1)} %get-tuple-element.8.refs_7_), channel_id=1, source_target_pairs={{0,32},{8,40},{16,48},{24,56},{32,64},{40,72},{48,80},{56,88},{64,... | collective-permute-start | bytes 405512 | tf_op jit(solution)/shard_map/ppermute | solution.py:369
  161.8 0.0 collective-permute-done.refs_0_
  161.8 3.9 %collective-permute-start.4 = (bf16[528,128]{1,0:T(8,128)(2,1)}, bf16[528,128]{1,0:T(8,128)(2,1)S(1)}, u32[]{:S(2)}, u32[]{:S(2)}) collective-permute-start(bf16[528,128]{1,0:T(8,128)(2,1)} %get-tuple-element.8.refs_7_), channel_id=1, source_target_pairs={{0,24},{8,32},{16,40},{24,48},{32,56},{40,64},{48,72},{56,80},{64,... | collective-permute-start | bytes 405512 | tf_op jit(solution)/shard_map/ppermute | solution.py:369
  165.6 0.0 collective-permute-done.1.refs_1_
  165.7 3.4 %collective-permute-start.5 = (bf16[528,128]{1,0:T(8,128)(2,1)}, bf16[528,128]{1,0:T(8,128)(2,1)S(1)}, u32[]{:S(2)}, u32[]{:S(2)}) collective-permute-start(bf16[528,128]{1,0:T(8,128)(2,1)} %get-tuple-element.8.refs_7_), channel_id=1, source_target_pairs={{0,16},{8,24},{16,32},{24,40},{32,48},{40,56},{48,64},{56,72},{64,... | collective-permute-start | bytes 405512 | tf_op jit(solution)/shard_map/ppermute | solution.py:369
  169.1 0.0 collective-permute-done.2.refs_2_
  169.1 1.9 collective-permute-start.6
  171.0 0.0 collective-permute-done.3.refs_3_
  171.0 0.0 collective-permute-done.4.refs_4_
  171.1 4.2 %collective-permute-done.5.refs_5_ = bf16[528,128]{1,0:T(8,128)(2,1)S(1)} collective-permute-done((bf16[528,128]{1,0:T(8,128)(2,1)}, bf16[528,128]{1,0:T(8,128)(2,1)S(1)}, u32[]{:S(2)}, u32[]{:S(2)}) %collective-permute-start.5) | collective-permute-done | bytes 135200 | tf_op jit(solution)/shard_map/ppermute | solution.py:369
  175.3 3.0 %collective-permute-done.6.refs_6_ = bf16[528,128]{1,0:T(8,128)(2,1)S(1)} collective-permute-done((bf16[528,128]{1,0:T(8,128)(2,1)}, bf16[528,128]{1,0:T(8,128)(2,1)S(1)}, u32[]{:S(2)}, u32[]{:S(2)}) %collective-permute-start.6) | collective-permute-done | bytes 135200 | tf_op jit(solution)/shard_map/ppermute | solution.py:369
  178.4 0.7 copy-done.9
  179.0 2.4 lay_window.1.own_ref
  181.4 1.9 collective-permute-start.7
  183.3 4.8 %project_queries.1.q_ref = bf16[4,4,128,128]{3,2,1,0:T(8,128)(2,1)} custom-call(bf16[2,4,256,512]{3,2,1,0:T(8,128)(2,1)} %get-tuple-element.7.x_ref, bf16[2048,1024]{1,0:T(8,128)(2,1)} %all-gather.2.cloned.1.call-done.w_ref.own_ref, f32[1,128]{1,0:T(1,128)} %bitcast.25, f32[512,128]{1,0:T(8,128)} %get-tuple-element.18.cos_ref, ...), custom_call_target="tpu_custom_call" | custom-call | tf_op jit(solution)/shard_map/project_queries/pallas_call | solution.py:57
  188.1 0.0 collective-permute-done.7.other_ref
  188.1 1.0 copy-done.1
  189.2 15.7 %attend.1 = bf16[512,512]{1,0:T(8,128)(2,1)} custom-call(s32[1]{0:T(128)} %bitcast.core_ref, bf16[4,4,128,128]{3,2,1,0:T(8,128)(2,1)} %project_queries.1.q_ref, bf16[4224,128]{1,0:T(8,128)(2,1)} %lay_window.1.own_ref, bf16[4224,128]{1,0:T(8,128)(2,1)} %copy-done.1), custom_call_target="tpu_custom_call" | custom-call | tf_op jit(solution)/shard_map/attend/pallas_call | solution.py:258
  204.9 6.1 %all_to_all.21.a_ref = bf16[2,256,512]{2,1,0:T(8,128)(2,1)} all-to-all(bf16[2,256,512]{2,1,0:T(8,128)(2,1)} %bitcast.18), channel_id=1, replica_groups=mesh['z'=16,'y'=4,'core'=2,'head'=4] {'core'}, dimensions={0} | all-to-all | bytes 1048576 | tf_op jit(solution)/shard_map/all_to_all | solution.py:378
  211.0 0.0 collective-permute-done.8.other_ref
  211.0 5.1 %project_out.1 = bf16[4,256,512]{2,1,0:T(8,128)(2,1)} custom-call(s32[1]{0:T(128)} %bitcast.core_ref, bf16[2,256,512]{2,1,0:T(8,128)(2,1)} %all_to_all.21.a_ref, bf16[2048,1024]{1,0:T(8,128)(2,1)} %all-gather.2.cloned.1.call-done.w_ref.own_ref, bf16[2048,512]{1,0:T(8,128)(2,1)} %collective-permute-done.8.other_ref), custom_call_target="tpu_custom_call" | custom-call | tf_op jit(solution)/shard_map/project_out/pallas_call | solution.py:292
  216.2 19.8 %all_to_all.22 = bf16[4,256,512]{2,1,0:T(8,128)(2,1)S(1)} all-to-all(bf16[4,256,512]{2,1,0:T(8,128)(2,1)} %project_out.1), channel_id=1, replica_groups=mesh['z'=16,'y'=4,'core'=2,'head'=4] {'head'}, dimensions={0} | all-to-all | bytes 2097152 | tf_op jit(solution)/shard_map/all_to_all | solution.py:380
  236.0 0.9 reduce_sum.12
  (29 shorter events, 0.1 us)
Async XLA Ops:
  6.5 15.2 %copy-start.2 = (bf16[256,512]{1,0:T(8,128)(2,1)S(1)}, bf16[256,512]{1,0:T(8,128)(2,1)}, u32[]{:S(2)}) copy-start(bf16[256,512]{1,0:T(8,128)(2,1)} %param.11) | copy-start | bytes 786436
  6.5 93.4 %all-gather.2.cloned.1.call-start = ((), (), s32[]{:S(2)}) async-start(), calls=%async_computation.4 | async-start | bytes 4456448 | tf_op jit(solution)/shard_map/all_gather | solution.py:338
  23.3 4.5 %copy-start.12 = (s32[2]{0:T(128)S(1)}, s32[2]{0:T(128)}, u32[]{:S(2)}) copy-start(s32[2]{0:T(128)} %param.21) | copy-start | bytes 28
  23.3 115.1 %all-to-all-start = ((bf16[8,256,512]{2,1,0:T(8,128)(2,1)}), bf16[8,256,512]{2,1,0:T(8,128)(2,1)S(1)}, u32[]{:S(2)}, u32[]{:S(2)}) async-start(bf16[8,256,512]{2,1,0:T(8,128)(2,1)} %broadcast_in_dim.6), calls=%async_computation | async-start | bytes 4194304 | tf_op jit(solution)/shard_map/all_to_all | solution.py:25
  28.7 77.3 %copy-start.10 = (s32[256]{0:T(256)S(1)}, s32[256]{0:T(256)}, u32[]{:S(2)}) copy-start(s32[256]{0:T(256)} %param.19) | copy-start | bytes 3076
  28.8 77.3 %copy-start.11 = (s32[256]{0:T(256)S(1)}, s32[256]{0:T(256)}, u32[]{:S(2)}) copy-start(s32[256]{0:T(256)} %param.20) | copy-start | bytes 3076
  103.1 107.9 %collective-permute-start.8 = (bf16[2048,512]{1,0:T(8,128)(2,1)}, bf16[2048,512]{1,0:T(8,128)(2,1)}, u32[]{:S(2)}, u32[]{:S(2)}) collective-permute-start(bf16[2048,512]{1,0:T(8,128)(2,1)} %slice.32), channel_id=1, source_target_pairs={{0,4},{4,0},{1,5},{5,1},{2,6},{6,2},{3,7},{7,3},{8,12},{12,8},{9,1... | collective-permute-start | bytes 6291464 | tf_op jit(solution)/shard_map/ppermute | solution.py:376
  138.4 1.4 copy-start
  144.0 17.7 %collective-permute-start = (bf16[528,128]{1,0:T(8,128)(2,1)}, bf16[528,128]{1,0:T(8,128)(2,1)S(1)}, u32[]{:S(2)}, u32[]{:S(2)}) collective-permute-start(bf16[528,128]{1,0:T(8,128)(2,1)} %get-tuple-element.8.refs_7_), channel_id=1, source_target_pairs={{0,56},{8,64},{16,72},{24,80},{32,88},{40,96},{48,104},{56,112},{6... | collective-permute-start | bytes 405512 | tf_op jit(solution)/shard_map/ppermute | solution.py:369
  151.0 14.6 %collective-permute-start.1 = (bf16[528,128]{1,0:T(8,128)(2,1)}, bf16[528,128]{1,0:T(8,128)(2,1)S(1)}, u32[]{:S(2)}, u32[]{:S(2)}) collective-permute-start(bf16[528,128]{1,0:T(8,128)(2,1)} %get-tuple-element.8.refs_7_), channel_id=1, source_target_pairs={{0,48},{8,56},{16,64},{24,72},{32,80},{40,88},{48,96},{56,104},{64... | collective-permute-start | bytes 405512 | tf_op jit(solution)/shard_map/ppermute | solution.py:369
  153.3 15.8 %collective-permute-start.2 = (bf16[528,128]{1,0:T(8,128)(2,1)}, bf16[528,128]{1,0:T(8,128)(2,1)S(1)}, u32[]{:S(2)}, u32[]{:S(2)}) collective-permute-start(bf16[528,128]{1,0:T(8,128)(2,1)} %get-tuple-element.8.refs_7_), channel_id=1, source_target_pairs={{0,40},{8,48},{16,56},{24,64},{32,72},{40,80},{48,88},{56,96},{64,... | collective-permute-start | bytes 405512 | tf_op jit(solution)/shard_map/ppermute | solution.py:369
  156.8 14.3 %collective-permute-start.3 = (bf16[528,128]{1,0:T(8,128)(2,1)}, bf16[528,128]{1,0:T(8,128)(2,1)S(1)}, u32[]{:S(2)}, u32[]{:S(2)}) collective-permute-start(bf16[528,128]{1,0:T(8,128)(2,1)} %get-tuple-element.8.refs_7_), channel_id=1, source_target_pairs={{0,32},{8,40},{16,48},{24,56},{32,64},{40,72},{48,80},{56,88},{64,... | collective-permute-start | bytes 405512 | tf_op jit(solution)/shard_map/ppermute | solution.py:369
  161.8 16.6 %copy-start.3 = (bf16[528,128]{1,0:T(8,128)(2,1)}, bf16[528,128]{1,0:T(8,128)(2,1)S(1)}, u32[]{:S(2)}) copy-start(bf16[528,128]{1,0:T(8,128)(2,1)S(1)} %collective-permute-done.refs_0_) | copy-start | bytes 405508
  161.8 9.3 %collective-permute-start.4 = (bf16[528,128]{1,0:T(8,128)(2,1)}, bf16[528,128]{1,0:T(8,128)(2,1)S(1)}, u32[]{:S(2)}, u32[]{:S(2)}) collective-permute-start(bf16[528,128]{1,0:T(8,128)(2,1)} %get-tuple-element.8.refs_7_), channel_id=1, source_target_pairs={{0,24},{8,32},{16,40},{24,48},{32,56},{40,64},{48,72},{56,80},{64,... | collective-permute-start | bytes 405512 | tf_op jit(solution)/shard_map/ppermute | solution.py:369
  165.6 12.7 %copy-start.4 = (bf16[528,128]{1,0:T(8,128)(2,1)}, bf16[528,128]{1,0:T(8,128)(2,1)S(1)}, u32[]{:S(2)}) copy-start(bf16[528,128]{1,0:T(8,128)(2,1)S(1)} %collective-permute-done.1.refs_1_) | copy-start | bytes 405508
  165.7 9.6 %collective-permute-start.5 = (bf16[528,128]{1,0:T(8,128)(2,1)}, bf16[528,128]{1,0:T(8,128)(2,1)S(1)}, u32[]{:S(2)}, u32[]{:S(2)}) collective-permute-start(bf16[528,128]{1,0:T(8,128)(2,1)} %get-tuple-element.8.refs_7_), channel_id=1, source_target_pairs={{0,16},{8,24},{16,32},{24,40},{32,48},{40,56},{48,64},{56,72},{64,... | collective-permute-start | bytes 405512 | tf_op jit(solution)/shard_map/ppermute | solution.py:369
  169.1 9.2 %copy-start.5 = (bf16[528,128]{1,0:T(8,128)(2,1)}, bf16[528,128]{1,0:T(8,128)(2,1)S(1)}, u32[]{:S(2)}) copy-start(bf16[528,128]{1,0:T(8,128)(2,1)S(1)} %collective-permute-done.2.refs_2_) | copy-start | bytes 405508
  169.1 9.2 %collective-permute-start.6 = (bf16[528,128]{1,0:T(8,128)(2,1)}, bf16[528,128]{1,0:T(8,128)(2,1)S(1)}, u32[]{:S(2)}, u32[]{:S(2)}) collective-permute-start(bf16[528,128]{1,0:T(8,128)(2,1)} %get-tuple-element.8.refs_7_), channel_id=1, source_target_pairs={{0,8},{8,16},{16,24},{24,32},{32,40},{40,48},{48,56},{56,64},{64,7... | collective-permute-start | bytes 405512 | tf_op jit(solution)/shard_map/ppermute | solution.py:369
  171.0 7.3 %copy-start.6 = (bf16[528,128]{1,0:T(8,128)(2,1)}, bf16[528,128]{1,0:T(8,128)(2,1)S(1)}, u32[]{:S(2)}) copy-start(bf16[528,128]{1,0:T(8,128)(2,1)S(1)} %collective-permute-done.3.refs_3_) | copy-start | bytes 405508
  171.1 7.3 %copy-start.7 = (bf16[528,128]{1,0:T(8,128)(2,1)}, bf16[528,128]{1,0:T(8,128)(2,1)S(1)}, u32[]{:S(2)}) copy-start(bf16[528,128]{1,0:T(8,128)(2,1)S(1)} %collective-permute-done.4.refs_4_) | copy-start | bytes 405508
  175.3 3.1 %copy-start.8 = (bf16[528,128]{1,0:T(8,128)(2,1)}, bf16[528,128]{1,0:T(8,128)(2,1)S(1)}, u32[]{:S(2)}) copy-start(bf16[528,128]{1,0:T(8,128)(2,1)S(1)} %collective-permute-done.5.refs_5_) | copy-start | bytes 405508
  178.4 0.7 copy-start.9
  181.4 6.7 %collective-permute-start.7 = (bf16[4224,128]{1,0:T(8,128)(2,1)}, bf16[4224,128]{1,0:T(8,128)(2,1)S(1)}, u32[]{:S(2)}, u32[]{:S(2)}) collective-permute-start(bf16[4224,128]{1,0:T(8,128)(2,1)} %lay_window.1.own_ref), channel_id=1, source_target_pairs={{0,4},{4,0},{1,5},{5,1},{2,6},{6,2},{3,7},{7,3},{8,12},{12,8},{9,1... | collective-permute-start | bytes 3244040 | tf_op jit(solution)/shard_map/ppermute | solution.py:373
  188.1 1.0 copy-start.1
Sparse Core Ops, SparseCore 0:
  21.8 78.0 all-gather.1

commit v3 on v2

--- a/solution.py
+++ b/solution.py
@@ -28,6 +28,8 @@
 
 
 def normed_and_turned(values, gain, cosine, sine):
+    cosine = jnp.concatenate([cosine, cosine], axis=1)
+    sine = jnp.concatenate([-sine, sine], axis=1)
     mean_square = jnp.mean(values * values, axis=-1, keepdims=True)
     scaled = values * lax.rsqrt(mean_square + EPSILON) * gain
     return scaled * cosine + pltpu.roll(scaled, HEAD // 2, 1) * sine
@@ -61,8 +63,8 @@
             pl.BlockSpec((1, 4, 256, 512), lambda k: (k, 0, 0, 0)),
             pl.BlockSpec((2048, 512), lambda k: (0, 0)),
             pl.BlockSpec((1, HEAD), lambda k: (0, 0)),
-            pl.BlockSpec((256, HEAD), lambda k: (k, 0)),
-            pl.BlockSpec((256, HEAD), lambda k: (k, 0)),
+            pl.BlockSpec((256, HEAD // 2), lambda k: (k, 0)),
+            pl.BlockSpec((256, HEAD // 2), lambda k: (k, 0)),
         ],
         out_specs=pl.BlockSpec((2, 4, TILE, HEAD), lambda k: (k, 0, 0, 0)),
         out_shape=jax.ShapeDtypeStruct((4, 4, TILE, HEAD), jnp.bfloat16),
@@ -278,30 +280,32 @@
     )(core, queries, own, other)
 
 
-def output_kernel(core_ref, a_ref, own_ref, other_ref, out_ref):
-    core = core_ref[0]
-    dims = (((1,), (1,)), ((), ()))
-    total = lax.dot_general(a_ref[core], own_ref[...], dims, preferred_element_type=jnp.float32)
-    total += lax.dot_general(
-        a_ref[1 - core], other_ref[...], dims, preferred_element_type=jnp.float32
-    )
-    out_ref[0] = total.astype(jnp.bfloat16)
-
-
-def project_out(core, attended, gathered, other):
+def output_kernel(a_ref, w_ref, *refs):
+    total = lax.dot_general(
+        a_ref[...], w_ref[...], (((1,), (1,)), ((), ())), preferred_element_type=jnp.float32
+    )
+    if len(refs) == 2:
+        total += refs[0][0].astype(jnp.float32)
+    refs[-1][0] = total.astype(jnp.bfloat16)
+
+
+def project_out(half, attended, weights, *shares):
+    block = pl.BlockSpec((1, 256, 512), lambda j, half_ref: (j, 0, 0))
     return pl.pallas_call(
-        output_kernel,
-        grid=(4,),
-        in_specs=[
-            pl.BlockSpec(memory_space=pltpu.SMEM),
-            pl.BlockSpec((2, 256, 512), lambda j: (0, 0, 0)),
-            pl.BlockSpec((512, 512), lambda j: (j, 1)),
-            pl.BlockSpec((512, 512), lambda j: (j, 0)),
-        ],
-        out_specs=pl.BlockSpec((1, 256, 512), lambda j: (j, 0, 0)),
+        lambda half_ref, *refs: output_kernel(*refs),
+        grid_spec=pltpu.PrefetchScalarGridSpec(
+            num_scalar_prefetch=1,
+            grid=(4,),
+            in_specs=[
+                pl.BlockSpec((256, 512), lambda j, half_ref: (half_ref[0], 0)),
+                pl.BlockSpec((512, 512), lambda j, half_ref: (j, 0)),
+            ]
+            + [block] * len(shares),
+            out_specs=block,
+        ),
         out_shape=jax.ShapeDtypeStruct((4, 256, 512), jnp.bfloat16),
         name="project_out",
-    )(core, attended, gathered, other)
+    )(half, attended, weights, *shares)
 
 
 def layer(
@@ -335,7 +339,8 @@
     ]
     pieces = jnp.broadcast_to(jnp.stack(halves)[None], (4, 2, 16, 1152)).reshape(8, 16, 1152)
     plane = lax.all_to_all(pieces, ("y", "core"), 0, 0, tiled=True).reshape(128, 1152)
-    wide = lax.all_gather(plane[:, :1024], "z", axis=0, tiled=True)
+    wide_query = lax.all_gather(plane[:, :512], "z", axis=0, tiled=True)
+    wide_out = lax.all_gather(plane[:, 512:1024], "z", axis=0, tiled=True)
     narrow = lax.all_gather(plane[:, 1024:], "z", axis=0, tiled=True)
 
     whole = copies(tokens, ("core", "head")).reshape(2, 4, 256, 512)
@@ -344,8 +349,6 @@
     freqs = THETA ** (-2.0 * jnp.arange(HEAD // 2, dtype=jnp.float32) / HEAD)
     angles = positions[:, None] * freqs[None, :]
     cosine, sine = jnp.cos(angles), jnp.sin(angles)
-    cosine = jnp.concatenate([cosine, cosine], axis=1)
-    sine = jnp.concatenate([-sine, sine], axis=1)
 
     tags = jnp.where(sentinel == 1, -(doc_ids + 1), doc_ids + 1).astype(jnp.bfloat16)
     extra = jnp.concatenate(
@@ -365,18 +368,18 @@
         sine,
         extra,
     )
-    earlier = [
-        lax.ppermute(own, CHIP, [(source, source + back) for source in range(64 - back)])
-        for back in range(BACK, 0, -1)
-    ]
+    earlier = []
+    for back in range(BACK, 0, -1):
+        steps = [(source, source + back) for source in range(64 - back)]
+        earlier.append(lax.ppermute(own, CHIP, steps))
     window = lay_window([*earlier, own])
     window_other = lax.ppermute(window, "core", [(0, 1), (1, 0)])
 
-    queries = project_queries(normed, wide, query_gain.reshape(1, HEAD), cosine, sine)
-    other = lax.ppermute(wide[:, 512:], "core", [(0, 1), (1, 0)])
+    queries = project_queries(normed, wide_query, query_gain.reshape(1, HEAD), cosine, sine)
     attended = attend(core_arg, queries, window, window_other)
-    attended = lax.all_to_all(attended.reshape(2, 256, 512), "core", 0, 0, tiled=True)
-    partials = project_out(core_arg, attended, wide, other)
+    away = project_out(1 - core_arg, attended, wide_out)
+    away = lax.ppermute(away, "core", [(0, 1), (1, 0)])
+    partials = project_out(core_arg, attended, wide_out, away)
     shares = lax.all_to_all(partials, "head", 0, 0, tiled=True)
     return jnp.sum(shares.astype(jnp.float32), axis=0).astype(jnp.bfloat16)
 

time: 245 us -> 219 us (0.89)
  the two profiles are of different devices: /device:TPU:96 before, /device:TPU:8 now
where the time goes in v3:
time: 219 us
  blocking collectives  74.8 us (34%)
  waiting for transfers between devices  58.9 us (27%)
  starting transfers between devices  32.5 us (15%)
  Pallas kernels  26.7 us (12%)
  between operations  13.7 us (6%)
  local copies, waits for them, and re-layouts  7.98 us (4%)
  other arithmetic  4.1 us (2%)
    all_gather x1, waiting for transfers between devices, layer(): wide_out = lax.all_gather(plane[:, 512:1024], 'z', axis=0, tiled=True)  50.4 us
    all_gather x1, blocking collectives, layer(): narrow = lax.all_gather(plane[:, 1024:], 'z', axis=0, tiled=True)  40.4 us
    ppermute x7, starting transfers between devices, layer(): earlier.append(lax.ppermute(own, CHIP, steps))  24.9 us
    all_to_all x1, blocking collectives, layer(): shares = lax.all_to_all(partials, 'head', 0, 0, tiled=True)  19.9 us
    all_to_all x1, blocking collectives, layer(): lax.all_to_all(pieces, ('y', 'core'), 0, 0, tiled=True).reshape(128, 1152)  14.6 us
    pallas_call x2, Pallas kernels, project_out(): pl.pallas_call(lambda half_ref, *refs: output_kernel(*refs), grid_spec=pl...  8.72 us
    pallas_call x1, Pallas kernels, attend(): pl.pallas_call(attention_kernel, grid=(4,), in_specs=[pl.BlockSpec(memory...  6.38 us
    ppermute x7, waiting for transfers between devices, layer(): earlier.append(lax.ppermute(own, CHIP, steps))  4.96 us
  transfers between devices with their start and end apart: 12, of which 4 were waited for; matrix products, arithmetic and copies ran while one was open for 2% of the time, Pallas kernels for 8%

profile of v3, /device:TPU:8, one launch (start us, length us, event | category | flops | bytes accessed | tf_op | source)
XLA Modules:
  0.0 218.7 jit_solution(11645897414663089792)
XLA Ops:
  6.5 0.8 fusion.8
  7.3 0.7 fusion.7
  8.1 0.7 maximum_bitcast_fusion
  8.8 14.6 %all_to_all.15 = bf16[8,16,1152]{2,1,0:T(8,128)(2,1)S(1)} all-to-all(bf16[8,16,1152]{2,1,0:T(8,128)(2,1)S(1)} %bitcast.19), channel_id=1, replica_groups=mesh['z'=16,'y'=4,'core'=2,'head'=4] {'y','core'}, dimensions={0} | all-to-all | bytes 589824 | tf_op jit(solution)/shard_map/all_to_all | solution.py:341
  23.4 0.7 fusion.6
  24.1 0.0 all-gather.3.cloned.1.call-update
  24.1 0.0 all-gather.5.cloned.1.call-start
  24.2 0.7 all-gather.5.cloned.1.call-update
  24.9 1.6 broadcast_in_dim.6
  26.5 3.7 %all-to-all-start = ((bf16[8,256,512]{2,1,0:T(8,128)(2,1)}), bf16[8,256,512]{2,1,0:T(8,128)(2,1)S(1)}, u32[]{:S(2)}, u32[]{:S(2)}) async-start(bf16[8,256,512]{2,1,0:T(8,128)(2,1)} %broadcast_in_dim.6), calls=%async_computation | async-start | bytes 4194304 | tf_op jit(solution)/shard_map/all_to_all | solution.py:25
  30.2 0.1 pad.7.clone
  30.4 0.7 fusion.3.extra_ref
  31.0 1.8 multiply_sine_fusion
  32.8 40.4 %all_gather.9.w_ref = bf16[2048,128]{1,0:T(8,128)(2,1)} all-gather(bf16[128,128]{1,0:T(8,128)(2,1)S(1)} %slice.30), channel_id=1, replica_groups=mesh['z'=16,'y'=4,'core'=2,'head'=4] {'z'}, dimensions={0}, use_global_device_ids=true | all-gather | bytes 557056 | tf_op jit(solution)/shard_map/all_gather | solution.py:344
  73.2 0.0 all-to-all-done
  73.2 1.4 copy-done
  74.6 4.4 %project_keys_or_values.1 = (bf16[528,128]{1,0:T(8,128)(2,1)}, bf16[2,4,256,512]{3,2,1,0:T(8,128)(2,1)}) custom-call(s32[1]{0:T(128)} %bitcast.core_ref.half_ref, bf16[2,4,256,512]{3,2,1,0:T(8,128)(2,1)} %bitcast.16, f32[4,1,512]{2,1,0:T(1,128)} %bitcast.21, bf16[2048,128]{1,0:T(8,128)(2,1)} %all_gather.9.w_ref, f32[1,128]{1,0:T(1,128)} %bitcast.22, ...), custom_call_target="tpu_custom_call" | custom-call | tf_op jit(solution)/shard_map/project_keys_or_values/pallas_call | solution.py:104
  78.9 2.9 %collective-permute-start = (bf16[528,128]{1,0:T(8,128)(2,1)}, bf16[528,128]{1,0:T(8,128)(2,1)S(1)}, u32[]{:S(2)}, u32[]{:S(2)}) collective-permute-start(bf16[528,128]{1,0:T(8,128)(2,1)} %get-tuple-element.8.refs_7_), channel_id=1, source_target_pairs={{0,56},{8,64},{16,72},{24,80},{32,88},{40,96},{48,104},{56,112},{6... | collective-permute-start | bytes 405512 | tf_op jit(solution)/shard_map/ppermute | solution.py:374
  81.8 2.9 %collective-permute-start.1 = (bf16[528,128]{1,0:T(8,128)(2,1)}, bf16[528,128]{1,0:T(8,128)(2,1)S(1)}, u32[]{:S(2)}, u32[]{:S(2)}) collective-permute-start(bf16[528,128]{1,0:T(8,128)(2,1)} %get-tuple-element.8.refs_7_), channel_id=1, source_target_pairs={{0,48},{8,56},{16,64},{24,72},{32,80},{40,88},{48,96},{56,104},{64... | collective-permute-start | bytes 405512 | tf_op jit(solution)/shard_map/ppermute | solution.py:374
  84.7 4.7 %collective-permute-start.2 = (bf16[528,128]{1,0:T(8,128)(2,1)}, bf16[528,128]{1,0:T(8,128)(2,1)S(1)}, u32[]{:S(2)}, u32[]{:S(2)}) collective-permute-start(bf16[528,128]{1,0:T(8,128)(2,1)} %get-tuple-element.8.refs_7_), channel_id=1, source_target_pairs={{0,40},{8,48},{16,56},{24,64},{32,72},{40,80},{48,88},{56,96},{64,... | collective-permute-start | bytes 405512 | tf_op jit(solution)/shard_map/ppermute | solution.py:374
  89.3 3.7 %collective-permute-start.3 = (bf16[528,128]{1,0:T(8,128)(2,1)}, bf16[528,128]{1,0:T(8,128)(2,1)S(1)}, u32[]{:S(2)}, u32[]{:S(2)}) collective-permute-start(bf16[528,128]{1,0:T(8,128)(2,1)} %get-tuple-element.8.refs_7_), channel_id=1, source_target_pairs={{0,32},{8,40},{16,48},{24,56},{32,64},{40,72},{48,80},{56,88},{64,... | collective-permute-start | bytes 405512 | tf_op jit(solution)/shard_map/ppermute | solution.py:374
  93.0 2.0 collective-permute-start.4
  95.0 0.0 collective-permute-done.refs_0_
  95.0 6.8 %collective-permute-start.5 = (bf16[528,128]{1,0:T(8,128)(2,1)}, bf16[528,128]{1,0:T(8,128)(2,1)S(1)}, u32[]{:S(2)}, u32[]{:S(2)}) collective-permute-start(bf16[528,128]{1,0:T(8,128)(2,1)} %get-tuple-element.8.refs_7_), channel_id=1, source_target_pairs={{0,16},{8,24},{16,32},{24,40},{32,48},{40,56},{48,64},{56,72},{64,... | collective-permute-start | bytes 405512 | tf_op jit(solution)/shard_map/ppermute | solution.py:374
  101.8 0.0 collective-permute-done.1.refs_1_
  101.9 2.1 collective-permute-start.6
  104.0 0.0 collective-permute-done.2.refs_2_
  104.0 0.0 copy-start.6
  104.0 0.0 collective-permute-done.3.refs_3_
  104.0 0.0 collective-permute-done.4.refs_4_
  104.0 0.7 collective-permute-done.5.refs_5_
  104.7 4.3 %collective-permute-done.6.refs_6_ = bf16[528,128]{1,0:T(8,128)(2,1)S(1)} collective-permute-done((bf16[528,128]{1,0:T(8,128)(2,1)}, bf16[528,128]{1,0:T(8,128)(2,1)S(1)}, u32[]{:S(2)}, u32[]{:S(2)}) %collective-permute-start.6) | collective-permute-done | bytes 135200 | tf_op jit(solution)/shard_map/ppermute | solution.py:374
  109.0 0.6 copy-done.10
  109.7 2.3 %lay_window.1.own_ref = bf16[4224,128]{1,0:T(8,128)(2,1)} custom-call(bf16[528,128]{1,0:T(8,128)(2,1)} %copy-done.4, bf16[528,128]{1,0:T(8,128)(2,1)} %copy-done.5, bf16[528,128]{1,0:T(8,128)(2,1)} %copy-done.6, bf16[528,128]{1,0:T(8,128)(2,1)} %copy-done.7, bf16[528,128]{1,0:T(8,128)(2,1)} %copy-done.8, bf16[528,128]{1,0:T(8,128)(2,1)} %copy-done.9, ...), custom_call_target="tpu_custom_call" | custom-call | tf_op jit(solution)/shard_map/lay_window/pallas_call | solution.py:125
  112.0 1.9 collective-permute-start.7
  113.9 0.0 all-gather.3.cloned.1.call-done.w_ref
  114.0 4.9 %project_queries.1.q_ref = bf16[4,4,128,128]{3,2,1,0:T(8,128)(2,1)} custom-call(bf16[2,4,256,512]{3,2,1,0:T(8,128)(2,1)} %get-tuple-element.7.x_ref, bf16[2048,512]{1,0:T(8,128)(2,1)} %all-gather.3.cloned.1.call-done.w_ref, f32[1,128]{1,0:T(1,128)} %bitcast.23, f32[512,64]{1,0:T(8,128)} %get-tuple-element.16.cos_ref, f32[512,64]{1,0:T(8,128)} %get-tuple-element.15.sin_ref), custom_call_target="tpu_custom_call" | custom-call | tf_op jit(solution)/shard_map/project_queries/pallas_call | solution.py:59
  118.8 0.0 collective-permute-done.7.other_ref
  118.8 1.0 copy-done.1
  119.8 6.4 %attend.1.refs_0_ = bf16[512,512]{1,0:T(8,128)(2,1)} custom-call(s32[1]{0:T(128)} %bitcast.core_ref.half_ref, bf16[4,4,128,128]{3,2,1,0:T(8,128)(2,1)} %project_queries.1.q_ref, bf16[4224,128]{1,0:T(8,128)(2,1)} %lay_window.1.own_ref, bf16[4224,128]{1,0:T(8,128)(2,1)} %copy-done.1), custom_call_target="tpu_custom_call" | custom-call | tf_op jit(solution)/shard_map/attend/pallas_call | solution.py:260
  126.2 50.4 %all-gather.5.cloned.1.call-done.refs_1_ = bf16[2048,512]{1,0:T(8,128)(2,1)} async-done(((bf16[128,512]{1,0:T(8,128)(2,1)}), bf16[2048,512]{1,0:T(8,128)(2,1)}) %all-gather.5.cloned.1.call-update) | async-done | bytes 2097168 | tf_op jit(solution)/shard_map/all_gather | solution.py:343
  176.6 4.3 %project_out.2 = bf16[4,256,512]{2,1,0:T(8,128)(2,1)} custom-call(s32[1]{0:T(128)S(6)} %sub.3.half_ref, bf16[512,512]{1,0:T(8,128)(2,1)} %attend.1.refs_0_, bf16[2048,512]{1,0:T(8,128)(2,1)} %all-gather.5.cloned.1.call-done.refs_1_), custom_call_target="tpu_custom_call" | custom-call | tf_op jit(solution)/shard_map/project_out/pallas_call | solution.py:294
  180.9 1.9 collective-permute-start.8
  182.8 2.8 %collective-permute-done.8.refs_2_ = bf16[4,256,512]{2,1,0:T(8,128)(2,1)S(1)} collective-permute-done((bf16[4,256,512]{2,1,0:T(8,128)(2,1)}, bf16[4,256,512]{2,1,0:T(8,128)(2,1)S(1)}, u32[]{:S(2)}, u32[]{:S(2)}) %collective-permute-start.8) | collective-permute-done | bytes 1048608 | tf_op jit(solution)/shard_map/ppermute | solution.py:381
  185.6 1.0 copy-done.2
  186.6 4.4 %project_out.3 = bf16[4,256,512]{2,1,0:T(8,128)(2,1)} custom-call(s32[1]{0:T(128)} %bitcast.core_ref.half_ref, bf16[512,512]{1,0:T(8,128)(2,1)} %attend.1.refs_0_, bf16[2048,512]{1,0:T(8,128)(2,1)} %all-gather.5.cloned.1.call-done.refs_1_, bf16[4,256,512]{2,1,0:T(8,128)(2,1)} %copy-done.2), custom_call_target="tpu_custom_call" | custom-call | tf_op jit(solution)/shard_map/project_out/pallas_call | solution.py:294
  191.0 19.9 %all_to_all.16 = bf16[4,256,512]{2,1,0:T(8,128)(2,1)S(1)} all-to-all(bf16[4,256,512]{2,1,0:T(8,128)(2,1)} %project_out.3), channel_id=1, replica_groups=mesh['z'=16,'y'=4,'core'=2,'head'=4] {'head'}, dimensions={0} | all-to-all | bytes 2097152 | tf_op jit(solution)/shard_map/all_to_all | solution.py:383
  210.9 0.9 reduce_sum.12
  (32 shorter events, 0.1 us)
Async XLA Ops:
  6.5 18.3 %copy-start.3 = (bf16[256,512]{1,0:T(8,128)(2,1)S(1)}, bf16[256,512]{1,0:T(8,128)(2,1)}, u32[]{:S(2)}) copy-start(bf16[256,512]{1,0:T(8,128)(2,1)} %param.11) | copy-start | bytes 786436
  6.5 107.4 %all-gather.3.cloned.1.call-start = ((), (), s32[]{:S(2)}) async-start(), calls=%async_computation.3 | async-start | bytes 2228224 | tf_op jit(solution)/shard_map/all_gather | solution.py:342
  24.1 152.4 %all-gather.5.cloned.1.call-start = ((), (), s32[]{:S(2)}) async-start(), calls=%async_computation.4 | async-start | bytes 2228224 | tf_op jit(solution)/shard_map/all_gather | solution.py:343
  26.4 3.9 %copy-start.13 = (s32[2]{0:T(128)S(1)}, s32[2]{0:T(128)}, u32[]{:S(2)}) copy-start(s32[2]{0:T(128)} %param.21) | copy-start | bytes 28
  26.4 3.9 %copy-start.11 = (s32[256]{0:T(256)S(1)}, s32[256]{0:T(256)}, u32[]{:S(2)}) copy-start(s32[256]{0:T(256)} %param.19) | copy-start | bytes 3076
  26.4 3.9 %copy-start.12 = (s32[256]{0:T(256)S(1)}, s32[256]{0:T(256)}, u32[]{:S(2)}) copy-start(s32[256]{0:T(256)} %param.20) | copy-start | bytes 3076
  26.5 46.7 %all-to-all-start = ((bf16[8,256,512]{2,1,0:T(8,128)(2,1)}), bf16[8,256,512]{2,1,0:T(8,128)(2,1)S(1)}, u32[]{:S(2)}, u32[]{:S(2)}) async-start(bf16[8,256,512]{2,1,0:T(8,128)(2,1)} %broadcast_in_dim.6), calls=%async_computation | async-start | bytes 4194304 | tf_op jit(solution)/shard_map/all_to_all | solution.py:25
  73.2 1.4 copy-start
  78.9 16.0 %collective-permute-start = (bf16[528,128]{1,0:T(8,128)(2,1)}, bf16[528,128]{1,0:T(8,128)(2,1)S(1)}, u32[]{:S(2)}, u32[]{:S(2)}) collective-permute-start(bf16[528,128]{1,0:T(8,128)(2,1)} %get-tuple-element.8.refs_7_), channel_id=1, source_target_pairs={{0,56},{8,64},{16,72},{24,80},{32,88},{40,96},{48,104},{56,112},{6... | collective-permute-start | bytes 405512 | tf_op jit(solution)/shard_map/ppermute | solution.py:374
  81.8 20.0 %collective-permute-start.1 = (bf16[528,128]{1,0:T(8,128)(2,1)}, bf16[528,128]{1,0:T(8,128)(2,1)S(1)}, u32[]{:S(2)}, u32[]{:S(2)}) collective-permute-start(bf16[528,128]{1,0:T(8,128)(2,1)} %get-tuple-element.8.refs_7_), channel_id=1, source_target_pairs={{0,48},{8,56},{16,64},{24,72},{32,80},{40,88},{48,96},{56,104},{64... | collective-permute-start | bytes 405512 | tf_op jit(solution)/shard_map/ppermute | solution.py:374
  84.7 19.3 %collective-permute-start.2 = (bf16[528,128]{1,0:T(8,128)(2,1)}, bf16[528,128]{1,0:T(8,128)(2,1)S(1)}, u32[]{:S(2)}, u32[]{:S(2)}) collective-permute-start(bf16[528,128]{1,0:T(8,128)(2,1)} %get-tuple-element.8.refs_7_), channel_id=1, source_target_pairs={{0,40},{8,48},{16,56},{24,64},{32,72},{40,80},{48,88},{56,96},{64,... | collective-permute-start | bytes 405512 | tf_op jit(solution)/shard_map/ppermute | solution.py:374
  89.3 14.6 %collective-permute-start.3 = (bf16[528,128]{1,0:T(8,128)(2,1)}, bf16[528,128]{1,0:T(8,128)(2,1)S(1)}, u32[]{:S(2)}, u32[]{:S(2)}) collective-permute-start(bf16[528,128]{1,0:T(8,128)(2,1)} %get-tuple-element.8.refs_7_), channel_id=1, source_target_pairs={{0,32},{8,40},{16,48},{24,56},{32,64},{40,72},{48,80},{56,88},{64,... | collective-permute-start | bytes 405512 | tf_op jit(solution)/shard_map/ppermute | solution.py:374
  93.0 11.0 %collective-permute-start.4 = (bf16[528,128]{1,0:T(8,128)(2,1)}, bf16[528,128]{1,0:T(8,128)(2,1)S(1)}, u32[]{:S(2)}, u32[]{:S(2)}) collective-permute-start(bf16[528,128]{1,0:T(8,128)(2,1)} %get-tuple-element.8.refs_7_), channel_id=1, source_target_pairs={{0,24},{8,32},{16,40},{24,48},{32,56},{40,64},{48,72},{56,80},{64,... | collective-permute-start | bytes 405512 | tf_op jit(solution)/shard_map/ppermute | solution.py:374
  95.0 14.0 %copy-start.4 = (bf16[528,128]{1,0:T(8,128)(2,1)}, bf16[528,128]{1,0:T(8,128)(2,1)S(1)}, u32[]{:S(2)}) copy-start(bf16[528,128]{1,0:T(8,128)(2,1)S(1)} %collective-permute-done.refs_0_) | copy-start | bytes 405508
  95.0 9.7 %collective-permute-start.5 = (bf16[528,128]{1,0:T(8,128)(2,1)}, bf16[528,128]{1,0:T(8,128)(2,1)S(1)}, u32[]{:S(2)}, u32[]{:S(2)}) collective-permute-start(bf16[528,128]{1,0:T(8,128)(2,1)} %get-tuple-element.8.refs_7_), channel_id=1, source_target_pairs={{0,16},{8,24},{16,32},{24,40},{32,48},{40,56},{48,64},{56,72},{64,... | collective-permute-start | bytes 405512 | tf_op jit(solution)/shard_map/ppermute | solution.py:374
  101.9 7.1 %copy-start.5 = (bf16[528,128]{1,0:T(8,128)(2,1)}, bf16[528,128]{1,0:T(8,128)(2,1)S(1)}, u32[]{:S(2)}) copy-start(bf16[528,128]{1,0:T(8,128)(2,1)S(1)} %collective-permute-done.1.refs_1_) | copy-start | bytes 405508
  101.9 7.1 %collective-permute-start.6 = (bf16[528,128]{1,0:T(8,128)(2,1)}, bf16[528,128]{1,0:T(8,128)(2,1)S(1)}, u32[]{:S(2)}, u32[]{:S(2)}) collective-permute-start(bf16[528,128]{1,0:T(8,128)(2,1)} %get-tuple-element.8.refs_7_), channel_id=1, source_target_pairs={{0,8},{8,16},{16,24},{24,32},{32,40},{40,48},{48,56},{56,64},{64,7... | collective-permute-start | bytes 405512 | tf_op jit(solution)/shard_map/ppermute | solution.py:374
  104.0 5.0 %copy-start.6 = (bf16[528,128]{1,0:T(8,128)(2,1)}, bf16[528,128]{1,0:T(8,128)(2,1)S(1)}, u32[]{:S(2)}) copy-start(bf16[528,128]{1,0:T(8,128)(2,1)S(1)} %collective-permute-done.2.refs_2_) | copy-start | bytes 405508
  104.0 5.0 %copy-start.7 = (bf16[528,128]{1,0:T(8,128)(2,1)}, bf16[528,128]{1,0:T(8,128)(2,1)S(1)}, u32[]{:S(2)}) copy-start(bf16[528,128]{1,0:T(8,128)(2,1)S(1)} %collective-permute-done.3.refs_3_) | copy-start | bytes 405508
  104.0 5.0 %copy-start.8 = (bf16[528,128]{1,0:T(8,128)(2,1)}, bf16[528,128]{1,0:T(8,128)(2,1)S(1)}, u32[]{:S(2)}) copy-start(bf16[528,128]{1,0:T(8,128)(2,1)S(1)} %collective-permute-done.4.refs_4_) | copy-start | bytes 405508
  104.7 4.3 %copy-start.9 = (bf16[528,128]{1,0:T(8,128)(2,1)}, bf16[528,128]{1,0:T(8,128)(2,1)S(1)}, u32[]{:S(2)}) copy-start(bf16[528,128]{1,0:T(8,128)(2,1)S(1)} %collective-permute-done.5.refs_5_) | copy-start | bytes 405508
  109.0 0.7 copy-start.10
  112.0 6.8 %collective-permute-start.7 = (bf16[4224,128]{1,0:T(8,128)(2,1)}, bf16[4224,128]{1,0:T(8,128)(2,1)S(1)}, u32[]{:S(2)}, u32[]{:S(2)}) collective-permute-start(bf16[4224,128]{1,0:T(8,128)(2,1)} %lay_window.1.own_ref), channel_id=1, source_target_pairs={{0,4},{4,0},{1,5},{5,1},{2,6},{6,2},{3,7},{7,3},{8,12},{12,8},{9,1... | collective-permute-start | bytes 3244040 | tf_op jit(solution)/shard_map/ppermute | solution.py:376
  118.8 1.0 copy-start.1
  180.9 4.8 %collective-permute-start.8 = (bf16[4,256,512]{2,1,0:T(8,128)(2,1)}, bf16[4,256,512]{2,1,0:T(8,128)(2,1)S(1)}, u32[]{:S(2)}, u32[]{:S(2)}) collective-permute-start(bf16[4,256,512]{2,1,0:T(8,128)(2,1)} %project_out.2), channel_id=1, source_target_pairs={{0,4},{4,0},{1,5},{5,1},{2,6},{6,2},{3,7},{7,3},{8,12},{12,8},{9,1... | collective-permute-start | bytes 3145736 | tf_op jit(solution)/shard_map/ppermute | solution.py:381
  185.6 1.0 copy-start.2
Sparse Core Ops, SparseCore 0:
  24.2 76.7 all-gather.2
  103.1 73.4 all-gather.4

commit v4 on v3

--- a/solution.py
+++ b/solution.py
@@ -75,36 +75,48 @@
 def key_value_kernel(
     core_ref, x_ref, norm_ref, w_ref, gain_ref, cos_ref, sin_ref, extra_ref, out_ref, normed_ref
 ):
-    is_key = core_ref[0] == 0
-    for half in range(2):
-        rows = pl.ds(half * 256, 256)
-        parts = [x_ref[half, part].astype(jnp.float32) for part in range(4)]
-        squares = functools.reduce(jnp.add, [part * part for part in parts])
-        mean_square = jnp.sum(squares, axis=1, keepdims=True) / 2048
-        level = lax.rsqrt(mean_square + EPSILON)
-        products = []
-        for part in range(4):
-            normed = (parts[part] * level * norm_ref[part]).astype(jnp.bfloat16)
-            normed_ref[half, part] = normed
-            products.append(
-                jnp.dot(
-                    normed,
-                    w_ref[part * 512 : (part + 1) * 512, :],
-                    preferred_element_type=jnp.float32,
-                )
+    rows = pl.ds(pl.multiple_of(pl.program_id(0) * 256, 256), 256)
+    parts = [x_ref[0, part].astype(jnp.float32) for part in range(4)]
+    squares = functools.reduce(jnp.add, [part * part for part in parts])
+    level = lax.rsqrt(jnp.sum(squares, axis=1, keepdims=True) / 2048 + EPSILON)
+    products = []
+    for part in range(4):
+        normed = (parts[part] * level * norm_ref[part]).astype(jnp.bfloat16)
+        normed_ref[0, part] = normed
+        products.append(
+            jnp.dot(
+                normed,
+                w_ref[part * 512 : (part + 1) * 512, :],
+                preferred_element_type=jnp.float32,
             )
-        total = functools.reduce(jnp.add, products)
-        turned = normed_and_turned(total, gain_ref[...], cos_ref[rows, :], sin_ref[rows, :])
-        out_ref[rows, :] = jnp.where(is_key, turned, total).astype(jnp.bfloat16)
-    out_ref[512:528, :] = extra_ref[...]
+        )
+    total = functools.reduce(jnp.add, products)
+    turned = normed_and_turned(total, gain_ref[...], cos_ref[...], sin_ref[...])
+    out_ref[rows, :] = jnp.where(core_ref[0] == 0, turned, total).astype(jnp.bfloat16)
+
+    @pl.when(pl.program_id(0) == 0)
+    def _():
+        out_ref[512:528, :] = extra_ref[...]
 
 
 def project_keys_or_values(core, x, norm_gain, weights, gain, cosine, sine, extra):
-    vmem = pl.BlockSpec(memory_space=pltpu.VMEM)
     return pl.pallas_call(
         key_value_kernel,
-        in_specs=[pl.BlockSpec(memory_space=pltpu.SMEM)] + [vmem] * 7,
-        out_specs=(vmem, vmem),
+        grid=(2,),
+        in_specs=[
+            pl.BlockSpec(memory_space=pltpu.SMEM),
+            pl.BlockSpec((1, 4, 256, 512), lambda k: (k, 0, 0, 0)),
+            pl.BlockSpec((4, 1, 512), lambda k: (0, 0, 0)),
+            pl.BlockSpec((2048, HEAD), lambda k: (0, 0)),
+            pl.BlockSpec((1, HEAD), lambda k: (0, 0)),
+            pl.BlockSpec((256, HEAD // 2), lambda k: (k, 0)),
+            pl.BlockSpec((256, HEAD // 2), lambda k: (k, 0)),
+            pl.BlockSpec((16, HEAD), lambda k: (0, 0)),
+        ],
+        out_specs=(
+            pl.BlockSpec((528, HEAD), lambda k: (0, 0)),
+            pl.BlockSpec((1, 4, 256, 512), lambda k: (k, 0, 0, 0)),
+        ),
         out_shape=(
             jax.ShapeDtypeStruct((528, HEAD), jnp.bfloat16),
             jax.ShapeDtypeStruct((2, 4, 256, 512), jnp.bfloat16),
@@ -113,26 +125,67 @@
     )(core, x, norm_gain, weights, gain, cosine, sine, extra)
 
 
-def window_kernel(*refs):
-    out_ref = refs[-1]
-    for place, ref in enumerate(refs[:-1]):
-        out_ref[512 * place : 512 * (place + 1), :] = ref[:512, :]
-        out_ref[WINDOW + 16 * place : WINDOW + 16 * (place + 1), :] = ref[512:, :]
-
-
-def lay_window(blocks):
+def parcel_kernel(y_ref, own_ref, next_ref, far_ref, out_ref):
+    for target in range(4):
+        ahead = y_ref[0] <= target
+
+        @pl.when(ahead)
+        def _(target=target):
+            out_ref[target, 0] = own_ref[...]
+            out_ref[target, 1] = next_ref[...]
+
+        @pl.when(jnp.logical_not(ahead))
+        def _(target=target):
+            out_ref[target, 0] = next_ref[...]
+            out_ref[target, 1] = far_ref[...]
+
+
+def parcels(y, own, next_plane, far_plane):
+    vmem = pl.BlockSpec(memory_space=pltpu.VMEM)
+    return pl.pallas_call(
+        parcel_kernel,
+        in_specs=[pl.BlockSpec(memory_space=pltpu.SMEM)] + [vmem] * 3,
+        out_specs=vmem,
+        out_shape=jax.ShapeDtypeStruct((4, 2, *own.shape), own.dtype),
+        name="parcels",
+    )(y, own, next_plane, far_plane)
+
+
+def window_kernel(y_ref, parts_ref, out_ref):
+    for back in range(BACK + 1):
+        place = BACK - back
+        source = lax.rem(y_ref[0] + 4 - back % 4, 4)
+        block = parts_ref[source, back // 4]
+        out_ref[512 * place : 512 * (place + 1), :] = block[:512]
+        out_ref[WINDOW + 16 * place : WINDOW + 16 * (place + 1), :] = block[512:]
+
+
+def lay_window(y, parts):
     vmem = pl.BlockSpec(memory_space=pltpu.VMEM)
     return pl.pallas_call(
         window_kernel,
-        in_specs=[vmem] * len(blocks),
+        in_specs=[pl.BlockSpec(memory_space=pltpu.SMEM), vmem],
         out_specs=vmem,
         out_shape=jax.ShapeDtypeStruct((WINDOW + 128, HEAD), jnp.bfloat16),
         name="lay_window",
-    )(*blocks)
+    )(y, parts)
 
 
 def attention_kernel(
-    core_ref, q_ref, own_ref, other_ref, out_ref, kv_ref, tags_ref, reach_ref, m_ref, l_ref, acc_ref
+    core_ref,
+    q_ref,
+    own_ref,
+    other_ref,
+    w_ref,
+    here_ref,
+    away_ref,
+    kv_ref,
+    tags_ref,
+    reach_ref,
+    m_ref,
+    l_ref,
+    acc_ref,
+    attended_ref,
 ):
     tile = pl.program_id(0)
     lanes = lax.broadcasted_iota(jnp.int32, (1, TILE), 1)
@@ -247,15 +300,31 @@
         return carry
 
     lax.fori_loop(1, block_count, one_block, 0)
+    tile_rows = pl.ds(pl.multiple_of(tile * TILE, TILE), TILE)
     for head in range(4):
         rows = slice(head * TILE, (head + 1) * TILE)
         total = jnp.sum(l_ref[rows, :], axis=1, keepdims=True)
-        out_ref[:, head * HEAD : (head + 1) * HEAD] = (acc_ref[rows, :] / total).astype(
-            jnp.bfloat16
-        )
-
-
-def attend(core, queries, own, other):
+        attended_ref[tile_rows, head * HEAD : (head + 1) * HEAD] = (
+            acc_ref[rows, :] / total
+        ).astype(jnp.bfloat16)
+
+    @pl.when(tile == 3)
+    def _():
+        here = pl.ds(pl.multiple_of(core_ref[0] * 256, 256), 256)
+        away = pl.ds(pl.multiple_of((1 - core_ref[0]) * 256, 256), 256)
+        both = jnp.concatenate([attended_ref[here, :], attended_ref[away, :]], axis=0)
+        for part in range(4):
+            sums = lax.dot_general(
+                both,
+                w_ref[part * 512 : (part + 1) * 512, :],
+                (((1,), (1,)), ((), ())),
+                preferred_element_type=jnp.float32,
+            )
+            here_ref[part] = sums[:256]
+            away_ref[part] = sums[256:].astype(jnp.bfloat16)
+
+
+def attend_and_project(core, queries, own, other, wide):
     rows = WINDOW + 128
     return pl.pallas_call(
         attention_kernel,
@@ -265,9 +334,16 @@
             pl.BlockSpec((1, 4, TILE, HEAD), lambda i: (i, 0, 0, 0)),
             pl.BlockSpec((rows, HEAD), lambda i: (0, 0)),
             pl.BlockSpec((rows, HEAD), lambda i: (0, 0)),
+            pl.BlockSpec((2048, 512), lambda i: (0, 1)),
         ],
-        out_specs=pl.BlockSpec((TILE, 4 * HEAD), lambda i: (i, 0)),
-        out_shape=jax.ShapeDtypeStruct((4 * TILE, 4 * HEAD), jnp.bfloat16),
+        out_specs=(
+            pl.BlockSpec((4, 256, 512), lambda i: (0, 0, 0)),
+            pl.BlockSpec((4, 256, 512), lambda i: (0, 0, 0)),
+        ),
+        out_shape=(
+            jax.ShapeDtypeStruct((4, 256, 512), jnp.float32),
+            jax.ShapeDtypeStruct((4, 256, 512), jnp.bfloat16),
+        ),
         scratch_shapes=[
             pltpu.VMEM((2, rows, HEAD), jnp.bfloat16),
             pltpu.VMEM((4 * (BACK + 1), TILE), jnp.float32),
@@ -275,37 +351,10 @@
             pltpu.VMEM((4 * TILE, HEAD), jnp.float32),
             pltpu.VMEM((4 * TILE, HEAD), jnp.float32),
             pltpu.VMEM((4 * TILE, HEAD), jnp.float32),
+            pltpu.VMEM((4 * TILE, 4 * HEAD), jnp.bfloat16),
         ],
-        name="attend",
-    )(core, queries, own, other)
-
-
-def output_kernel(a_ref, w_ref, *refs):
-    total = lax.dot_general(
-        a_ref[...], w_ref[...], (((1,), (1,)), ((), ())), preferred_element_type=jnp.float32
-    )
-    if len(refs) == 2:
-        total += refs[0][0].astype(jnp.float32)
-    refs[-1][0] = total.astype(jnp.bfloat16)
-
-
-def project_out(half, attended, weights, *shares):
-    block = pl.BlockSpec((1, 256, 512), lambda j, half_ref: (j, 0, 0))
-    return pl.pallas_call(
-        lambda half_ref, *refs: output_kernel(*refs),
-        grid_spec=pltpu.PrefetchScalarGridSpec(
-            num_scalar_prefetch=1,
-            grid=(4,),
-            in_specs=[
-                pl.BlockSpec((256, 512), lambda j, half_ref: (half_ref[0], 0)),
-                pl.BlockSpec((512, 512), lambda j, half_ref: (j, 0)),
-            ]
-            + [block] * len(shares),
-            out_specs=block,
-        ),
-        out_shape=jax.ShapeDtypeStruct((4, 256, 512), jnp.bfloat16),
-        name="project_out",
-    )(half, attended, weights, *shares)
+        name="attend_and_project",
+    )(core, queries, own, other, wide)
 
 
 def layer(
@@ -339,8 +388,7 @@
     ]
     pieces = jnp.broadcast_to(jnp.stack(halves)[None], (4, 2, 16, 1152)).reshape(8, 16, 1152)
     plane = lax.all_to_all(pieces, ("y", "core"), 0, 0, tiled=True).reshape(128, 1152)
-    wide_query = lax.all_gather(plane[:, :512], "z", axis=0, tiled=True)
-    wide_out = lax.all_gather(plane[:, 512:1024], "z", axis=0, tiled=True)
+    wide = lax.all_gather(plane[:, :1024], "z", axis=0, tiled=True)
     narrow = lax.all_gather(plane[:, 1024:], "z", axis=0, tiled=True)
 
     whole = copies(tokens, ("core", "head")).reshape(2, 4, 256, 512)
@@ -368,18 +416,19 @@
         sine,
         extra,
     )
-    earlier = []
-    for back in range(BACK, 0, -1):
-        steps = [(source, source + back) for source in range(64 - back)]
-        earlier.append(lax.ppermute(own, CHIP, steps))
-    window = lay_window([*earlier, own])
+    y_arg = lax.axis_index("y").astype(jnp.int32).reshape(1)
+    next_plane, far_plane = (
+        lax.ppermute(own, "z", [(source, source + step) for source in range(16 - step)])
+        for step in (1, 2)
+    )
+    parts = parcels(y_arg, own, next_plane, far_plane)
+    parts = lax.all_to_all(parts, "y", 0, 0, tiled=True)
+    window = lay_window(y_arg, parts)
     window_other = lax.ppermute(window, "core", [(0, 1), (1, 0)])
-
-    queries = project_queries(normed, wide_query, query_gain.reshape(1, HEAD), cosine, sine)
-    attended = attend(core_arg, queries, window, window_other)
-    away = project_out(1 - core_arg, attended, wide_out)
+    queries = project_queries(normed, wide, query_gain.reshape(1, HEAD), cosine, sine)
+    here, away = attend_and_project(core_arg, queries, window, window_other, wide)
     away = lax.ppermute(away, "core", [(0, 1), (1, 0)])
-    partials = project_out(core_arg, attended, wide_out, away)
+    partials = (here + away.astype(jnp.float32)).astype(jnp.bfloat16)
     shares = lax.all_to_all(partials, "head", 0, 0, tiled=True)
     return jnp.sum(shares.astype(jnp.float32), axis=0).astype(jnp.bfloat16)
 

time: 219 us -> 176 us (0.80)
  the two profiles are of different devices: /device:TPU:8 before, /device:TPU:96 now
where the time goes in v4:
time: 176 us
  blocking collectives  87.2 us (50%)
  Pallas kernels  32.3 us (18%)
  starting transfers between devices  15.8 us (9%)
  waiting for transfers between devices  13.8 us (8%)
  between operations  13.5 us (8%)
  local copies, waits for them, and re-layouts  6.98 us (4%)
  other arithmetic  6.04 us (3%)
    all_gather x1, blocking collectives, layer(): narrow = lax.all_gather(plane[:, 1024:], 'z', axis=0, tiled=True)  39.7 us
    all_to_all x1, blocking collectives, layer(): shares = lax.all_to_all(partials, 'head', 0, 0, tiled=True)  20 us
    pallas_call x1, Pallas kernels, attend_and_project(): pl.pallas_call(attention_kernel, grid=(4,), in_specs=[pl.BlockSpec(memory...  18.8 us
    all_to_all x1, blocking collectives, layer(): parts = lax.all_to_all(parts, 'y', 0, 0, tiled=True)  15.4 us
    all_to_all x1, blocking collectives, layer(): lax.all_to_all(pieces, ('y', 'core'), 0, 0, tiled=True).reshape(128, 1152)  12.1 us
    ppermute x2, waiting for transfers between devices, layer(): lax.ppermute(own, 'z', [(source, source + step) for source in range(16 -...  11.3 us
    ppermute x2, starting transfers between devices, layer(): lax.ppermute(own, 'z', [(source, source + step) for source in range(16 -...  7.05 us
    pallas_call x1, Pallas kernels, project_queries(): pl.pallas_call(query_kernel, grid=(2,), in_specs=[pl.BlockSpec((1, 4, 256...  4.83 us
  transfers between devices with their start and end apart: 6, of which 3 were waited for; matrix products, arithmetic and copies ran while one was open for 2% of the time, Pallas kernels for 8%

profile of v4, /device:TPU:96, one launch (start us, length us, event | category | flops | bytes accessed | tf_op | source)
XLA Modules:
  0.0 175.6 jit_solution(12039902508946972631)
XLA Ops:
  6.5 0.0 copy-start.2
  6.5 0.0 all-gather.2.cloned.1.call-start
  6.5 0.8 fusion.6
  7.3 0.7 fusion.7
  8.1 0.7 maximum_bitcast_fusion
  8.8 12.1 %all_to_all.20 = bf16[8,16,1152]{2,1,0:T(8,128)(2,1)S(1)} all-to-all(bf16[8,16,1152]{2,1,0:T(8,128)(2,1)S(1)} %bitcast.20), channel_id=1, replica_groups=mesh['z'=16,'y'=4,'core'=2,'head'=4] {'y','core'}, dimensions={0} | all-to-all | bytes 589824 | tf_op jit(solution)/shard_map/all_to_all | solution.py:390
  20.9 0.7 slice.27
  21.7 0.0 all-gather.2.cloned.1.call-update
  21.7 0.0 copy-done.2
  21.7 1.5 broadcast_in_dim.6
  23.2 0.0 copy-start.7
  23.2 0.0 copy-start.5
  23.3 0.0 copy-start.6
  23.3 4.4 %all-to-all-start = ((bf16[8,256,512]{2,1,0:T(8,128)(2,1)}), bf16[8,256,512]{2,1,0:T(8,128)(2,1)S(1)}, u32[]{:S(2)}, u32[]{:S(2)}) async-start(bf16[8,256,512]{2,1,0:T(8,128)(2,1)} %broadcast_in_dim.6), calls=%async_computation | async-start | bytes 4194304 | tf_op jit(solution)/shard_map/all_to_all | solution.py:25
  27.7 0.1 pad.7.clone
  27.8 0.0 copy-done.7
  27.8 0.0 copy-done.5
  27.8 0.0 copy-done.6
  27.8 0.7 fusion.3.extra_ref
  28.5 1.8 %multiply_sine_fusion = (f32[512,64]{1,0:T(8,128)}, f32[512,64]{1,0:T(8,128)}) fusion(f32[64]{0:T(128)S(1)} %multiply_power_fusion, f32[512]{0:T(512)S(1)} %add_convert_fusion.1), kind=kLoop, calls=%fused_computation.1 | loop fusion | flops 32768 | bytes 264448 | tf_op jit(solution)/shard_map/sin | solution.py:399
  30.3 39.7 %all_gather.6.w_ref = bf16[2048,128]{1,0:T(8,128)(2,1)} all-gather(bf16[128,128]{1,0:T(8,128)(2,1)S(1)} %slice.26), channel_id=1, replica_groups=mesh['z'=16,'y'=4,'core'=2,'head'=4] {'z'}, dimensions={0}, use_global_device_ids=true | all-gather | bytes 557056 | tf_op jit(solution)/shard_map/all_gather | solution.py:392
  70.0 0.0 all-to-all-done
  70.0 0.0 copy-start
  70.0 1.4 copy-done
  71.3 4.2 %project_keys_or_values.1 = (bf16[528,128]{1,0:T(8,128)(2,1)}, bf16[2,4,256,512]{3,2,1,0:T(8,128)(2,1)}) custom-call(s32[1]{0:T(128)} %bitcast.core_ref, bf16[2,4,256,512]{3,2,1,0:T(8,128)(2,1)} %bitcast.17, f32[4,1,512]{2,1,0:T(1,128)} %bitcast.22, bf16[2048,128]{1,0:T(8,128)(2,1)} %all_gather.6.w_ref, f32[1,128]{1,0:T(1,128)} %bitcast.23, ...), custom_call_target="tpu_custom_call" | custom-call | tf_op jit(solution)/shard_map/project_keys_or_values/pallas_call | solution.py:103
  75.6 4.4 %collective-permute-start.1 = (bf16[528,128]{1,0:T(8,128)(2,1)}, bf16[528,128]{1,0:T(8,128)(2,1)S(1)}, u32[]{:S(2)}, u32[]{:S(2)}) collective-permute-start(bf16[528,128]{1,0:T(8,128)(2,1)} %get-tuple-element.10.own_ref), channel_id=1, source_target_pairs={{0,64},{32,96},{64,128},{96,160},{128,192},{160,224},{192,256},{22... | collective-permute-start | bytes 405512 | tf_op jit(solution)/shard_map/ppermute | solution.py:421
  80.0 2.6 %collective-permute-start = (bf16[528,128]{1,0:T(8,128)(2,1)}, bf16[528,128]{1,0:T(8,128)(2,1)S(1)}, u32[]{:S(2)}, u32[]{:S(2)}) collective-permute-start(bf16[528,128]{1,0:T(8,128)(2,1)} %get-tuple-element.10.own_ref), channel_id=1, source_target_pairs={{0,32},{32,64},{64,96},{96,128},{128,160},{160,192},{192,224},{224... | collective-permute-start | bytes 405512 | tf_op jit(solution)/shard_map/ppermute | solution.py:421
  82.6 6.1 %collective-permute-done.1.far_ref = bf16[528,128]{1,0:T(8,128)(2,1)S(1)} collective-permute-done((bf16[528,128]{1,0:T(8,128)(2,1)}, bf16[528,128]{1,0:T(8,128)(2,1)S(1)}, u32[]{:S(2)}, u32[]{:S(2)}) %collective-permute-start.1) | collective-permute-done | bytes 135200 | tf_op jit(solution)/shard_map/ppermute | solution.py:421
  88.8 0.0 copy-start.3
  88.8 5.2 %collective-permute-done.next_ref = bf16[528,128]{1,0:T(8,128)(2,1)S(1)} collective-permute-done((bf16[528,128]{1,0:T(8,128)(2,1)}, bf16[528,128]{1,0:T(8,128)(2,1)S(1)}, u32[]{:S(2)}, u32[]{:S(2)}) %collective-permute-start) | collective-permute-done | bytes 135200 | tf_op jit(solution)/shard_map/ppermute | solution.py:421
  93.9 0.0 copy-start.4
  93.9 0.0 copy-done.3
  93.9 0.6 copy-done.4
  94.6 2.1 %parcels.1 = bf16[4,2,528,128]{3,2,1,0:T(8,128)(2,1)} custom-call(s32[1]{0:T(128)} %bitcast.12.y_ref, bf16[528,128]{1,0:T(8,128)(2,1)} %get-tuple-element.10.own_ref, bf16[528,128]{1,0:T(8,128)(2,1)} %copy-done.4, bf16[528,128]{1,0:T(8,128)(2,1)} %copy-done.3), custom_call_target="tpu_custom_call" | custom-call | tf_op jit(solution)/shard_map/parcels/pallas_call | solution.py:145
  96.7 15.4 %all_to_all.21.parts_ref = bf16[4,2,528,128]{3,2,1,0:T(8,128)(2,1)} all-to-all(bf16[4,2,528,128]{3,2,1,0:T(8,128)(2,1)} %parcels.1), channel_id=1, replica_groups=mesh['z'=16,'y'=4,'core'=2,'head'=4] {'y'}, dimensions={0} | all-to-all | bytes 2162688 | tf_op jit(solution)/shard_map/all_to_all | solution.py:425
  112.1 2.3 %lay_window.1.own_ref = bf16[4224,128]{1,0:T(8,128)(2,1)} custom-call(s32[1]{0:T(128)} %bitcast.12.y_ref, bf16[4,2,528,128]{3,2,1,0:T(8,128)(2,1)} %all_to_all.21.parts_ref), custom_call_target="tpu_custom_call" | custom-call | tf_op jit(solution)/shard_map/lay_window/pallas_call | solution.py:165
  114.4 1.9 %collective-permute-start.2 = (bf16[4224,128]{1,0:T(8,128)(2,1)}, bf16[4224,128]{1,0:T(8,128)(2,1)S(1)}, u32[]{:S(2)}, u32[]{:S(2)}) collective-permute-start(bf16[4224,128]{1,0:T(8,128)(2,1)} %lay_window.1.own_ref), channel_id=1, source_target_pairs={{0,4},{4,0},{1,5},{5,1},{2,6},{6,2},{3,7},{7,3},{8,12},{12,8},{9,1... | collective-permute-start | bytes 3244040 | tf_op jit(solution)/shard_map/ppermute | solution.py:427
  116.3 0.0 all-gather.2.cloned.1.call-done.w_ref
  116.3 4.8 %project_queries.1.q_ref = bf16[4,4,128,128]{3,2,1,0:T(8,128)(2,1)} custom-call(bf16[2,4,256,512]{3,2,1,0:T(8,128)(2,1)} %get-tuple-element.9.x_ref, bf16[2048,1024]{1,0:T(8,128)(2,1)} %all-gather.2.cloned.1.call-done.w_ref, f32[1,128]{1,0:T(1,128)} %bitcast.24, f32[512,64]{1,0:T(8,128)} %get-tuple-element.18.cos_ref, f32[512,64]{1,0:T(8,128)} %get-tuple-element.17.sin_ref), custom_call_target="tpu_custom_call" | custom-call | tf_op jit(solution)/shard_map/project_queries/pallas_call | solution.py:59
  121.1 0.0 collective-permute-done.2.other_ref
  121.1 0.0 copy-start.1
  121.1 1.1 copy-done.1
  122.2 18.8 %attend_and_project.1 = (f32[4,256,512]{2,1,0:T(8,128)}, bf16[4,256,512]{2,1,0:T(8,128)(2,1)}) custom-call(s32[1]{0:T(128)} %bitcast.core_ref, bf16[4,4,128,128]{3,2,1,0:T(8,128)(2,1)} %project_queries.1.q_ref, bf16[4224,128]{1,0:T(8,128)(2,1)} %lay_window.1.own_ref, bf16[4224,128]{1,0:T(8,128)(2,1)} %copy-done.1, ...), custom_call_target="tpu_custom_call" | custom-call | tf_op jit(solution)/shard_map/attend_and_project/pallas_call | solution.py:329
  141.0 2.4 %collective-permute-start.3 = (bf16[4,256,512]{2,1,0:T(8,128)(2,1)}, bf16[4,256,512]{2,1,0:T(8,128)(2,1)S(1)}, u32[]{:S(2)}, u32[]{:S(2)}) collective-permute-start(bf16[4,256,512]{2,1,0:T(8,128)(2,1)} %get-tuple-element.12), channel_id=1, source_target_pairs={{0,4},{4,0},{1,5},{5,1},{2,6},{6,2},{3,7},{7,3},{8,12},{12,8},{9,1... | collective-permute-start | bytes 3145736 | tf_op jit(solution)/shard_map/ppermute | solution.py:430
  143.4 2.5 %collective-permute-done.3 = bf16[4,256,512]{2,1,0:T(8,128)(2,1)S(1)} collective-permute-done((bf16[4,256,512]{2,1,0:T(8,128)(2,1)}, bf16[4,256,512]{2,1,0:T(8,128)(2,1)S(1)}, u32[]{:S(2)}, u32[]{:S(2)}) %collective-permute-start.3) | collective-permute-done | bytes 1048608 | tf_op jit(solution)/shard_map/ppermute | solution.py:430
  145.9 1.9 %add_convert_fusion = bf16[4,256,512]{2,1,0:T(8,128)(2,1)S(1)} fusion(f32[4,256,512]{2,1,0:T(8,128)} %get-tuple-element.11, bf16[4,256,512]{2,1,0:T(8,128)(2,1)S(1)} %collective-permute-done.3), kind=kLoop, calls=%fused_computation | loop fusion | flops 1572864 | bytes 4194304 | tf_op jit(solution)/shard_map/convert_element_type | solution.py:431
  147.8 20.0 %all_to_all.22 = bf16[4,256,512]{2,1,0:T(8,128)(2,1)S(1)} all-to-all(bf16[4,256,512]{2,1,0:T(8,128)(2,1)S(1)} %add_convert_fusion), channel_id=1, replica_groups=mesh['z'=16,'y'=4,'core'=2,'head'=4] {'head'}, dimensions={0} | all-to-all | bytes 2097152 | tf_op jit(solution)/shard_map/all_to_all | solution.py:432
  167.8 0.9 reduce_sum.12
  (8 shorter events, 0.1 us)
Async XLA Ops:
  6.5 15.2 %copy-start.2 = (bf16[256,512]{1,0:T(8,128)(2,1)S(1)}, bf16[256,512]{1,0:T(8,128)(2,1)}, u32[]{:S(2)}) copy-start(bf16[256,512]{1,0:T(8,128)(2,1)} %param.11) | copy-start | bytes 786436
  6.5 109.8 %all-gather.2.cloned.1.call-start = ((), (), s32[]{:S(2)}) async-start(), calls=%async_computation.4 | async-start | bytes 4456448 | tf_op jit(solution)/shard_map/all_gather | solution.py:391
  23.2 4.5 %copy-start.7 = (s32[2]{0:T(128)S(1)}, s32[2]{0:T(128)}, u32[]{:S(2)}) copy-start(s32[2]{0:T(128)} %param.21) | copy-start | bytes 28
  23.2 4.6 %copy-start.5 = (s32[256]{0:T(256)S(1)}, s32[256]{0:T(256)}, u32[]{:S(2)}) copy-start(s32[256]{0:T(256)} %param.19) | copy-start | bytes 3076
  23.3 4.6 %copy-start.6 = (s32[256]{0:T(256)S(1)}, s32[256]{0:T(256)}, u32[]{:S(2)}) copy-start(s32[256]{0:T(256)} %param.20) | copy-start | bytes 3076
  23.3 46.7 %all-to-all-start = ((bf16[8,256,512]{2,1,0:T(8,128)(2,1)}), bf16[8,256,512]{2,1,0:T(8,128)(2,1)S(1)}, u32[]{:S(2)}, u32[]{:S(2)}) async-start(bf16[8,256,512]{2,1,0:T(8,128)(2,1)} %broadcast_in_dim.6), calls=%async_computation | async-start | bytes 4194304 | tf_op jit(solution)/shard_map/all_to_all | solution.py:25
  70.0 1.4 copy-start
  75.6 13.2 %collective-permute-start.1 = (bf16[528,128]{1,0:T(8,128)(2,1)}, bf16[528,128]{1,0:T(8,128)(2,1)S(1)}, u32[]{:S(2)}, u32[]{:S(2)}) collective-permute-start(bf16[528,128]{1,0:T(8,128)(2,1)} %get-tuple-element.10.own_ref), channel_id=1, source_target_pairs={{0,64},{32,96},{64,128},{96,160},{128,192},{160,224},{192,256},{22... | collective-permute-start | bytes 405512 | tf_op jit(solution)/shard_map/ppermute | solution.py:421
  80.0 13.9 %collective-permute-start = (bf16[528,128]{1,0:T(8,128)(2,1)}, bf16[528,128]{1,0:T(8,128)(2,1)S(1)}, u32[]{:S(2)}, u32[]{:S(2)}) collective-permute-start(bf16[528,128]{1,0:T(8,128)(2,1)} %get-tuple-element.10.own_ref), channel_id=1, source_target_pairs={{0,32},{32,64},{64,96},{96,128},{128,160},{160,192},{192,224},{224... | collective-permute-start | bytes 405512 | tf_op jit(solution)/shard_map/ppermute | solution.py:421
  88.8 5.2 %copy-start.3 = (bf16[528,128]{1,0:T(8,128)(2,1)}, bf16[528,128]{1,0:T(8,128)(2,1)S(1)}, u32[]{:S(2)}) copy-start(bf16[528,128]{1,0:T(8,128)(2,1)S(1)} %collective-permute-done.1.far_ref) | copy-start | bytes 405508
  93.9 0.6 copy-start.4
  114.4 6.8 %collective-permute-start.2 = (bf16[4224,128]{1,0:T(8,128)(2,1)}, bf16[4224,128]{1,0:T(8,128)(2,1)S(1)}, u32[]{:S(2)}, u32[]{:S(2)}) collective-permute-start(bf16[4224,128]{1,0:T(8,128)(2,1)} %lay_window.1.own_ref), channel_id=1, source_target_pairs={{0,4},{4,0},{1,5},{5,1},{2,6},{6,2},{3,7},{7,3},{8,12},{12,8},{9,1... | collective-permute-start | bytes 3244040 | tf_op jit(solution)/shard_map/ppermute | solution.py:427
  121.1 1.1 copy-start.1
  141.0 4.9 %collective-permute-start.3 = (bf16[4,256,512]{2,1,0:T(8,128)(2,1)}, bf16[4,256,512]{2,1,0:T(8,128)(2,1)S(1)}, u32[]{:S(2)}, u32[]{:S(2)}) collective-permute-start(bf16[4,256,512]{2,1,0:T(8,128)(2,1)} %get-tuple-element.12), channel_id=1, source_target_pairs={{0,4},{4,0},{1,5},{5,1},{2,6},{6,2},{3,7},{7,3},{8,12},{12,8},{9,1... | collective-permute-start | bytes 3145736 | tf_op jit(solution)/shard_map/ppermute | solution.py:430
Sparse Core Ops, SparseCore 0:
  21.8 86.6 all-gather.1

commit v5 on v4

--- a/solution.py
+++ b/solution.py
@@ -18,6 +18,10 @@
 THETA = 10000000.0
 TOK = ("z", "y", "core")
 CHIP = ("z", "y")
+
+
+def grant(mebibytes):
+    return pltpu.CompilerParams(vmem_limit_bytes=mebibytes << 20)
 
 
 def copies(shard, axis):
@@ -68,6 +72,7 @@
         ],
         out_specs=pl.BlockSpec((2, 4, TILE, HEAD), lambda k: (k, 0, 0, 0)),
         out_shape=jax.ShapeDtypeStruct((4, 4, TILE, HEAD), jnp.bfloat16),
+        compiler_params=grant(16),
         name="project_queries",
     )(x, weights, gain, cosine, sine)
 
@@ -121,6 +126,7 @@
             jax.ShapeDtypeStruct((528, HEAD), jnp.bfloat16),
             jax.ShapeDtypeStruct((2, 4, 256, 512), jnp.bfloat16),
         ),
+        compiler_params=grant(12),
         name="project_keys_or_values",
     )(core, x, norm_gain, weights, gain, cosine, sine, extra)
 
@@ -147,6 +153,7 @@
         in_specs=[pl.BlockSpec(memory_space=pltpu.SMEM)] + [vmem] * 3,
         out_specs=vmem,
         out_shape=jax.ShapeDtypeStruct((4, 2, *own.shape), own.dtype),
+        compiler_params=grant(4),
         name="parcels",
     )(y, own, next_plane, far_plane)
 
@@ -167,6 +174,7 @@
         in_specs=[pl.BlockSpec(memory_space=pltpu.SMEM), vmem],
         out_specs=vmem,
         out_shape=jax.ShapeDtypeStruct((WINDOW + 128, HEAD), jnp.bfloat16),
+        compiler_params=grant(4),
         name="lay_window",
     )(y, parts)
 
@@ -353,6 +361,7 @@
             pltpu.VMEM((4 * TILE, HEAD), jnp.float32),
             pltpu.VMEM((4 * TILE, 4 * HEAD), jnp.bfloat16),
         ],
+        compiler_params=grant(26),
         name="attend_and_project",
     )(core, queries, own, other, wide)
 
@@ -425,7 +434,14 @@
     parts = lax.all_to_all(parts, "y", 0, 0, tiled=True)
     window = lay_window(y_arg, parts)
     window_other = lax.ppermute(window, "core", [(0, 1), (1, 0)])
-    queries = project_queries(normed, wide, query_gain.reshape(1, HEAD), cosine, sine)
+    queries = project_queries(
+        pltpu.with_memory_space_constraint(normed, pltpu.HBM),
+        pltpu.with_memory_space_constraint(wide, pltpu.HBM),
+        query_gain.reshape(1, HEAD),
+        cosine,
+        sine,
+    )
+    window_other = pltpu.with_memory_space_constraint(window_other, pltpu.VMEM)
     here, away = attend_and_project(core_arg, queries, window, window_other, wide)
     away = lax.ppermute(away, "core", [(0, 1), (1, 0)])
     partials = (here + away.astype(jnp.float32)).astype(jnp.bfloat16)

time: 176 us -> 160 us (0.909)
  Pallas kernels: 32.3 us -> 22 us
  waiting for transfers between devices: 13.8 us -> 19 us
  blocking collectives: 87.2 us -> 82.1 us
  local copies, waits for them, and re-layouts: 6.98 us -> 3.92 us
  other arithmetic: 6.04 us -> 3.05 us
    all_gather x1, waiting for transfers between devices: 0.02 us -> 4.99 us  [layer(): wide = lax.all_gather(plane[:, :1024], 'z', axis=0, tiled=True)]
    all_gather x1, blocking collectives: 39.7 us -> 36.4 us  [layer(): narrow = lax.all_gather(plane[:, 1024:], 'z', axis=0, tiled=True)]
    unnamed x16 -> x18, local copies, waits for them, and re-layouts: 3.08 us -> 0.04 us
    pallas_call x1, Pallas kernels: 18.8 us -> 15.9 us  [attend_and_project(): pl.pallas_call(attention_kernel, grid=(4,), in_specs=[pl.BlockSpec(memory...]
    pallas_call x1, Pallas kernels: 4.23 us -> 1.71 us  [project_keys_or_values(): pl.pallas_call(key_value_kernel, grid=(2,), in_specs=[pl.BlockSpec(memory...]
    pallas_call x1, Pallas kernels: 2.29 us -> 0.07 us  [lay_window(): pl.pallas_call(window_kernel, in_specs=[pl.BlockSpec(memory_space=pltpu.S...]
    pallas_call x1, Pallas kernels: 2.13 us -> 0.1 us  [parcels(): pl.pallas_call(parcel_kernel, in_specs=[pl.BlockSpec(memory_space=pltpu.S...]
  transfers between devices with their start and end apart: 6 -> 6, of which waited for: 3 -> 4; matrix products, arithmetic and copies ran while one was open for 2% -> 2% of each run, Pallas kernels for 8% -> 4%
where the time goes in v5:
time: 160 us
  blocking collectives  82.1 us (51%)
  Pallas kernels  22 us (14%)
  waiting for transfers between devices  19 us (12%)
  starting transfers between devices  15.9 us (10%)
  between operations  13.6 us (8%)
  local copies, waits for them, and re-layouts  3.92 us (2%)
  other arithmetic  3.05 us (2%)
    all_gather x1, blocking collectives, layer(): narrow = lax.all_gather(plane[:, 1024:], 'z', axis=0, tiled=True)  36.4 us
    all_to_all x1, blocking collectives, layer(): shares = lax.all_to_all(partials, 'head', 0, 0, tiled=True)  20 us
    pallas_call x1, Pallas kernels, attend_and_project(): pl.pallas_call(attention_kernel, grid=(4,), in_specs=[pl.BlockSpec(memory...  15.9 us
    all_to_all x1, blocking collectives, layer(): parts = lax.all_to_all(parts, 'y', 0, 0, tiled=True)  13.6 us
    all_to_all x1, blocking collectives, layer(): lax.all_to_all(pieces, ('y', 'core'), 0, 0, tiled=True).reshape(128, 1152)  12.1 us
    ppermute x2, waiting for transfers between devices, layer(): lax.ppermute(own, 'z', [(source, source + step) for source in range(16 -...  11.4 us
    ppermute x2, starting transfers between devices, layer(): lax.ppermute(own, 'z', [(source, source + step) for source in range(16 -...  7.59 us
    all_gather x1, waiting for transfers between devices, layer(): wide = lax.all_gather(plane[:, :1024], 'z', axis=0, tiled=True)  4.99 us
  transfers between devices with their start and end apart: 6, of which 4 were waited for; matrix products, arithmetic and copies ran while one was open for 2% of the time, Pallas kernels for 4%

profile of v5, /device:TPU:96, one launch (start us, length us, event | category | flops | bytes accessed | tf_op | source)
XLA Modules:
  0.0 159.6 jit_solution(14120706702117196466)
XLA Ops:
  6.5 0.0 copy-start.5
  6.5 0.0 all-gather.2.cloned.1.call-start
  6.5 0.8 fusion.6
  7.3 0.7 fusion.7
  8.1 0.7 maximum_bitcast_fusion
  8.8 12.1 %all_to_all.20 = bf16[8,16,1152]{2,1,0:T(8,128)(2,1)S(1)} all-to-all(bf16[8,16,1152]{2,1,0:T(8,128)(2,1)S(1)} %bitcast.23), channel_id=1, replica_groups=mesh['z'=16,'y'=4,'core'=2,'head'=4] {'y','core'}, dimensions={0} | all-to-all | bytes 589824 | tf_op jit(solution)/shard_map/all_to_all | solution.py:399
  20.9 0.7 slice.27
  21.7 0.0 all-gather.2.cloned.1.call-update
  21.7 0.0 copy-done.5
  21.7 1.5 broadcast_in_dim.6
  23.2 0.0 copy-start.8
  23.2 0.0 copy-start.6
  23.2 0.0 copy-start.7
  23.2 0.0 copy-start.3
  23.3 4.4 %all-to-all-start = ((bf16[8,256,512]{2,1,0:T(8,128)(2,1)}), bf16[8,256,512]{2,1,0:T(8,128)(2,1)S(1)}, u32[]{:S(2)}, u32[]{:S(2)}) async-start(bf16[8,256,512]{2,1,0:T(8,128)(2,1)} %broadcast_in_dim.6), calls=%async_computation | async-start | bytes 4194304 | tf_op jit(solution)/shard_map/all_to_all | solution.py:29
  27.7 0.1 pad.7.clone
  27.8 0.0 copy-done.8
  27.8 0.0 copy-done.6
  27.8 0.0 copy-done.7
  27.8 0.1 fusion.3.extra_ref
  27.9 1.0 multiply_sine_fusion
  28.9 36.4 %all_gather.6.w_ref = bf16[2048,128]{1,0:T(8,128)(2,1)S(1)} all-gather(bf16[128,128]{1,0:T(8,128)(2,1)S(1)} %slice.26), channel_id=1, replica_groups=mesh['z'=16,'y'=4,'core'=2,'head'=4] {'z'}, dimensions={0}, use_global_device_ids=true | all-gather | bytes 557056 | tf_op jit(solution)/shard_map/all_gather | solution.py:401
  65.3 0.0 all-to-all-done
  65.3 0.0 copy-done.2
  65.3 0.0 copy-done.3
  65.3 1.7 %project_keys_or_values.1 = (bf16[528,128]{1,0:T(8,128)(2,1)S(1)}, bf16[2,4,256,512]{3,2,1,0:T(8,128)(2,1)S(1)}) custom-call(s32[1]{0:T(128)} %bitcast.core_ref, bf16[2,4,256,512]{3,2,1,0:T(8,128)(2,1)S(1)} %bitcast.17, f32[4,1,512]{2,1,0:T(1,128)S(1)} %bitcast.18, bf16[2048,128]{1,0:T(8,128)(2,1)S(1)} %all_gather.6.w_ref, f32[1,128]{1,0:T(1,128)S(1)} %bitcast.19, ...), custom_call_target="tpu_custom_call" | custom-call | tf_op jit(solution)/shard_map/project_keys_or_values/pallas_call | solution.py:108
  67.1 0.0 copy-start.1
  67.1 4.3 %collective-permute-start.1 = (bf16[528,128]{1,0:T(8,128)(2,1)S(1)}, bf16[528,128]{1,0:T(8,128)(2,1)S(1)}, u32[]{:S(2)}, u32[]{:S(2)}) collective-permute-start(bf16[528,128]{1,0:T(8,128)(2,1)S(1)} %get-tuple-element.10.own_ref), channel_id=1, source_target_pairs={{0,64},{32,96},{64,128},{96,160},{128,192},{160,224},{192,256},{22... | collective-permute-start | bytes 405512 | tf_op jit(solution)/shard_map/ppermute | solution.py:430
  71.3 3.3 %collective-permute-start = (bf16[528,128]{1,0:T(8,128)(2,1)S(1)}, bf16[528,128]{1,0:T(8,128)(2,1)S(1)}, u32[]{:S(2)}, u32[]{:S(2)}) collective-permute-start(bf16[528,128]{1,0:T(8,128)(2,1)S(1)} %get-tuple-element.10.own_ref), channel_id=1, source_target_pairs={{0,32},{32,64},{64,96},{96,128},{128,160},{160,192},{192,224},{224... | collective-permute-start | bytes 405512 | tf_op jit(solution)/shard_map/ppermute | solution.py:430
  74.7 5.9 %collective-permute-done.1.far_ref = bf16[528,128]{1,0:T(8,128)(2,1)S(1)} collective-permute-done((bf16[528,128]{1,0:T(8,128)(2,1)S(1)}, bf16[528,128]{1,0:T(8,128)(2,1)S(1)}, u32[]{:S(2)}, u32[]{:S(2)}) %collective-permute-start.1) | collective-permute-done | bytes 135200 | tf_op jit(solution)/shard_map/ppermute | solution.py:430
  80.6 5.5 %collective-permute-done.next_ref = bf16[528,128]{1,0:T(8,128)(2,1)S(1)} collective-permute-done((bf16[528,128]{1,0:T(8,128)(2,1)S(1)}, bf16[528,128]{1,0:T(8,128)(2,1)S(1)}, u32[]{:S(2)}, u32[]{:S(2)}) %collective-permute-start) | collective-permute-done | bytes 135200 | tf_op jit(solution)/shard_map/ppermute | solution.py:430
  86.1 0.1 parcels.1
  86.2 0.0 copy-start.4
  86.2 13.6 %all_to_all.21.parts_ref = bf16[4,2,528,128]{3,2,1,0:T(8,128)(2,1)S(1)} all-to-all(bf16[4,2,528,128]{3,2,1,0:T(8,128)(2,1)S(1)} %parcels.1), channel_id=1, replica_groups=mesh['z'=16,'y'=4,'core'=2,'head'=4] {'y'}, dimensions={0} | all-to-all | bytes 2162688 | tf_op jit(solution)/shard_map/all_to_all | solution.py:434
  99.8 0.1 lay_window.1.own_ref
  99.9 0.0 copy-done.1
  99.9 1.9 %collective-permute-start.2 = (bf16[4224,128]{1,0:T(8,128)(2,1)S(1)}, bf16[4224,128]{1,0:T(8,128)(2,1)}, u32[]{:S(2)}, u32[]{:S(2)}) collective-permute-start(bf16[4224,128]{1,0:T(8,128)(2,1)S(1)} %lay_window.1.own_ref), channel_id=1, source_target_pairs={{0,4},{4,0},{1,5},{5,1},{2,6},{6,2},{3,7},{7,3},{8,12},{12,8},{9,1... | collective-permute-start | bytes 3244040 | tf_op jit(solution)/shard_map/ppermute | solution.py:436
  101.9 5.0 %all-gather.2.cloned.1.call-done.w_ref = bf16[2048,1024]{1,0:T(8,128)(2,1)} async-done(((bf16[128,1024]{1,0:T(8,128)(2,1)}), bf16[2048,1024]{1,0:T(8,128)(2,1)}) %all-gather.2.cloned.1.call-update) | async-done | bytes 4194320 | tf_op jit(solution)/shard_map/all_gather | solution.py:400
  106.8 0.0 copy-done.4
  106.8 4.1 %project_queries.1.q_ref = bf16[4,4,128,128]{3,2,1,0:T(8,128)(2,1)S(1)} custom-call(bf16[2,4,256,512]{3,2,1,0:T(8,128)(2,1)} %copy-done.1, bf16[2048,1024]{1,0:T(8,128)(2,1)} %all-gather.2.cloned.1.call-done.w_ref, f32[1,128]{1,0:T(1,128)S(1)} %bitcast.20, f32[512,64]{1,0:T(8,128)S(1)} %get-tuple-element.18.cos_ref, f32[512,64]{1,0:T(8,128)S(1)} %get-tuple-element.17.sin_ref), custom_call_target="tpu_custom_call" | custom-call | tf_op jit(solution)/shard_map/project_queries/pallas_call | solution.py:63
  111.0 0.0 collective-permute-done.2.other_ref
  111.0 0.0 copy-done
  111.0 15.9 %attend_and_project.1 = (f32[4,256,512]{2,1,0:T(8,128)S(1)}, bf16[4,256,512]{2,1,0:T(8,128)(2,1)S(1)}) custom-call(s32[1]{0:T(128)} %bitcast.core_ref, bf16[4,4,128,128]{3,2,1,0:T(8,128)(2,1)S(1)} %project_queries.1.q_ref, bf16[4224,128]{1,0:T(8,128)(2,1)S(1)} %lay_window.1.own_ref, bf16[4224,128]{1,0:T(8,128)(2,1)} %collective-permute-done.2.other_ref, ...), custom_call_target="tpu_custom_call" | custom-call | tf_op jit(solution)/shard_map/attend_and_project/pallas_call | solution.py:337
  127.0 1.9 %collective-permute-start.3 = (bf16[4,256,512]{2,1,0:T(8,128)(2,1)S(1)}, bf16[4,256,512]{2,1,0:T(8,128)(2,1)S(1)}, u32[]{:S(2)}, u32[]{:S(2)}) collective-permute-start(bf16[4,256,512]{2,1,0:T(8,128)(2,1)S(1)} %get-tuple-element.12), channel_id=1, source_target_pairs={{0,4},{4,0},{1,5},{5,1},{2,6},{6,2},{3,7},{7,3},{8,12},{12,8},{9,1... | collective-permute-start | bytes 3145736 | tf_op jit(solution)/shard_map/ppermute | solution.py:446
  128.9 2.6 %collective-permute-done.3 = bf16[4,256,512]{2,1,0:T(8,128)(2,1)S(1)} collective-permute-done((bf16[4,256,512]{2,1,0:T(8,128)(2,1)S(1)}, bf16[4,256,512]{2,1,0:T(8,128)(2,1)S(1)}, u32[]{:S(2)}, u32[]{:S(2)}) %collective-permute-start.3) | collective-permute-done | bytes 1048608 | tf_op jit(solution)/shard_map/ppermute | solution.py:446
  131.5 0.3 add_convert_fusion
  131.9 20.0 %all_to_all.22 = bf16[4,256,512]{2,1,0:T(8,128)(2,1)S(1)} all-to-all(bf16[4,256,512]{2,1,0:T(8,128)(2,1)S(1)} %add_convert_fusion), channel_id=1, replica_groups=mesh['z'=16,'y'=4,'core'=2,'head'=4] {'head'}, dimensions={0} | all-to-all | bytes 2097152 | tf_op jit(solution)/shard_map/all_to_all | solution.py:448
  151.8 0.9 reduce_sum.12
  (10 shorter events, 0.1 us)
Async XLA Ops:
  6.5 15.2 %copy-start.5 = (bf16[256,512]{1,0:T(8,128)(2,1)S(1)}, bf16[256,512]{1,0:T(8,128)(2,1)}, u32[]{:S(2)}) copy-start(bf16[256,512]{1,0:T(8,128)(2,1)} %param.11) | copy-start | bytes 786436
  6.5 100.3 %all-gather.2.cloned.1.call-start = ((), (), s32[]{:S(2)}) async-start(), calls=%async_computation.4 | async-start | bytes 4456448 | tf_op jit(solution)/shard_map/all_gather | solution.py:400
  23.2 4.6 %copy-start.8 = (s32[2]{0:T(128)S(1)}, s32[2]{0:T(128)}, u32[]{:S(2)}) copy-start(s32[2]{0:T(128)} %param.21) | copy-start | bytes 28
  23.2 4.6 %copy-start.6 = (s32[256]{0:T(256)S(1)}, s32[256]{0:T(256)}, u32[]{:S(2)}) copy-start(s32[256]{0:T(256)} %param.19) | copy-start | bytes 3076
  23.2 4.6 %copy-start.7 = (s32[256]{0:T(256)S(1)}, s32[256]{0:T(256)}, u32[]{:S(2)}) copy-start(s32[256]{0:T(256)} %param.20) | copy-start | bytes 3076
  23.2 42.1 %copy-start.2 = (f32[2048]{0:T(1024)S(1)}, f32[2048]{0:T(1024)}, u32[]{:S(2)}) copy-start(f32[2048]{0:T(1024)} %param.12) | copy-start | bytes 24580
  23.2 42.1 %copy-start.3 = (f32[128]{0:T(128)S(1)}, f32[128]{0:T(128)}, u32[]{:S(2)}) copy-start(f32[128]{0:T(128)} %param.17) | copy-start | bytes 1540
  23.3 42.1 %all-to-all-start = ((bf16[8,256,512]{2,1,0:T(8,128)(2,1)}), bf16[8,256,512]{2,1,0:T(8,128)(2,1)S(1)}, u32[]{:S(2)}, u32[]{:S(2)}) async-start(bf16[8,256,512]{2,1,0:T(8,128)(2,1)} %broadcast_in_dim.6), calls=%async_computation | async-start | bytes 4194304 | tf_op jit(solution)/shard_map/all_to_all | solution.py:29
  67.1 32.9 %copy-start.1 = (bf16[2,4,256,512]{3,2,1,0:T(8,128)(2,1)}, bf16[2,4,256,512]{3,2,1,0:T(8,128)(2,1)S(1)}, u32[]{:S(2)}) copy-start(bf16[2,4,256,512]{3,2,1,0:T(8,128)(2,1)S(1)} %get-tuple-element.9.x_ref) | copy-start | bytes 6291460
  67.1 13.5 %collective-permute-start.1 = (bf16[528,128]{1,0:T(8,128)(2,1)S(1)}, bf16[528,128]{1,0:T(8,128)(2,1)S(1)}, u32[]{:S(2)}, u32[]{:S(2)}) collective-permute-start(bf16[528,128]{1,0:T(8,128)(2,1)S(1)} %get-tuple-element.10.own_ref), channel_id=1, source_target_pairs={{0,64},{32,96},{64,128},{96,160},{128,192},{160,224},{192,256},{22... | collective-permute-start | bytes 405512 | tf_op jit(solution)/shard_map/ppermute | solution.py:430
  71.3 14.7 %collective-permute-start = (bf16[528,128]{1,0:T(8,128)(2,1)S(1)}, bf16[528,128]{1,0:T(8,128)(2,1)S(1)}, u32[]{:S(2)}, u32[]{:S(2)}) collective-permute-start(bf16[528,128]{1,0:T(8,128)(2,1)S(1)} %get-tuple-element.10.own_ref), channel_id=1, source_target_pairs={{0,32},{32,64},{64,96},{96,128},{128,160},{160,192},{192,224},{224... | collective-permute-start | bytes 405512 | tf_op jit(solution)/shard_map/ppermute | solution.py:430
  86.2 20.7 %copy-start.4 = (f32[128]{0:T(128)S(1)}, f32[128]{0:T(128)}, u32[]{:S(2)}) copy-start(f32[128]{0:T(128)} %param.16) | copy-start | bytes 1540
  99.9 11.1 %collective-permute-start.2 = (bf16[4224,128]{1,0:T(8,128)(2,1)S(1)}, bf16[4224,128]{1,0:T(8,128)(2,1)}, u32[]{:S(2)}, u32[]{:S(2)}) collective-permute-start(bf16[4224,128]{1,0:T(8,128)(2,1)S(1)} %lay_window.1.own_ref), channel_id=1, source_target_pairs={{0,4},{4,0},{1,5},{5,1},{2,6},{6,2},{3,7},{7,3},{8,12},{12,8},{9,1... | collective-permute-start | bytes 3244040 | tf_op jit(solution)/shard_map/ppermute | solution.py:436
  106.8 4.2 %copy-start = (bf16[2048,1024]{1,0:T(8,128)(2,1)S(1)}, bf16[2048,1024]{1,0:T(8,128)(2,1)}, u32[]{:S(2)}) copy-start(bf16[2048,1024]{1,0:T(8,128)(2,1)} %all-gather.2.cloned.1.call-done.w_ref) | copy-start | bytes 12582916
  127.0 4.6 %collective-permute-start.3 = (bf16[4,256,512]{2,1,0:T(8,128)(2,1)S(1)}, bf16[4,256,512]{2,1,0:T(8,128)(2,1)S(1)}, u32[]{:S(2)}, u32[]{:S(2)}) collective-permute-start(bf16[4,256,512]{2,1,0:T(8,128)(2,1)S(1)} %get-tuple-element.12), channel_id=1, source_target_pairs={{0,4},{4,0},{1,5},{5,1},{2,6},{6,2},{3,7},{7,3},{8,12},{12,8},{9,1... | collective-permute-start | bytes 3145736 | tf_op jit(solution)/shard_map/ppermute | solution.py:446
Sparse Core Ops, SparseCore 0:
  21.8 84.9 all-gather.1

commit v6 on v5

--- a/solution.py
+++ b/solution.py
@@ -24,11 +24,36 @@
     return pltpu.CompilerParams(vmem_limit_bytes=mebibytes << 20)
 
 
+def off_chip(array):
+    return pltpu.with_memory_space_constraint(array, pltpu.HBM)
+
+
 def copies(shard, axis):
     count = lax.axis_size(axis)
     return lax.all_to_all(
         jnp.broadcast_to(shard[None], (count, *shard.shape)), axis, 0, 0, tiled=True
     )
+
+
+def pieces_kernel(query_ref, out_ref_rows, key_ref, value_ref, pieces_ref):
+    for y in range(4):
+        for half in range(2):
+            columns = slice(512 * half, 512 * (half + 1))
+            pieces_ref[y, half, :, :512] = query_ref[:, columns]
+            pieces_ref[y, half, :, 512:1024] = out_ref_rows[:, columns]
+            pieces_ref[y, half, :, 1024:] = (key_ref, value_ref)[half][...]
+
+
+def lay_pieces(query_rows, out_rows, key_rows, value_rows):
+    vmem = pl.BlockSpec(memory_space=pltpu.VMEM)
+    return pl.pallas_call(
+        pieces_kernel,
+        in_specs=[vmem] * 4,
+        out_specs=vmem,
+        out_shape=pltpu.VMEM((4, 2, 16, 1152), jnp.bfloat16),
+        compiler_params=grant(4),
+        name="lay_pieces",
+    )(query_rows, out_rows, key_rows, value_rows)
 
 
 def normed_and_turned(values, gain, cosine, sine):
@@ -39,42 +64,14 @@
     return scaled * cosine + pltpu.roll(scaled, HEAD // 2, 1) * sine
 
 
-def query_kernel(x_ref, w_ref, gain_ref, cos_ref, sin_ref, out_ref):
-    total = functools.reduce(
-        jnp.add,
-        [
-            jnp.dot(
-                x_ref[0, part],
-                w_ref[part * 512 : (part + 1) * 512, :],
-                preferred_element_type=jnp.float32,
-            )
-            for part in range(4)
-        ],
-    )
+def query_part(total, q_ref, half, gain, cos_ref, sin_ref):
     for tile in range(2):
         rows = slice(tile * TILE, (tile + 1) * TILE)
+        place = slice((2 * half + tile) * TILE, (2 * half + tile + 1) * TILE)
         for head in range(4):
             one = total[rows, head * HEAD : (head + 1) * HEAD]
-            turned = normed_and_turned(one, gain_ref[...], cos_ref[rows, :], sin_ref[rows, :])
-            out_ref[tile, head] = turned.astype(jnp.bfloat16)
-
-
-def project_queries(x, weights, gain, cosine, sine):
-    return pl.pallas_call(
-        query_kernel,
-        grid=(2,),
-        in_specs=[
-            pl.BlockSpec((1, 4, 256, 512), lambda k: (k, 0, 0, 0)),
-            pl.BlockSpec((2048, 512), lambda k: (0, 0)),
-            pl.BlockSpec((1, HEAD), lambda k: (0, 0)),
-            pl.BlockSpec((256, HEAD // 2), lambda k: (k, 0)),
-            pl.BlockSpec((256, HEAD // 2), lambda k: (k, 0)),
-        ],
-        out_specs=pl.BlockSpec((2, 4, TILE, HEAD), lambda k: (k, 0, 0, 0)),
-        out_shape=jax.ShapeDtypeStruct((4, 4, TILE, HEAD), jnp.bfloat16),
-        compiler_params=grant(16),
-        name="project_queries",
-    )(x, weights, gain, cosine, sine)
+            turned = normed_and_turned(one, gain, cos_ref[place, :], sin_ref[place, :])
+            q_ref[2 * half + tile, head] = turned.astype(jnp.bfloat16)
 
 
 def key_value_kernel(
@@ -181,12 +178,23 @@
 
 def attention_kernel(
     core_ref,
-    q_ref,
+    tokens_ref,
+    gain_ref,
+    cos_ref,
+    sin_ref,
     own_ref,
     other_ref,
-    w_ref,
+    wide_ref,
     here_ref,
     away_ref,
+    x_ref,
+    wq_ref,
+    w_ref,
+    token_sems,
+    q_sems,
+    kv_sems,
+    out_sem,
+    q_ref,
     kv_ref,
     tags_ref,
     reach_ref,
@@ -198,10 +206,48 @@
     tile = pl.program_id(0)
     lanes = lax.broadcasted_iota(jnp.int32, (1, TILE), 1)
 
+    def query_copy(part):
+        rows = pl.ds(part * 512, 512)
+        return pltpu.make_async_copy(
+            wide_ref.at[rows, pl.ds(0, 512)], wq_ref.at[rows, :], q_sems.at[part]
+        )
+
+    def token_copy(half):
+        return pltpu.make_async_copy(tokens_ref.at[half], x_ref.at[half], token_sems.at[half])
+
+    def out_copy():
+        return pltpu.make_async_copy(wide_ref.at[:, pl.ds(512, 512)], w_ref, out_sem)
+
+    own_copy = pltpu.make_async_copy(own_ref, kv_ref.at[core_ref[0]], kv_sems.at[0])
+    other_copy = pltpu.make_async_copy(other_ref, kv_ref.at[1 - core_ref[0]], kv_sems.at[1])
+
     @pl.when(tile == 0)
     def _():
-        kv_ref[core_ref[0]] = own_ref[...]
-        kv_ref[1 - core_ref[0]] = other_ref[...]
+        token_copy(0).start()
+        for part in range(4):
+            query_copy(part).start()
+        token_copy(1).start()
+        own_copy.start()
+        other_copy.start()
+        out_copy().start()
+        for part in range(4):
+            query_copy(part).wait()
+        for half in range(2):
+            token_copy(half).wait()
+            total = functools.reduce(
+                jnp.add,
+                [
+                    jnp.dot(
+                        x_ref[half, part],
+                        wq_ref[part * 512 : (part + 1) * 512, :],
+                        preferred_element_type=jnp.float32,
+                    )
+                    for part in range(4)
+                ],
+            )
+            query_part(total, q_ref, half, gain_ref[...], cos_ref, sin_ref)
+        own_copy.wait()
+        other_copy.wait()
         for chip in range(BACK + 1):
             for core in range(2):
                 row = WINDOW + 16 * chip
@@ -225,7 +271,7 @@
     first_tile = jnp.maximum(lowest, before // TILE)
     block_count = (own_tile - first_tile) // 4 + 1
     factor = math.log2(math.e) / math.sqrt(HEAD)
-    query = q_ref[0].reshape(4 * TILE, HEAD)
+    query = q_ref[tile].reshape(4 * TILE, HEAD)
     wide_doc = jnp.broadcast_to(query_doc, (TILE, TILE))
 
     def scores_of(start_tile):
@@ -280,18 +326,20 @@
         start_tile = jnp.maximum(end_tile - 4, 0)
         scores = scores_of(start_tile)
         tags = tags_of(start_tile, end_tile)
-        visible = [wide_doc == tags[place] for place in range(4)]
+        bias = [jnp.where(wide_doc == tags[place], 0.0, -1e30) for place in range(4)]
         weights, shrinks = [], []
         for head in range(4):
             rows = slice(head * TILE, (head + 1) * TILE)
             pieces = [
-                jnp.where(visible[place], scores[rows, place * TILE : (place + 1) * TILE], -1e30)
+                scores[rows, place * TILE : (place + 1) * TILE] * factor + bias[place]
                 for place in range(4)
             ]
-            peak = jnp.max(functools.reduce(jnp.maximum, pieces), axis=1, keepdims=True) * factor
+            peak = jnp.max(functools.reduce(jnp.maximum, pieces), axis=1, keepdims=True)
             m_old = m_ref[rows, :]
             m_new = jnp.maximum(m_old, peak)
-            total, exps = lay_sums(pieces, m_new)
+            exps = [jnp.exp2(piece - m_new) for piece in pieces]
+            total = functools.reduce(jnp.add, exps)
+            exps = [piece.astype(jnp.bfloat16) for piece in exps]
             shrink = jnp.exp2(m_old - m_new)
             m_ref[rows, :] = m_new
             l_ref[rows, :] = l_ref[rows, :] * shrink + total
@@ -318,6 +366,7 @@
 
     @pl.when(tile == 3)
     def _():
+        out_copy().wait()
         here = pl.ds(pl.multiple_of(core_ref[0] * 256, 256), 256)
         away = pl.ds(pl.multiple_of((1 - core_ref[0]) * 256, 256), 256)
         both = jnp.concatenate([attended_ref[here, :], attended_ref[away, :]], axis=0)
@@ -332,17 +381,20 @@
             away_ref[part] = sums[256:].astype(jnp.bfloat16)
 
 
-def attend_and_project(core, queries, own, other, wide):
+def attend_and_project(core, x, gain, cosine, sine, own, other, wide):
     rows = WINDOW + 128
     return pl.pallas_call(
         attention_kernel,
         grid=(4,),
         in_specs=[
             pl.BlockSpec(memory_space=pltpu.SMEM),
-            pl.BlockSpec((1, 4, TILE, HEAD), lambda i: (i, 0, 0, 0)),
-            pl.BlockSpec((rows, HEAD), lambda i: (0, 0)),
-            pl.BlockSpec((rows, HEAD), lambda i: (0, 0)),
-            pl.BlockSpec((2048, 512), lambda i: (0, 1)),
+            pl.BlockSpec(memory_space=pltpu.HBM),
+            pl.BlockSpec((1, HEAD), lambda i: (0, 0)),
+            pl.BlockSpec((512, HEAD // 2), lambda i: (0, 0)),
+            pl.BlockSpec((512, HEAD // 2), lambda i: (0, 0)),
+            pl.BlockSpec(memory_space=pltpu.HBM),
+            pl.BlockSpec(memory_space=pltpu.HBM),
+            pl.BlockSpec(memory_space=pltpu.HBM),
         ],
         out_specs=(
             pl.BlockSpec((4, 256, 512), lambda i: (0, 0, 0)),
@@ -353,6 +405,14 @@
             jax.ShapeDtypeStruct((4, 256, 512), jnp.bfloat16),
         ),
         scratch_shapes=[
+            pltpu.VMEM((2, 4, 256, 512), jnp.bfloat16),
+            pltpu.VMEM((2048, 512), jnp.bfloat16),
+            pltpu.VMEM((2048, 512), jnp.bfloat16),
+            pltpu.SemaphoreType.DMA((2,)),
+            pltpu.SemaphoreType.DMA((4,)),
+            pltpu.SemaphoreType.DMA((2,)),
+            pltpu.SemaphoreType.DMA,
+            pltpu.VMEM((4, 4, TILE, HEAD), jnp.bfloat16),
             pltpu.VMEM((2, rows, HEAD), jnp.bfloat16),
             pltpu.VMEM((4 * (BACK + 1), TILE), jnp.float32),
             pltpu.VMEM((8, TILE), jnp.float32),
@@ -361,9 +421,9 @@
             pltpu.VMEM((4 * TILE, HEAD), jnp.float32),
             pltpu.VMEM((4 * TILE, 4 * HEAD), jnp.bfloat16),
         ],
-        compiler_params=grant(26),
+        compiler_params=grant(32),
         name="attend_and_project",
-    )(core, queries, own, other, wide)
+    )(core, x, gain, cosine, sine, own, other, wide)
 
 
 def layer(
@@ -383,19 +443,8 @@
     core_arg = core.astype(jnp.int32).reshape(1)
     chip = lax.axis_index(CHIP)
 
-    out_rows = w_out.T
-    halves = [
-        jnp.concatenate(
-            [
-                w_query[:, 512 * half : 512 * (half + 1)],
-                out_rows[:, 512 * half : 512 * (half + 1)],
-                (key_weight, value_weight)[half],
-            ],
-            axis=1,
-        )
-        for half in range(2)
-    ]
-    pieces = jnp.broadcast_to(jnp.stack(halves)[None], (4, 2, 16, 1152)).reshape(8, 16, 1152)
+    rows = [off_chip(rows) for rows in (w_query, w_out.T, key_weight, value_weight)]
+    pieces = lay_pieces(*rows).reshape(8, 16, 1152)
     plane = lax.all_to_all(pieces, ("y", "core"), 0, 0, tiled=True).reshape(128, 1152)
     wide = lax.all_gather(plane[:, :1024], "z", axis=0, tiled=True)
     narrow = lax.all_gather(plane[:, 1024:], "z", axis=0, tiled=True)
@@ -434,15 +483,16 @@
     parts = lax.all_to_all(parts, "y", 0, 0, tiled=True)
     window = lay_window(y_arg, parts)
     window_other = lax.ppermute(window, "core", [(0, 1), (1, 0)])
-    queries = project_queries(
-        pltpu.with_memory_space_constraint(normed, pltpu.HBM),
-        pltpu.with_memory_space_constraint(wide, pltpu.HBM),
+    here, away = attend_and_project(
+        core_arg,
+        off_chip(normed),
         query_gain.reshape(1, HEAD),
         cosine,
         sine,
-    )
-    window_other = pltpu.with_memory_space_constraint(window_other, pltpu.VMEM)
-    here, away = attend_and_project(core_arg, queries, window, window_other, wide)
+        off_chip(window),
+        off_chip(window_other),
+        off_chip(wide),
+    )
     away = lax.ppermute(away, "core", [(0, 1), (1, 0)])
     partials = (here + away.astype(jnp.float32)).astype(jnp.bfloat16)
     shares = lax.all_to_all(partials, "head", 0, 0, tiled=True)

time: 160 us -> 157 us (0.981)
  waiting for transfers between devices: 19 us -> 16.2 us
  blocking collectives: 82.1 us -> 84.3 us
    all_gather x1, waiting for transfers between devices: 4.99 us -> 0.39 us  [layer(): wide = lax.all_gather(plane[:, :1024], 'z', axis=0, tiled=True)]
    pallas_call x1, Pallas kernels: 4.15 us -> 0.8 us  [lay_pieces(): pl.pallas_call(pieces_kernel, in_specs=[vmem] * 4, out_specs=vmem, out_sh...]
    ppermute x1, waiting for transfers between devices: 0.01 us -> 2.8 us  [layer(): window_other = lax.ppermute(window, 'core', [(0, 1), (1, 0)])]
    pallas_call x1, Pallas kernels: 15.9 us -> 18.4 us  [attend_and_project(): pl.pallas_call(attention_kernel, grid=(4,), in_specs=[pl.BlockSpec(memory...]
    all_to_all x1, blocking collectives: 13.6 us -> 15.9 us  [layer(): parts = lax.all_to_all(parts, 'y', 0, 0, tiled=True)]
  transfers between devices with their start and end apart: 6 -> 6, of which waited for: 4 -> 5; matrix products, arithmetic and copies ran while one was open for 2% -> 2% of each run, Pallas kernels for 4% -> 1%
where the time goes in v6:
time: 157 us
  blocking collectives  84.3 us (54%)
  Pallas kernels  21 us (13%)
  starting transfers between devices  16.2 us (10%)
  waiting for transfers between devices  16.2 us (10%)
  between operations  13.6 us (9%)
  local copies, waits for them, and re-layouts  3.33 us (2%)
  other arithmetic  2.33 us (1%)
    all_gather x1, blocking collectives, layer(): narrow = lax.all_gather(plane[:, 1024:], 'z', axis=0, tiled=True)  36 us
    all_to_all x1, blocking collectives, layer(): shares = lax.all_to_all(partials, 'head', 0, 0, tiled=True)  20.3 us
    pallas_call x1, Pallas kernels, attend_and_project(): pl.pallas_call(attention_kernel, grid=(4,), in_specs=[pl.BlockSpec(memory...  18.4 us
    all_to_all x1, blocking collectives, layer(): parts = lax.all_to_all(parts, 'y', 0, 0, tiled=True)  15.9 us
    all_to_all x1, blocking collectives, layer(): lax.all_to_all(pieces, ('y', 'core'), 0, 0, tiled=True).reshape(128, 1152)  12.1 us
    ppermute x2, waiting for transfers between devices, layer(): lax.ppermute(own, 'z', [(source, source + step) for source in range(16 -...  10.4 us
    ppermute x2, starting transfers between devices, layer(): lax.ppermute(own, 'z', [(source, source + step) for source in range(16 -...  7.95 us
    all_to_all x1, starting transfers between devices, copies(): lax.all_to_all(jnp.broadcast_to(shard[None], (count, *shard.shape)), axis...  4.44 us
  transfers between devices with their start and end apart: 6, of which 5 were waited for; matrix products, arithmetic and copies ran while one was open for 2% of the time, Pallas kernels for 1%

profile of v6, /device:TPU:96, one launch (start us, length us, event | category | flops | bytes accessed | tf_op | source)
XLA Modules:
  0.0 157.0 jit_solution(9170277875443004316)
XLA Ops:
  6.5 0.0 all-gather.2.cloned.1.call-start
  6.5 0.8 lay_pieces.1
  7.3 12.1 %all_to_all.20 = bf16[8,16,1152]{2,1,0:T(8,128)(2,1)S(1)} all-to-all(bf16[8,16,1152]{2,1,0:T(8,128)(2,1)S(1)} %bitcast.14), channel_id=1, replica_groups=mesh['z'=16,'y'=4,'core'=2,'head'=4] {'y','core'}, dimensions={0} | all-to-all | bytes 589824 | tf_op jit(solution)/shard_map/all_to_all | solution.py:448
  19.5 0.7 slice.9
  20.2 0.0 all-gather.2.cloned.1.call-update
  20.2 2.5 %broadcast_in_dim.4 = bf16[8,256,512]{2,1,0:T(8,128)(2,1)} broadcast(bf16[256,512]{1,0:T(8,128)(2,1)} %param.11), dimensions={1,2} | broadcast | bytes 2359296 | tf_op jit(solution)/shard_map/broadcast_in_dim | solution.py:34
  22.7 0.0 copy-start.7
  22.7 0.0 copy-start.5
  22.7 0.0 copy-start.6
  22.7 0.0 copy-start.2
  22.7 0.0 copy-start.3
  22.7 4.4 %all-to-all-start = ((bf16[8,256,512]{2,1,0:T(8,128)(2,1)}), bf16[8,256,512]{2,1,0:T(8,128)(2,1)S(1)}, u32[]{:S(2)}, u32[]{:S(2)}) async-start(bf16[8,256,512]{2,1,0:T(8,128)(2,1)} %broadcast_in_dim.4), calls=%async_computation | async-start | bytes 4194304 | tf_op jit(solution)/shard_map/all_to_all | solution.py:33
  27.2 0.1 pad.7.clone
  27.3 0.0 copy-done.7
  27.3 0.0 copy-done.5
  27.3 0.0 copy-done.6
  27.3 0.1 fusion.3.extra_ref
  27.4 1.0 multiply_sine_fusion
  28.4 36.0 %all_gather.6.w_ref = bf16[2048,128]{1,0:T(8,128)(2,1)S(1)} all-gather(bf16[128,128]{1,0:T(8,128)(2,1)S(1)} %slice.8), channel_id=1, replica_groups=mesh['z'=16,'y'=4,'core'=2,'head'=4] {'z'}, dimensions={0}, use_global_device_ids=true | all-gather | bytes 557056 | tf_op jit(solution)/shard_map/all_gather | solution.py:450
  64.4 0.0 all-to-all-done
  64.4 0.0 copy-done.2
  64.4 0.0 copy-done.3
  64.4 1.7 %project_keys_or_values.1 = (bf16[528,128]{1,0:T(8,128)(2,1)S(1)}, bf16[2,4,256,512]{3,2,1,0:T(8,128)(2,1)S(1)}) custom-call(s32[1]{0:T(128)} %bitcast.core_ref, bf16[2,4,256,512]{3,2,1,0:T(8,128)(2,1)S(1)} %bitcast.13, f32[4,1,512]{2,1,0:T(1,128)S(1)} %bitcast.15, bf16[2048,128]{1,0:T(8,128)(2,1)S(1)} %all_gather.6.w_ref, f32[1,128]{1,0:T(1,128)S(1)} %bitcast.16, ...), custom_call_target="tpu_custom_call" | custom-call | tf_op jit(solution)/shard_map/project_keys_or_values/pallas_call | solution.py:105
  66.1 0.0 copy-start.1
  66.1 4.3 %collective-permute-start.1 = (bf16[528,128]{1,0:T(8,128)(2,1)S(1)}, bf16[528,128]{1,0:T(8,128)(2,1)S(1)}, u32[]{:S(2)}, u32[]{:S(2)}) collective-permute-start(bf16[528,128]{1,0:T(8,128)(2,1)S(1)} %get-tuple-element.10.own_ref), channel_id=1, source_target_pairs={{0,64},{32,96},{64,128},{96,160},{128,192},{160,224},{192,256},{22... | collective-permute-start | bytes 405512 | tf_op jit(solution)/shard_map/ppermute | solution.py:479
  70.4 3.7 %collective-permute-start = (bf16[528,128]{1,0:T(8,128)(2,1)S(1)}, bf16[528,128]{1,0:T(8,128)(2,1)S(1)}, u32[]{:S(2)}, u32[]{:S(2)}) collective-permute-start(bf16[528,128]{1,0:T(8,128)(2,1)S(1)} %get-tuple-element.10.own_ref), channel_id=1, source_target_pairs={{0,32},{32,64},{64,96},{96,128},{128,160},{160,192},{192,224},{224... | collective-permute-start | bytes 405512 | tf_op jit(solution)/shard_map/ppermute | solution.py:479
  74.1 5.5 %collective-permute-done.1.far_ref = bf16[528,128]{1,0:T(8,128)(2,1)S(1)} collective-permute-done((bf16[528,128]{1,0:T(8,128)(2,1)S(1)}, bf16[528,128]{1,0:T(8,128)(2,1)S(1)}, u32[]{:S(2)}, u32[]{:S(2)}) %collective-permute-start.1) | collective-permute-done | bytes 135200 | tf_op jit(solution)/shard_map/ppermute | solution.py:479
  79.6 4.8 %collective-permute-done.next_ref = bf16[528,128]{1,0:T(8,128)(2,1)S(1)} collective-permute-done((bf16[528,128]{1,0:T(8,128)(2,1)S(1)}, bf16[528,128]{1,0:T(8,128)(2,1)S(1)}, u32[]{:S(2)}, u32[]{:S(2)}) %collective-permute-start) | collective-permute-done | bytes 135200 | tf_op jit(solution)/shard_map/ppermute | solution.py:479
  84.4 0.1 parcels.1
  84.5 0.0 copy-start.4
  84.5 15.9 %all_to_all.21.parts_ref = bf16[4,2,528,128]{3,2,1,0:T(8,128)(2,1)S(1)} all-to-all(bf16[4,2,528,128]{3,2,1,0:T(8,128)(2,1)S(1)} %parcels.1), channel_id=1, replica_groups=mesh['z'=16,'y'=4,'core'=2,'head'=4] {'y'}, dimensions={0} | all-to-all | bytes 2162688 | tf_op jit(solution)/shard_map/all_to_all | solution.py:483
  100.4 0.1 lay_window.1.own_ref
  100.5 0.0 copy-done.1
  100.5 0.0 copy-start
  100.5 1.9 %collective-permute-start.2 = (bf16[4224,128]{1,0:T(8,128)(2,1)S(1)}, bf16[4224,128]{1,0:T(8,128)(2,1)}, u32[]{:S(2)}, u32[]{:S(2)}) collective-permute-start(bf16[4224,128]{1,0:T(8,128)(2,1)S(1)} %lay_window.1.own_ref), channel_id=1, source_target_pairs={{0,4},{4,0},{1,5},{5,1},{2,6},{6,2},{3,7},{7,3},{8,12},{12,8},{9,1... | collective-permute-start | bytes 3244040 | tf_op jit(solution)/shard_map/ppermute | solution.py:485
  102.5 2.8 %collective-permute-done.2.other_ref = bf16[4224,128]{1,0:T(8,128)(2,1)} collective-permute-done((bf16[4224,128]{1,0:T(8,128)(2,1)S(1)}, bf16[4224,128]{1,0:T(8,128)(2,1)}, u32[]{:S(2)}, u32[]{:S(2)}) %collective-permute-start.2) | collective-permute-done | bytes 1081376 | tf_op jit(solution)/shard_map/ppermute | solution.py:485
  105.3 0.4 all-gather.2.cloned.1.call-done.wide_ref
  105.6 0.0 copy-done
  105.7 0.0 copy-done.4
  105.7 18.4 %attend_and_project.1 = (f32[4,256,512]{2,1,0:T(8,128)S(1)}, bf16[4,256,512]{2,1,0:T(8,128)(2,1)S(1)}) custom-call(s32[1]{0:T(128)} %bitcast.core_ref, bf16[2,4,256,512]{3,2,1,0:T(8,128)(2,1)} %copy-done.1, f32[1,128]{1,0:T(1,128)S(1)} %bitcast.17, f32[512,64]{1,0:T(8,128)S(1)} %get-tuple-element.14.cos_ref, f32[512,64]{1,0:T(8,128)S(1)} %get-tuple-element.13.sin_ref, ...), custom_call_target="tpu_custom_call" | custom-call | tf_op jit(solution)/shard_map/attend_and_project/pallas_call | solution.py:386
  124.0 1.9 %collective-permute-start.3 = (bf16[4,256,512]{2,1,0:T(8,128)(2,1)S(1)}, bf16[4,256,512]{2,1,0:T(8,128)(2,1)S(1)}, u32[]{:S(2)}, u32[]{:S(2)}) collective-permute-start(bf16[4,256,512]{2,1,0:T(8,128)(2,1)S(1)} %get-tuple-element.12), channel_id=1, source_target_pairs={{0,4},{4,0},{1,5},{5,1},{2,6},{6,2},{3,7},{7,3},{8,12},{12,8},{9,1... | collective-permute-start | bytes 3145736 | tf_op jit(solution)/shard_map/ppermute | solution.py:496
  126.0 2.6 %collective-permute-done.3 = bf16[4,256,512]{2,1,0:T(8,128)(2,1)S(1)} collective-permute-done((bf16[4,256,512]{2,1,0:T(8,128)(2,1)S(1)}, bf16[4,256,512]{2,1,0:T(8,128)(2,1)S(1)}, u32[]{:S(2)}, u32[]{:S(2)}) %collective-permute-start.3) | collective-permute-done | bytes 1048608 | tf_op jit(solution)/shard_map/ppermute | solution.py:496
  128.6 0.3 add_convert_fusion
  128.9 20.3 %all_to_all.22 = bf16[4,256,512]{2,1,0:T(8,128)(2,1)S(1)} all-to-all(bf16[4,256,512]{2,1,0:T(8,128)(2,1)S(1)} %add_convert_fusion), channel_id=1, replica_groups=mesh['z'=16,'y'=4,'core'=2,'head'=4] {'head'}, dimensions={0} | all-to-all | bytes 2097152 | tf_op jit(solution)/shard_map/all_to_all | solution.py:498
  149.2 0.9 reduce_sum.12
  (6 shorter events, 0.0 us)
Async XLA Ops:
  6.5 99.1 %all-gather.2.cloned.1.call-start = ((), (), s32[]{:S(2)}) async-start(), calls=%async_computation.4 | async-start | bytes 4456448 | tf_op jit(solution)/shard_map/all_gather | solution.py:449
  22.7 4.6 %copy-start.7 = (s32[2]{0:T(128)S(1)}, s32[2]{0:T(128)}, u32[]{:S(2)}) copy-start(s32[2]{0:T(128)} %param.21) | copy-start | bytes 28
  22.7 4.6 %copy-start.5 = (s32[256]{0:T(256)S(1)}, s32[256]{0:T(256)}, u32[]{:S(2)}) copy-start(s32[256]{0:T(256)} %param.19) | copy-start | bytes 3076
  22.7 4.6 %copy-start.6 = (s32[256]{0:T(256)S(1)}, s32[256]{0:T(256)}, u32[]{:S(2)}) copy-start(s32[256]{0:T(256)} %param.20) | copy-start | bytes 3076
  22.7 41.7 %copy-start.2 = (f32[2048]{0:T(1024)S(1)}, f32[2048]{0:T(1024)}, u32[]{:S(2)}) copy-start(f32[2048]{0:T(1024)} %param.12) | copy-start | bytes 24580
  22.7 41.7 %copy-start.3 = (f32[128]{0:T(128)S(1)}, f32[128]{0:T(128)}, u32[]{:S(2)}) copy-start(f32[128]{0:T(128)} %param.17) | copy-start | bytes 1540
  22.7 41.6 %all-to-all-start = ((bf16[8,256,512]{2,1,0:T(8,128)(2,1)}), bf16[8,256,512]{2,1,0:T(8,128)(2,1)S(1)}, u32[]{:S(2)}, u32[]{:S(2)}) async-start(bf16[8,256,512]{2,1,0:T(8,128)(2,1)} %broadcast_in_dim.4), calls=%async_computation | async-start | bytes 4194304 | tf_op jit(solution)/shard_map/all_to_all | solution.py:33
  66.1 34.4 %copy-start.1 = (bf16[2,4,256,512]{3,2,1,0:T(8,128)(2,1)}, bf16[2,4,256,512]{3,2,1,0:T(8,128)(2,1)S(1)}, u32[]{:S(2)}) copy-start(bf16[2,4,256,512]{3,2,1,0:T(8,128)(2,1)S(1)} %get-tuple-element.9.tokens_ref) | copy-start | bytes 6291460
  66.1 13.5 %collective-permute-start.1 = (bf16[528,128]{1,0:T(8,128)(2,1)S(1)}, bf16[528,128]{1,0:T(8,128)(2,1)S(1)}, u32[]{:S(2)}, u32[]{:S(2)}) collective-permute-start(bf16[528,128]{1,0:T(8,128)(2,1)S(1)} %get-tuple-element.10.own_ref), channel_id=1, source_target_pairs={{0,64},{32,96},{64,128},{96,160},{128,192},{160,224},{192,256},{22... | collective-permute-start | bytes 405512 | tf_op jit(solution)/shard_map/ppermute | solution.py:479
  70.4 14.0 %collective-permute-start = (bf16[528,128]{1,0:T(8,128)(2,1)S(1)}, bf16[528,128]{1,0:T(8,128)(2,1)S(1)}, u32[]{:S(2)}, u32[]{:S(2)}) collective-permute-start(bf16[528,128]{1,0:T(8,128)(2,1)S(1)} %get-tuple-element.10.own_ref), channel_id=1, source_target_pairs={{0,32},{32,64},{64,96},{96,128},{128,160},{160,192},{192,224},{224... | collective-permute-start | bytes 405512 | tf_op jit(solution)/shard_map/ppermute | solution.py:479
  84.5 21.1 %copy-start.4 = (f32[128]{0:T(128)S(1)}, f32[128]{0:T(128)}, u32[]{:S(2)}) copy-start(f32[128]{0:T(128)} %param.16) | copy-start | bytes 1540
  100.5 5.1 %copy-start = (bf16[4224,128]{1,0:T(8,128)(2,1)}, bf16[4224,128]{1,0:T(8,128)(2,1)S(1)}, u32[]{:S(2)}) copy-start(bf16[4224,128]{1,0:T(8,128)(2,1)S(1)} %lay_window.1.own_ref) | copy-start | bytes 3244036
  100.5 4.7 %collective-permute-start.2 = (bf16[4224,128]{1,0:T(8,128)(2,1)S(1)}, bf16[4224,128]{1,0:T(8,128)(2,1)}, u32[]{:S(2)}, u32[]{:S(2)}) collective-permute-start(bf16[4224,128]{1,0:T(8,128)(2,1)S(1)} %lay_window.1.own_ref), channel_id=1, source_target_pairs={{0,4},{4,0},{1,5},{5,1},{2,6},{6,2},{3,7},{7,3},{8,12},{12,8},{9,1... | collective-permute-start | bytes 3244040 | tf_op jit(solution)/shard_map/ppermute | solution.py:485
  124.0 4.6 %collective-permute-start.3 = (bf16[4,256,512]{2,1,0:T(8,128)(2,1)S(1)}, bf16[4,256,512]{2,1,0:T(8,128)(2,1)S(1)}, u32[]{:S(2)}, u32[]{:S(2)}) collective-permute-start(bf16[4,256,512]{2,1,0:T(8,128)(2,1)S(1)} %get-tuple-element.12), channel_id=1, source_target_pairs={{0,4},{4,0},{1,5},{5,1},{2,6},{6,2},{3,7},{7,3},{8,12},{12,8},{9,1... | collective-permute-start | bytes 3145736 | tf_op jit(solution)/shard_map/ppermute | solution.py:496
Sparse Core Ops, SparseCore 0:
  20.3 85.2 all-gather.1

commit v7 on v6

--- a/solution.py
+++ b/solution.py
@@ -475,10 +475,9 @@
         extra,
     )
     y_arg = lax.axis_index("y").astype(jnp.int32).reshape(1)
-    next_plane, far_plane = (
-        lax.ppermute(own, "z", [(source, source + step) for source in range(16 - step)])
-        for step in (1, 2)
-    )
+    ahead = [(source, source + 1) for source in range(15)]
+    next_plane = lax.ppermute(own, "z", ahead)
+    far_plane = lax.ppermute(next_plane, "z", ahead)
     parts = parcels(y_arg, own, next_plane, far_plane)
     parts = lax.all_to_all(parts, "y", 0, 0, tiled=True)
     window = lay_window(y_arg, parts)

time: 157 us -> 157 us (level)
  blocking collectives: 84.3 us -> 81.2 us
  starting transfers between devices: 16.2 us -> 17.9 us
    all_to_all x1, blocking collectives: 15.9 us -> 13.5 us  [layer(): parts = lax.all_to_all(parts, 'y', 0, 0, tiled=True)]
    ppermute x2, waiting for transfers between devices: 10.4 us -> 12 us  [the longest x1 6.78 us: layer(): next_plane = lax.ppermute(own, 'z', ahead)]
  transfers between devices with their start and end apart: 6 -> 6, of which waited for: 5 -> 4; matrix products, arithmetic and copies ran while one was open for 2% -> 2% of each run, Pallas kernels for 1% -> 1%
where the time goes in v7:
time: 157 us
  blocking collectives  81.2 us (52%)
  Pallas kernels  21.1 us (13%)
  starting transfers between devices  17.9 us (11%)
  waiting for transfers between devices  17.3 us (11%)
  between operations  13.6 us (9%)
  local copies, waits for them, and re-layouts  3.33 us (2%)
  other arithmetic  2.33 us (1%)
    all_gather x1, blocking collectives, layer(): narrow = lax.all_gather(plane[:, 1024:], 'z', axis=0, tiled=True)  36 us
    all_to_all x1, blocking collectives, layer(): shares = lax.all_to_all(partials, 'head', 0, 0, tiled=True)  19.7 us
    pallas_call x1, Pallas kernels, attend_and_project(): pl.pallas_call(attention_kernel, grid=(4,), in_specs=[pl.BlockSpec(memory...  18.4 us
    all_to_all x1, blocking collectives, layer(): parts = lax.all_to_all(parts, 'y', 0, 0, tiled=True)  13.5 us
    all_to_all x1, blocking collectives, layer(): lax.all_to_all(pieces, ('y', 'core'), 0, 0, tiled=True).reshape(128, 1152)  12.1 us
    ppermute x1, waiting for transfers between devices, layer(): next_plane = lax.ppermute(own, 'z', ahead)  6.78 us
    ppermute x1, starting transfers between devices, layer(): next_plane = lax.ppermute(own, 'z', ahead)  5.27 us
    ppermute x1, waiting for transfers between devices, layer(): far_plane = lax.ppermute(next_plane, 'z', ahead)  5.21 us
  transfers between devices with their start and end apart: 6, of which 4 were waited for; matrix products, arithmetic and copies ran while one was open for 2% of the time, Pallas kernels for 1%

profile of v7, /device:TPU:96, one launch (start us, length us, event | category | flops | bytes accessed | tf_op | source)
XLA Modules:
  0.0 156.7 jit_solution(5236100242120606069)
XLA Ops:
  6.5 0.0 all-gather.2.cloned.1.call-start
  6.5 0.8 lay_pieces.1
  7.3 12.1 %all_to_all.20 = bf16[8,16,1152]{2,1,0:T(8,128)(2,1)S(1)} all-to-all(bf16[8,16,1152]{2,1,0:T(8,128)(2,1)S(1)} %bitcast.14), channel_id=1, replica_groups=mesh['z'=16,'y'=4,'core'=2,'head'=4] {'y','core'}, dimensions={0} | all-to-all | bytes 589824 | tf_op jit(solution)/shard_map/all_to_all | solution.py:448
  19.5 0.7 slice.9
  20.2 0.0 all-gather.2.cloned.1.call-update
  20.2 2.5 %broadcast_in_dim.4 = bf16[8,256,512]{2,1,0:T(8,128)(2,1)} broadcast(bf16[256,512]{1,0:T(8,128)(2,1)} %param.11), dimensions={1,2} | broadcast | bytes 2359296 | tf_op jit(solution)/shard_map/broadcast_in_dim | solution.py:34
  22.7 0.0 copy-start.7
  22.7 0.0 copy-start.5
  22.7 0.0 copy-start.6
  22.7 0.0 copy-start.2
  22.7 0.0 copy-start.3
  22.7 4.4 %all-to-all-start = ((bf16[8,256,512]{2,1,0:T(8,128)(2,1)}), bf16[8,256,512]{2,1,0:T(8,128)(2,1)S(1)}, u32[]{:S(2)}, u32[]{:S(2)}) async-start(bf16[8,256,512]{2,1,0:T(8,128)(2,1)} %broadcast_in_dim.4), calls=%async_computation | async-start | bytes 4194304 | tf_op jit(solution)/shard_map/all_to_all | solution.py:33
  27.2 0.1 pad.7.clone
  27.3 0.0 copy-done.7
  27.3 0.0 copy-done.5
  27.3 0.0 copy-done.6
  27.3 0.1 fusion.3.extra_ref
  27.4 1.0 multiply_sine_fusion
  28.4 36.0 %all_gather.6.w_ref = bf16[2048,128]{1,0:T(8,128)(2,1)S(1)} all-gather(bf16[128,128]{1,0:T(8,128)(2,1)S(1)} %slice.8), channel_id=1, replica_groups=mesh['z'=16,'y'=4,'core'=2,'head'=4] {'z'}, dimensions={0}, use_global_device_ids=true | all-gather | bytes 557056 | tf_op jit(solution)/shard_map/all_gather | solution.py:450
  64.4 0.0 all-to-all-done
  64.4 0.0 copy-done.2
  64.4 0.0 copy-done.3
  64.4 1.7 %project_keys_or_values.1 = (bf16[528,128]{1,0:T(8,128)(2,1)S(1)}, bf16[2,4,256,512]{3,2,1,0:T(8,128)(2,1)S(1)}) custom-call(s32[1]{0:T(128)} %bitcast.core_ref, bf16[2,4,256,512]{3,2,1,0:T(8,128)(2,1)S(1)} %bitcast.13, f32[4,1,512]{2,1,0:T(1,128)S(1)} %bitcast.15, bf16[2048,128]{1,0:T(8,128)(2,1)S(1)} %all_gather.6.w_ref, f32[1,128]{1,0:T(1,128)S(1)} %bitcast.16, ...), custom_call_target="tpu_custom_call" | custom-call | tf_op jit(solution)/shard_map/project_keys_or_values/pallas_call | solution.py:105
  66.1 0.0 copy-start.1
  66.1 5.3 %collective-permute-start = (bf16[528,128]{1,0:T(8,128)(2,1)S(1)}, bf16[528,128]{1,0:T(8,128)(2,1)S(1)}, u32[]{:S(2)}, u32[]{:S(2)}) collective-permute-start(bf16[528,128]{1,0:T(8,128)(2,1)S(1)} %get-tuple-element.10.own_ref), channel_id=1, source_target_pairs={{0,32},{32,64},{64,96},{96,128},{128,160},{160,192},{192,224},{224... | collective-permute-start | bytes 405512 | tf_op jit(solution)/shard_map/ppermute | solution.py:479
  71.4 6.8 %collective-permute-done.next_ref = bf16[528,128]{1,0:T(8,128)(2,1)S(1)} collective-permute-done((bf16[528,128]{1,0:T(8,128)(2,1)S(1)}, bf16[528,128]{1,0:T(8,128)(2,1)S(1)}, u32[]{:S(2)}, u32[]{:S(2)}) %collective-permute-start) | collective-permute-done | bytes 135200 | tf_op jit(solution)/shard_map/ppermute | solution.py:479
  78.2 4.2 %collective-permute-start.1 = (bf16[528,128]{1,0:T(8,128)(2,1)S(1)}, bf16[528,128]{1,0:T(8,128)(2,1)S(1)}, u32[]{:S(2)}, u32[]{:S(2)}) collective-permute-start(bf16[528,128]{1,0:T(8,128)(2,1)S(1)} %collective-permute-done.next_ref), channel_id=1, source_target_pairs={{0,32},{32,64},{64,96},{96,128},{128,160},{160,192},{192,224},{224... | collective-permute-start | bytes 405512 | tf_op jit(solution)/shard_map/ppermute | solution.py:480
  82.4 5.2 %collective-permute-done.1.far_ref = bf16[528,128]{1,0:T(8,128)(2,1)S(1)} collective-permute-done((bf16[528,128]{1,0:T(8,128)(2,1)S(1)}, bf16[528,128]{1,0:T(8,128)(2,1)S(1)}, u32[]{:S(2)}, u32[]{:S(2)}) %collective-permute-start.1) | collective-permute-done | bytes 135200 | tf_op jit(solution)/shard_map/ppermute | solution.py:480
  87.6 0.1 parcels.1
  87.7 0.0 copy-start.4
  87.7 13.5 %all_to_all.21.parts_ref = bf16[4,2,528,128]{3,2,1,0:T(8,128)(2,1)S(1)} all-to-all(bf16[4,2,528,128]{3,2,1,0:T(8,128)(2,1)S(1)} %parcels.1), channel_id=1, replica_groups=mesh['z'=16,'y'=4,'core'=2,'head'=4] {'y'}, dimensions={0} | all-to-all | bytes 2162688 | tf_op jit(solution)/shard_map/all_to_all | solution.py:482
  101.2 0.1 lay_window.1.own_ref
  101.3 0.0 copy-done.1
  101.3 0.0 copy-start
  101.3 1.9 %collective-permute-start.2 = (bf16[4224,128]{1,0:T(8,128)(2,1)S(1)}, bf16[4224,128]{1,0:T(8,128)(2,1)}, u32[]{:S(2)}, u32[]{:S(2)}) collective-permute-start(bf16[4224,128]{1,0:T(8,128)(2,1)S(1)} %lay_window.1.own_ref), channel_id=1, source_target_pairs={{0,4},{4,0},{1,5},{5,1},{2,6},{6,2},{3,7},{7,3},{8,12},{12,8},{9,1... | collective-permute-start | bytes 3244040 | tf_op jit(solution)/shard_map/ppermute | solution.py:484
  103.2 2.8 %collective-permute-done.2.other_ref = bf16[4224,128]{1,0:T(8,128)(2,1)} collective-permute-done((bf16[4224,128]{1,0:T(8,128)(2,1)S(1)}, bf16[4224,128]{1,0:T(8,128)(2,1)}, u32[]{:S(2)}, u32[]{:S(2)}) %collective-permute-start.2) | collective-permute-done | bytes 1081376 | tf_op jit(solution)/shard_map/ppermute | solution.py:484
  106.0 0.0 all-gather.2.cloned.1.call-done.wide_ref
  106.0 0.0 copy-done
  106.0 0.0 copy-done.4
  106.0 18.4 %attend_and_project.1 = (f32[4,256,512]{2,1,0:T(8,128)S(1)}, bf16[4,256,512]{2,1,0:T(8,128)(2,1)S(1)}) custom-call(s32[1]{0:T(128)} %bitcast.core_ref, bf16[2,4,256,512]{3,2,1,0:T(8,128)(2,1)} %copy-done.1, f32[1,128]{1,0:T(1,128)S(1)} %bitcast.17, f32[512,64]{1,0:T(8,128)S(1)} %get-tuple-element.14.cos_ref, f32[512,64]{1,0:T(8,128)S(1)} %get-tuple-element.13.sin_ref, ...), custom_call_target="tpu_custom_call" | custom-call | tf_op jit(solution)/shard_map/attend_and_project/pallas_call | solution.py:386
  124.4 2.0 %collective-permute-start.3 = (bf16[4,256,512]{2,1,0:T(8,128)(2,1)S(1)}, bf16[4,256,512]{2,1,0:T(8,128)(2,1)S(1)}, u32[]{:S(2)}, u32[]{:S(2)}) collective-permute-start(bf16[4,256,512]{2,1,0:T(8,128)(2,1)S(1)} %get-tuple-element.12), channel_id=1, source_target_pairs={{0,4},{4,0},{1,5},{5,1},{2,6},{6,2},{3,7},{7,3},{8,12},{12,8},{9,1... | collective-permute-start | bytes 3145736 | tf_op jit(solution)/shard_map/ppermute | solution.py:495
  126.5 2.5 %collective-permute-done.3 = bf16[4,256,512]{2,1,0:T(8,128)(2,1)S(1)} collective-permute-done((bf16[4,256,512]{2,1,0:T(8,128)(2,1)S(1)}, bf16[4,256,512]{2,1,0:T(8,128)(2,1)S(1)}, u32[]{:S(2)}, u32[]{:S(2)}) %collective-permute-start.3) | collective-permute-done | bytes 1048608 | tf_op jit(solution)/shard_map/ppermute | solution.py:495
  129.0 0.3 add_convert_fusion
  129.3 19.7 %all_to_all.22 = bf16[4,256,512]{2,1,0:T(8,128)(2,1)S(1)} all-to-all(bf16[4,256,512]{2,1,0:T(8,128)(2,1)S(1)} %add_convert_fusion), channel_id=1, replica_groups=mesh['z'=16,'y'=4,'core'=2,'head'=4] {'head'}, dimensions={0} | all-to-all | bytes 2097152 | tf_op jit(solution)/shard_map/all_to_all | solution.py:497
  149.0 0.9 reduce_sum.12
  (6 shorter events, 0.0 us)
Async XLA Ops:
  6.5 99.5 %all-gather.2.cloned.1.call-start = ((), (), s32[]{:S(2)}) async-start(), calls=%async_computation.4 | async-start | bytes 4456448 | tf_op jit(solution)/shard_map/all_gather | solution.py:449
  22.7 4.6 %copy-start.7 = (s32[2]{0:T(128)S(1)}, s32[2]{0:T(128)}, u32[]{:S(2)}) copy-start(s32[2]{0:T(128)} %param.21) | copy-start | bytes 28
  22.7 4.6 %copy-start.5 = (s32[256]{0:T(256)S(1)}, s32[256]{0:T(256)}, u32[]{:S(2)}) copy-start(s32[256]{0:T(256)} %param.19) | copy-start | bytes 3076
  22.7 4.6 %copy-start.6 = (s32[256]{0:T(256)S(1)}, s32[256]{0:T(256)}, u32[]{:S(2)}) copy-start(s32[256]{0:T(256)} %param.20) | copy-start | bytes 3076
  22.7 41.7 %copy-start.2 = (f32[2048]{0:T(1024)S(1)}, f32[2048]{0:T(1024)}, u32[]{:S(2)}) copy-start(f32[2048]{0:T(1024)} %param.12) | copy-start | bytes 24580
  22.7 41.7 %copy-start.3 = (f32[128]{0:T(128)S(1)}, f32[128]{0:T(128)}, u32[]{:S(2)}) copy-start(f32[128]{0:T(128)} %param.17) | copy-start | bytes 1540
  22.7 41.6 %all-to-all-start = ((bf16[8,256,512]{2,1,0:T(8,128)(2,1)}), bf16[8,256,512]{2,1,0:T(8,128)(2,1)S(1)}, u32[]{:S(2)}, u32[]{:S(2)}) async-start(bf16[8,256,512]{2,1,0:T(8,128)(2,1)} %broadcast_in_dim.4), calls=%async_computation | async-start | bytes 4194304 | tf_op jit(solution)/shard_map/all_to_all | solution.py:33
  66.1 35.2 %copy-start.1 = (bf16[2,4,256,512]{3,2,1,0:T(8,128)(2,1)}, bf16[2,4,256,512]{3,2,1,0:T(8,128)(2,1)S(1)}, u32[]{:S(2)}) copy-start(bf16[2,4,256,512]{3,2,1,0:T(8,128)(2,1)S(1)} %get-tuple-element.9.tokens_ref) | copy-start | bytes 6291460
  66.1 12.1 %collective-permute-start = (bf16[528,128]{1,0:T(8,128)(2,1)S(1)}, bf16[528,128]{1,0:T(8,128)(2,1)S(1)}, u32[]{:S(2)}, u32[]{:S(2)}) collective-permute-start(bf16[528,128]{1,0:T(8,128)(2,1)S(1)} %get-tuple-element.10.own_ref), channel_id=1, source_target_pairs={{0,32},{32,64},{64,96},{96,128},{128,160},{160,192},{192,224},{224... | collective-permute-start | bytes 405512 | tf_op jit(solution)/shard_map/ppermute | solution.py:479
  78.2 9.4 %collective-permute-start.1 = (bf16[528,128]{1,0:T(8,128)(2,1)S(1)}, bf16[528,128]{1,0:T(8,128)(2,1)S(1)}, u32[]{:S(2)}, u32[]{:S(2)}) collective-permute-start(bf16[528,128]{1,0:T(8,128)(2,1)S(1)} %collective-permute-done.next_ref), channel_id=1, source_target_pairs={{0,32},{32,64},{64,96},{96,128},{128,160},{160,192},{192,224},{224... | collective-permute-start | bytes 405512 | tf_op jit(solution)/shard_map/ppermute | solution.py:480
  87.7 18.3 %copy-start.4 = (f32[128]{0:T(128)S(1)}, f32[128]{0:T(128)}, u32[]{:S(2)}) copy-start(f32[128]{0:T(128)} %param.16) | copy-start | bytes 1540
  101.3 4.7 %copy-start = (bf16[4224,128]{1,0:T(8,128)(2,1)}, bf16[4224,128]{1,0:T(8,128)(2,1)S(1)}, u32[]{:S(2)}) copy-start(bf16[4224,128]{1,0:T(8,128)(2,1)S(1)} %lay_window.1.own_ref) | copy-start | bytes 3244036
  101.3 4.7 %collective-permute-start.2 = (bf16[4224,128]{1,0:T(8,128)(2,1)S(1)}, bf16[4224,128]{1,0:T(8,128)(2,1)}, u32[]{:S(2)}, u32[]{:S(2)}) collective-permute-start(bf16[4224,128]{1,0:T(8,128)(2,1)S(1)} %lay_window.1.own_ref), channel_id=1, source_target_pairs={{0,4},{4,0},{1,5},{5,1},{2,6},{6,2},{3,7},{7,3},{8,12},{12,8},{9,1... | collective-permute-start | bytes 3244040 | tf_op jit(solution)/shard_map/ppermute | solution.py:484
  124.4 4.6 %collective-permute-start.3 = (bf16[4,256,512]{2,1,0:T(8,128)(2,1)S(1)}, bf16[4,256,512]{2,1,0:T(8,128)(2,1)S(1)}, u32[]{:S(2)}, u32[]{:S(2)}) collective-permute-start(bf16[4,256,512]{2,1,0:T(8,128)(2,1)S(1)} %get-tuple-element.12), channel_id=1, source_target_pairs={{0,4},{4,0},{1,5},{5,1},{2,6},{6,2},{3,7},{7,3},{8,12},{12,8},{9,1... | collective-permute-start | bytes 3145736 | tf_op jit(solution)/shard_map/ppermute | solution.py:495
Sparse Core Ops, SparseCore 0:
  20.3 82.1 all-gather.1
